TPU v7x, 32 devices: a whole 2x2x4 slice. The times are simulated.
32 devices in a mesh: row: 8 (over z, x), col: 4 (over y, core).
Axes of the slice: x: 2, y: 2, z: 4, core: 2. Of those that a mesh axis runs over, the one named last changes fastest.
Arguments:
- front_pivot: float32 [64, 128, 128], P('col', 'row'), may hold values from -256 to 256, as said below
- front_update: float32 [64, 640, 768], P('col', 'row'), may hold values from -12 to 12, as said below
- child_blocks: float32 [64, 2, 512, 512], P('col', None, 'row'), may hold values from -0.5 to 0.5, as said below
- child_map: int32 [64, 2, 512], P('col'), may hold values from -1 to 767, as said below
Outputs:
- lhat: float32 [64, 640, 128], P('col', 'row')
- schur: float32 [64, 640, 640], P('col', 'row')
- negative_share: float32 [], replicated
Inputs may be any that keep to these rules, and one draw needn't show every extreme that they name: `front_pivot`: symmetric in its last two dimensions. With both children's entries added, the pivot block of every front has an LDL^T factorization without pivoting whose pivots have magnitudes 4 to 40. `front_update`: the last 640 columns of each front form a symmetric matrix. `child_blocks`: symmetric in its last two dimensions. child_map[f, c, i] is the row and column of front f's assembled matrix that row and column i of child c go to, or -1 for padding. A child's entries of 0 or more are distinct, come before its padding, and number at least 385, and more than half of 512. Parent row p is held by grid row p // 16 if p < 128, else by (p - 128) // 80. Of the 64 rows i of a child with the same i // 64, at most 16 go to rows held by any one grid row, and every child reaches that bound.
All inputs are finite; a program needn't handle non-finite values.
Results may differ from a plain program's by a relative error of at most 0.0003.
Values sent between devices are 32-bit elements; how exact they have to be, the bound alone decides.
No kernel may reach another device: no remote copies, remote signals or barrier semaphores. Data moves between devices by JAX's collectives and lax.ppermute only.
A program may use at most 64 MiB of HBM per device.

v0:
```python
import jax
import jax.numpy as jnp
from jax import lax
from jax.sharding import PartitionSpec as P

highest = lax.Precision.HIGHEST


def factor(blocks):
    fronts, count = (blocks.shape[0], blocks.shape[-1])
    panel_width = 8
    index = jnp.arange(count, dtype=jnp.int32)

    def panel_step(panel, carry):
        current, lower, pivots = carry
        start = panel * panel_width
        strip = lax.dynamic_slice_in_dim(current, start, panel_width, 2)
        columns = []
        values = []
        for inner in range(panel_width):
            place = start + inner
            leading = lax.dynamic_index_in_dim(strip, place, 1, keepdims=False)
            pivot = leading[:, inner]
            below = index[None, :] > place
            column = strip[:, :, inner]
            multiplier = jnp.where(below, column / pivot[:, None], jnp.zeros_like(column))
            strip = strip - multiplier[:, :, None] * leading[:, None, :]
            columns.append(multiplier)
            values.append(pivot)
        panel_lower = jnp.stack(columns, axis=2)
        panel_pivots = jnp.stack(values, axis=1)
        lower = lax.dynamic_update_slice_in_dim(lower, panel_lower, start, 2)
        pivots = lax.dynamic_update_slice_in_dim(pivots, panel_pivots, start, 1)
        product = jnp.einsum(
            "fiw,fjw->fij", panel_lower * panel_pivots[:, None, :], panel_lower, precision=highest
        )
        later = index >= start + panel_width
        current = current - jnp.where(
            later[:, None] & later[None, :], product, jnp.zeros_like(product)
        )
        return (current, lower, pivots)

    start_state = (blocks, jnp.zeros_like(blocks), jnp.zeros((fronts, count), blocks.dtype))
    current, lower, pivots = lax.fori_loop(0, count // panel_width, panel_step, start_state)
    identity = jnp.eye(count, dtype=blocks.dtype)
    inverse = jax.vmap(
        lambda matrix: jax.scipy.linalg.solve_triangular(
            matrix, identity, lower=True, unit_diagonal=True
        )
    )(lower)
    return (inverse, pivots)


def local(front_pivot, front_update, child_blocks, child_map):
    row_count = lax.axis_size("row")
    my_row = lax.axis_index("row")
    fronts, pivot_rows, pivot_width = front_pivot.shape
    update_rows, width = (front_update.shape[1], front_update.shape[2])
    held, child_width = (child_blocks.shape[2], child_blocks.shape[3])
    capacity = 2 * held // row_count
    slot_count = row_count * capacity
    local_rows = pivot_rows + update_rows
    valid = child_map >= 0
    in_pivot = child_map < pivot_width
    owner = jnp.where(in_pivot, child_map // pivot_rows, (child_map - pivot_width) // update_rows)
    owner = jnp.where(valid, owner, row_count)
    target_row = jnp.where(
        in_pivot, child_map % pivot_rows, pivot_rows + (child_map - pivot_width) % update_rows
    )
    owner_hot = (owner[..., None] == jnp.arange(row_count, dtype=jnp.int32)).astype(jnp.int32)
    blocked = owner_hot.reshape(fronts, 2, row_count, held, row_count)
    earlier = jnp.cumsum(blocked, axis=3) - blocked
    rank = jnp.sum(earlier * blocked, axis=4).reshape(fronts, 2, child_width)
    position = jnp.arange(child_width, dtype=jnp.int32)
    slot = owner * capacity + rank
    arrival = (position // held)[None, None, :] * capacity + rank
    my_slot = lax.dynamic_slice_in_dim(slot, my_row * held, held, 2)
    my_valid = lax.dynamic_slice_in_dim(valid, my_row * held, held, 2)
    slot_range = jnp.arange(slot_count, dtype=jnp.int32)
    packing = (
        (my_slot[:, :, None, :] == slot_range[None, None, :, None]) & my_valid[:, :, None, :]
    ).astype(jnp.float32)
    outgoing = jnp.einsum("fcsq,fcqj->fcsj", packing, child_blocks, precision=highest)
    outgoing = outgoing.reshape(fronts, 2, row_count, capacity, child_width)
    incoming = lax.all_to_all(outgoing, "row", split_axis=2, concat_axis=2, tiled=True)
    incoming = incoming.reshape(fronts, 2, slot_count, child_width)
    mine = valid & (owner == my_row)
    row_hot = (
        (target_row[..., None] == jnp.arange(local_rows, dtype=jnp.int32)) & mine[..., None]
    ).astype(jnp.float32)
    arrival_hot = (arrival[..., None] == slot_range).astype(jnp.float32)
    placing = jnp.einsum("fcil,fcip->fclp", row_hot, arrival_hot, precision=highest)
    placed = jnp.einsum("fclp,fcpq->fclq", placing, incoming, precision=highest)
    column_range = jnp.arange(width, dtype=jnp.int32)

    def place_columns(inputs):
        rows_placed, indices = inputs
        column_hot = (indices[:, :, None] == column_range[None, None, :]).astype(jnp.float32)
        total = jnp.dot(
            rows_placed[0], column_hot[0], precision=highest, preferred_element_type=jnp.float32
        )
        return total + jnp.dot(
            rows_placed[1], column_hot[1], precision=highest, preferred_element_type=jnp.float32
        )

    added = lax.map(place_columns, (placed, child_map))
    pivot_local = front_pivot + added[:, :pivot_rows, :pivot_width]
    update_local = front_update + added[:, pivot_rows:, :]
    coupling = update_local[:, :, :pivot_width]
    trailing = update_local[:, :, pivot_width:]
    own_fronts = lax.all_to_all(pivot_local, "row", split_axis=0, concat_axis=1, tiled=True)
    own_inverse, own_pivots = factor(own_fronts)
    inverse, pivots = (
        lax.all_gather(own_inverse, "row", axis=0, tiled=True),
        lax.all_gather(own_pivots, "row", axis=0, tiled=True),
    )
    lhat = jnp.einsum("fik,fjk->fij", coupling, inverse, precision=highest)
    scaled = lhat / pivots[:, None, :]
    correction = jnp.einsum(
        "fik,fjk->fij", scaled, lax.all_gather(lhat, "row", axis=1, tiled=True), precision=highest
    )
    schur = trailing - correction
    negatives = jnp.sum(jnp.where(pivots < 0.0, 1.0, 0.0).astype(jnp.float32))
    total = lax.psum(negatives, "col")
    negative_share = total / (fronts * lax.axis_size("col") * pivot_width)
    return (lhat, schur, negative_share)


def solution(mesh):
    in_specs = (
        P("col", "row", None),
        P("col", "row", None),
        P("col", None, "row", None),
        P("col", None, None),
    )
    out_specs = (P("col", "row", None), P("col", "row", None), P())
    return jax.shard_map(local, mesh=mesh, in_specs=in_specs, out_specs=out_specs, check_vma=False)
```

profile of v0, /device:TPU:0, one launch (start us, length us, event | category | flops | bytes accessed | tf_op | source)
XLA Modules:
  0.0 599.0 jit_solution(478743614236139514)
XLA Ops:
  8.6 42.6 %fusion.18 = s32[16,2,8,64]{2,3,1,0:T(8,128)S(1)} fusion(s32[16,2,8,64]{2,3,1,0:T(8,128)S(1)} %copy.48), kind=kOutput, calls=%fused_computation.74 | output fusion | flops 9158656 | bytes 131072 | tf_op jit(solution)/shard_map/jit(cumsum)/reduce_window_sum | solution.py:72
  51.8 6.6 %fusion.27 = f32[16,2,128,512]{3,2,1,0:T(8,128)S(1)} fusion(f32[16,2,64,512]{3,2,1,0:T(8,128)} %param.10, s32[16,2,64]{2,1,0:T(2,128)S(1)} %copy.51, pred[16,2,64]{2,1,0:T(4,128)(4,1)S(1)} %copy.52), kind=kOutput, calls=%fused_computation.88 | convolution fusion | flops 1611137024 | bytes 12593152 | tf_op jit(solution)/shard_map/fcsq,fcqj->fcsj/dot_general | solution.py:83
  58.4 4.3 copy.53
  62.7 7.4 %all-to-all-start = ((f32[16,2,8,16,512]{4,3,1,0,2:T(8,128)}), f32[16,2,8,16,512]{4,3,1,0,2:T(8,128)}, u32[]{:S(2)}, u32[]{:S(2)}) async-start(f32[16,2,8,16,512]{4,3,1,0,2:T(8,128)} %copy.53), calls=%async_computation | async-start | bytes 16777216 | tf_op jit(solution)/shard_map/all_to_all | solution.py:85
  70.4 6.0 fusion.19
  76.3 176.9 %all-to-all-done = f32[16,2,8,16,512]{4,3,1,0,2:T(8,128)} async-done(((f32[16,2,8,16,512]{4,3,1,0,2:T(8,128)}), f32[16,2,8,16,512]{4,3,1,0,2:T(8,128)}, u32[]{:S(2)}, u32[]{:S(2)}) %all-to-all-start) | async-done | bytes 8388640 | tf_op jit(solution)/shard_map/all_to_all | solution.py:85
  253.3 4.4 copy.54
  257.7 7.6 %fusion.61 = f32[16,2,96,512]{3,2,1,0:T(8,128)} fusion(f32[16,2,96,128]{3,2,1,0:T(8,128)S(1)} %fusion.19, f32[16,2,128,512]{3,2,1,0:T(8,128)S(1)} %bitcast.85), kind=kOutput, calls=%fused_computation.148 | convolution fusion | flops 2415919104 | bytes 16252928 | tf_op jit(solution)/shard_map/fclp,fcpq->fclq/dot_general | solution.py:93
  265.3 69.4 %while.33 = (s32[]{:T(128)}, f32[16,96,768]{2,1,0:T(8,128)}, f32[16,2,96,512]{3,2,1,0:T(8,128)}, s32[16,2,512]{2,1,0:T(2,128)S(1)}, s32[]{:T(128)}, /*index=5*/s32[]{:T(128)}, s32[]{}) while((s32[]{:T(128)}, f32[16,96,768]{2,1,0:T(8,128)}, f32[16,2,96,512]{3,2,1,0:T(8,128)}, s32[16,2,512]{2,1,0:T(2,128)S(1)}, s32[]{:T(128)}, ...), condition=%wide.region_3.4_spmd.clone, body=%wide.region_2.3_spmd.clone.sunk | while | flops 906829824 | bytes 2864737 | solution.py:106
  293.3 2.3 fusion.82
  297.7 2.3 fusion.82
  302.0 2.3 fusion.82
  310.7 2.3 fusion.82
  336.2 3.6 all-to-all-start.1
  340.0 7.2 %all-to-all-done.1 = f32[16,16,128]{2,1,0:T(8,128)S(1)} async-done(((f32[16,16,128]{2,1,0:T(8,128)}), f32[16,16,128]{2,1,0:T(8,128)S(1)}, u32[]{:S(2)}, u32[]{:S(2)}) %all-to-all-start.1) | async-done | bytes 131104 | tf_op jit(solution)/shard_map/all_to_all | solution.py:111
  347.4 83.5 %while.34 = (s32[]{:T(128)}, f32[2,128,128]{1,2,0:T(8,128)S(1)}, f32[2,128,128]{1,2,0:T(8,128)S(1)}, f32[2,128]{1,0:T(2,128)S(1)}, s32[]{:T(128)}, /*index=5*/s3...) while((s32[]{:T(128)}, f32[2,128,128]{1,2,0:T(8,128)S(1)}, ...), condition=%wide.region_5.6_spmd.clone.clone, body=%wide.region_4.5_spmd.clone.clone.sunk | while | flops 3349669 | bytes 1026329 | solution.py:44
  431.0 19.7 %custom-call.4 = f32[2,1,128,128]{2,3,1,0:T(8,128)S(1)} custom-call(f32[2,1,128,128]{3,2,1,0:T(8,128)S(1)} %add_bitcast_fusion), custom_call_target="InvertDiagBlocksLowerTriangular" | custom-call | tf_op jit(solution)/shard_map/vmap(jit(_solve_triangular))/triangular_solve | solution.py:47
  452.0 5.8 slice_add_fusion
  457.8 32.4 %all-gather.4.cloned.1.call-done = f32[16,128,128]{2,1,0:T(8,128)} async-done(((f32[2,128,128]{2,1,0:T(8,128)}), f32[16,128,128]{2,1,0:T(8,128)}) %all-gather.4.cloned.1.call-update) | async-done | bytes 1048592 | tf_op jit(solution)/shard_map/all_gather | solution.py:114
  490.1 4.4 fusion.29
  494.6 18.7 %all-gather = f32[8,2,128]{2,1,0:T(2,128)S(1)} all-gather(f32[1,2,128]{2,1,0:T(2,128)S(1)} %bitcast.118), channel_id=1, replica_groups=mesh['row'=8,'col'=4] {'row'}, dimensions={0}, use_global_device_ids=true | all-gather | bytes 9216 | tf_op jit(solution)/shard_map/all_gather | solution.py:115
  513.9 6.7 %psum.7 = f32[]{:T(128)} all-reduce(f32[]{:T(128)} %select_reduce_fusion), channel_id=1, replica_groups=mesh['row'=8,'col'=4] {'col'}, use_global_device_ids=true, to_apply=%region_7.8 | all-reduce | flops 1 | bytes 8 | tf_op jit(solution)/shard_map/psum | solution.py:124
  521.2 58.1 %all-gather.6.cloned.1.call-done = f32[16,640,128]{2,1,0:T(8,128)} async-done(((f32[16,80,128]{2,1,0:T(8,128)}), f32[16,640,128]{2,1,0:T(8,128)}) %all-gather.6.cloned.1.call-update) | async-done | bytes 5242896 | tf_op jit(solution)/shard_map/all_gather | solution.py:120
  579.4 11.6 %slice_subtract_fusion = f32[16,80,640]{2,1,0:T(8,128)} fusion(f32[16,80,768]{2,1,0:T(8,128)} %slice_add_fusion, f32[16,640,128]{2,1,0:T(8,128)} %all-gather.6.cloned.1.call-done, f32[16,80,128]{2,1,0:T(8,128)} %fusion.29, f32[16,128]{1,0:T(8,128)S(1)} %bitcast.117), kind=kOutput, calls=%fused_computation.83 | convolution fusion | flops 1259274240 | bytes 12460032 | tf_op jit(solution)/shard_map/fik,fjk->fij/dot_general | solution.py:119
  (864 shorter events, 146.7 us)
Async XLA Ops:
  62.7 7.5 %copy-start = (s32[16,2,512]{2,1,0:T(2,128)S(1)}, s32[16,2,512]{2,1,0:T(2,128)}, u32[]{:S(2)}) copy-start(s32[16,2,512]{2,1,0:T(2,128)} %param.11) | copy-start | bytes 196612
  62.7 190.6 %all-to-all-start = ((f32[16,2,8,16,512]{4,3,1,0,2:T(8,128)}), f32[16,2,8,16,512]{4,3,1,0,2:T(8,128)}, u32[]{:S(2)}, u32[]{:S(2)}) async-start(f32[16,2,8,16,512]{4,3,1,0,2:T(8,128)} %copy.53), calls=%async_computation | async-start | bytes 16777216 | tf_op jit(solution)/shard_map/all_to_all | solution.py:85
  265.3 69.4 %copy-start.1 = (f32[16,16,128]{2,1,0:T(8,128)S(1)}, f32[16,16,128]{2,1,0:T(8,128)}, u32[]{:S(2)}) copy-start(f32[16,16,128]{2,1,0:T(8,128)} %param.8) | copy-start | bytes 393220
  336.2 11.0 %all-to-all-start.1 = ((f32[16,16,128]{2,1,0:T(8,128)}), f32[16,16,128]{2,1,0:T(8,128)S(1)}, u32[]{:S(2)}, u32[]{:S(2)}) async-start(f32[16,16,128]{2,1,0:T(8,128)} %slice_add_fusion.1), calls=%async_computation.1 | async-start | bytes 262144 | tf_op jit(solution)/shard_map/all_to_all | solution.py:111
  339.9 150.3 %all-gather.4.cloned.1.call-start = ((), (), s32[]{:S(2)}) async-start(), calls=%async_computation.2 | async-start | bytes 1179648 | tf_op jit(solution)/shard_map/all_gather | solution.py:114
  451.7 127.7 %all-gather.6.cloned.1.call-start = ((), (), s32[]{:S(2)}) async-start(), calls=%async_computation.3 | async-start | bytes 5898240 | tf_op jit(solution)/shard_map/all_gather | solution.py:120
Sparse Core Ops, SparseCore 0:
  451.8 38.2 all-gather.3
  494.7 84.6 all-gather.5
where the time goes:
time: 600 us; the launch traced here: 599 us
  waiting for transfers between devices  275 us (46%)
  matrix products  106 us (18%)
  other arithmetic  101 us (17%)
  local copies, waits for them, and re-layouts  62.1 us (10%)
  blocking collectives  25.4 us (4%)
  between operations  16 us (3%)
  starting transfers between devices  11.3 us (2%)
    all_to_all x1, waiting for transfers between devices, local(): lax.all_to_all(outgoing, 'row', split_axis=2, concat_axis=2, tiled=True)  177 us
    all_gather x1, waiting for transfers between devices, local(): lax.all_gather(lhat, 'row', axis=1, tiled=True)  58.1 us
    another operation x1, other arithmetic, local(): earlier = jnp.cumsum(blocked, axis=3) - blocked  42.6 us
    dot_general x16, matrix products, place_columns(): jnp.dot(rows_placed[0], column_hot[0], precision=highest, preferred_eleme...  36.3 us
    all_gather x1, waiting for transfers between devices, local(): lax.all_gather(own_inverse, 'row', axis=0, tiled=True)  32.4 us
    dot_general x16, matrix products, place_columns(): jnp.dot(rows_placed[1], column_hot[1], precision=highest, preferred_eleme...  24.8 us
    slice x128, local copies, waits for them, and re-layouts, panel_step(): pivot = leading[:, inner]  22.7 us
    dynamic_slice x128, local copies, waits for them, and re-layouts, panel_step(): leading = lax.dynamic_index_in_dim(strip, place, 1, keepdims=False)  20.2 us
  transfers between devices with their start and end apart: 4, of which 4 were waited for; matrix products, arithmetic and copies ran while one was open for 2% of the time, Pallas kernels for 0%

commit v1 on v0

v1 whole, which is shorter than its diff:
```python
import functools

import jax
import jax.numpy as jnp
from jax import lax
from jax.experimental import pallas as pl
from jax.experimental.pallas import tpu as pltpu
from jax.sharding import PartitionSpec as P

LANES = 128
highest = lax.Precision.HIGHEST


def split2(x):
    high = x.astype(jnp.bfloat16)
    low = (x - high.astype(jnp.float32)).astype(jnp.bfloat16)
    return high, low


def pack_kernel(dims, row_ref, child_ref, update_ref, pivot_ref, out_ref):
    n, held, planes, extra_rows = dims
    row = row_ref[0]
    width = child_ref.shape[-1]
    lane = lax.broadcasted_iota(jnp.int32, (held, LANES), 1)
    extras = []
    at = 0
    for child in range(2):
        rolled = pltpu.roll(child_ref[0, child], lax.rem(width - row * held, width), 1)
        for plane in range(planes):
            part = rolled[:, plane * LANES : (plane + 1) * LANES]
            if plane == 0:
                part = jnp.where(lane < held, 0.5 * part, part)
            out_ref[0, at : at + held, :] = part
            at += held
        extras.append(rolled[:, planes * LANES : (planes + 1) * LANES])
    extra = jnp.where(row < n // 2, extras[0], extras[1])
    packed = jnp.zeros((extra_rows, LANES), jnp.float32)
    lane = lax.broadcasted_iota(jnp.int32, (extra_rows, LANES), 1)
    for piece in range(held // extra_rows):
        rows = extra[piece * extra_rows : (piece + 1) * extra_rows]
        if piece:
            rows = pltpu.roll(rows, piece * held, 1)
        packed = jnp.where(lane // held == piece, rows, packed)
    out_ref[0, at : at + extra_rows, :] = packed
    at += extra_rows
    out_ref[0, at : at + update_ref.shape[1], :] = update_ref[0]
    at += update_ref.shape[1]
    out_ref[0, at : at + pivot_ref.shape[1], :] = pivot_ref[0]


def front_kernel(dims, map_ref, turned_ref, in_ref, out_ref, pivots_ref, hot_ref, half_ref, sum_ref, aug_ref, coup_ref):
    n, held, planes, extra_rows, update_rows, pivot_rows = dims
    width = map_ref.shape[-1]
    order = sum_ref.shape[0]
    size = aug_ref.shape[0]
    f32, bf16 = jnp.float32, jnp.bfloat16

    def hot(indices):
        count = indices.shape[-1]
        place = lax.broadcasted_iota(jnp.int32, (order, count), 0)
        return jnp.where(place == indices, 1.0, 0.0).astype(bf16)

    last = (((1,), (1,)), ((), ()))
    for child in range(2):
        hot_ref[:, child * width : (child + 1) * width] = hot(map_ref[child : child + 1, :])
        for source in range(n):
            base = child * planes * held
            parts = [
                in_ref[source, base + plane * held : base + (plane + 1) * held, :] for plane in range(planes)
            ]
            columns = planes * LANES
            if (source < n // 2) == (child == 0):
                at = 2 * planes * held
                extra = in_ref[source, at : at + extra_rows, :]
                lane = lax.broadcasted_iota(jnp.int32, (extra_rows, LANES), 1)
                pieces = [
                    jnp.where(lane // held == piece, extra, 0.0) for piece in range(held // extra_rows)
                ]
                parts.append(jnp.concatenate(pieces, axis=0))
                columns += LANES
            high, low = split2(jnp.concatenate(parts, axis=1))
            both = jnp.concatenate([high, low], axis=0)
            spread = lax.dot_general(
                both, hot(turned_ref[source, child : child + 1, :columns]), last, preferred_element_type=f32
            ).astype(bf16)
            at = child * width + source * held
            half_ref[at : at + held, :] = spread[:held]
            half_ref[2 * width + at : 2 * width + at + held, :] = spread[held:]
    for block in range(order // LANES):
        rows = pl.ds(block * LANES, LANES)
        sum_ref[rows, :] = jnp.dot(
            hot_ref[rows, :], half_ref[: 2 * width, :], preferred_element_type=f32
        ) + jnp.dot(hot_ref[rows, :], half_ref[2 * width :, :], preferred_element_type=f32)

    at = 2 * planes * held + extra_rows
    for source in range(n):
        coup_ref[source * update_rows : (source + 1) * update_rows, :] = in_ref[
            source, at : at + update_rows, :
        ]
        aug_ref[source * pivot_rows : (source + 1) * pivot_rows, :size] = in_ref[
            source, at + update_rows : at + update_rows + pivot_rows, :
        ]
    coup_ref[...] += sum_ref[size:, :size] + sum_ref[:size, size:].T
    aug_ref[:, :size] += sum_ref[:size, :size] + sum_ref[:size, :size].T
    square = (size, size)
    aug_ref[:, size:] = jnp.where(
        lax.broadcasted_iota(jnp.int32, square, 0) == lax.broadcasted_iota(jnp.int32, square, 1), 1.0, 0.0
    )

    lanes = lax.broadcasted_iota(jnp.int32, (1, size), 1)
    step = 32
    pivots = jnp.zeros((1, size), f32)
    for start in range(0, size, step):
        rest = size - start
        below = start + lax.broadcasted_iota(jnp.int32, (rest, 1), 0)

        def eliminate(k, pivots, start=start, below=below):
            row = aug_ref[pl.ds(k, 1), :]
            whole = aug_ref[start:, :]
            chosen = lanes == k
            column = jnp.sum(jnp.where(chosen, whole[:, :size], 0.0), axis=1, keepdims=True)
            pivot = jnp.sum(jnp.where(chosen, row[:, :size], 0.0), axis=1, keepdims=True)
            multiplier = jnp.where(below > k, column / pivot, 0.0)
            aug_ref[start:, :] = whole - multiplier * row
            return jnp.where(chosen, pivot, pivots)

        pivots = lax.fori_loop(start, start + step, eliminate, pivots)
    pivots_ref[...] = pivots

    lhat = lax.dot_general(coup_ref[...], aug_ref[:, size:], last, precision=highest, preferred_element_type=f32)
    out_ref[:, :size] = lhat
    coup_ref[...] = lhat / pivots
    for start in range(0, order - size, LANES):
        rows = pl.ds(start, LANES)
        correction = lax.dot_general(
            coup_ref[rows, :], out_ref[:, :size], last, precision=highest, preferred_element_type=f32
        )
        here = size + start
        out_ref[rows, size:] = (
            sum_ref[here : here + LANES, size:] + sum_ref[size:, here : here + LANES].T - correction
        )


def finish_kernel(size, update_ref, back_ref, *refs):
    lhat_ref, schur_ref = refs[-2:]
    lhat_ref[0] = back_ref[0, :, :size]
    schur_ref[0] = update_ref[0, :, size:] + back_ref[0, :, size:]


def local(front_pivot, front_update, child_blocks, child_map):
    f32 = jnp.float32
    n = lax.axis_size("row")
    my_row = lax.axis_index("row")
    fronts, pivot_rows, size = front_pivot.shape
    update_rows, order = front_update.shape[1:]
    held, width = child_blocks.shape[2:]
    per = fronts // n
    planes = width // 2 // LANES
    extra_rows = held * held // LANES
    rows = 2 * planes * held + extra_rows + update_rows + pivot_rows
    row_number = my_row.astype(jnp.int32).reshape(1)

    def pack(turn):
        return pl.pallas_call(
            functools.partial(pack_kernel, (n, held, planes, extra_rows)),
            grid_spec=pltpu.PrefetchScalarGridSpec(
                num_scalar_prefetch=1,
                grid=(n,),
                in_specs=[
                    pl.BlockSpec((1, 2, held, width), lambda g, r: (g * per + turn, 0, 0, 0)),
                    pl.BlockSpec((1, update_rows, size), lambda g, r: (g * per + turn, 0, 0)),
                    pl.BlockSpec((1, pivot_rows, size), lambda g, r: (g * per + turn, 0, 0)),
                ],
                out_specs=pl.BlockSpec((1, rows, LANES), lambda g, r: (g, 0, 0)),
            ),
            out_shape=jax.ShapeDtypeStruct((n, rows, LANES), f32),
            name="pack",
        )(row_number, child_blocks, front_update, front_pivot)

    def whole_front(arrived, turn):
        maps = lax.dynamic_index_in_dim(child_map, my_row * per + turn, 0, keepdims=False)
        twice = jnp.concatenate([maps, maps], axis=1)
        turned = []
        for source in range(n):
            at = source * held
            main = twice[:, at : at + width // 2]
            tail = twice[:, at + width // 2 : at + width // 2 + held]
            turned.append(jnp.concatenate([main] + [tail] * (LANES // held), axis=1))
        turned = jnp.stack(turned)
        return pl.pallas_call(
            functools.partial(front_kernel, (n, held, planes, extra_rows, update_rows, pivot_rows)),
            out_shape=(
                jax.ShapeDtypeStruct((order - size, order), f32),
                jax.ShapeDtypeStruct((1, size), f32),
            ),
            scratch_shapes=[
                pltpu.VMEM((order, 2 * width), jnp.bfloat16),
                pltpu.VMEM((4 * width, order), jnp.bfloat16),
                pltpu.VMEM((order, order), f32),
                pltpu.VMEM((size, 2 * size), f32),
                pltpu.VMEM((order - size, size), f32),
            ],
            name="front",
        )(maps, turned, arrived)

    def finish(back, turn, before):
        aliases = {2: 0, 3: 1} if before else {}
        anywhere = [pl.BlockSpec(memory_space=pl.ANY)] * len(before)
        return pl.pallas_call(
            functools.partial(finish_kernel, size),
            grid=(n,),
            in_specs=[
                pl.BlockSpec((1, update_rows, order), lambda g: (g * per + turn, 0, 0)),
                pl.BlockSpec((1, update_rows, order), lambda g: (g, 0, 0)),
            ]
            + anywhere,
            out_specs=(
                pl.BlockSpec((1, update_rows, size), lambda g: (g * per + turn, 0, 0)),
                pl.BlockSpec((1, update_rows, order - size), lambda g: (g * per + turn, 0, 0)),
            ),
            out_shape=(
                jax.ShapeDtypeStruct((fronts, update_rows, size), f32),
                jax.ShapeDtypeStruct((fronts, update_rows, order - size), f32),
            ),
            input_output_aliases=aliases,
            name="finish",
        )(front_update, back, *before)

    exchange = functools.partial(lax.all_to_all, axis_name="row", split_axis=0, concat_axis=0, tiled=True)
    arrived = [exchange(pack(turn)) for turn in range(per)]
    negatives = jnp.zeros((), f32)
    backs = []
    for turn in range(per):
        rows_out, pivots = whole_front(arrived[turn], turn)
        backs.append(exchange(rows_out.reshape(n, update_rows, order)))
        negatives = negatives + jnp.sum(jnp.where(pivots < 0.0, 1.0, 0.0))
    done = ()
    for turn in range(per):
        done = finish(backs[turn], turn, done)
    lhat, schur = done
    total = lax.psum(negatives, ("row", "col"))
    negative_share = total / (fronts * lax.axis_size("col") * size)
    return (lhat, schur, negative_share)


def solution(mesh):
    in_specs = (
        P("col", "row", None),
        P("col", "row", None),
        P("col", None, "row", None),
        P("col", None, None),
    )
    out_specs = (P("col", "row", None), P("col", "row", None), P())
    return jax.shard_map(local, mesh=mesh, in_specs=in_specs, out_specs=out_specs, check_vma=False)
```

time: 600 us -> 230 us (0.38)
  waiting for transfers between devices: 275 us -> 56.3 us
  matrix products: 106 us -> 0 us
  other arithmetic: 101 us -> 8.67 us
  Pallas kernels: 0 us -> 71.3 us
  local copies, waits for them, and re-layouts: 62.1 us -> 6.93 us
  blocking collectives: 25.4 us -> 63.3 us
  between operations: 16 us -> 3.77 us
  starting transfers between devices: 11.3 us -> 18.3 us
    all_to_all x2 -> x4, waiting for transfers between devices: 184 us -> 56.3 us  [the longest x2 40.8 us: local(): arrived = [exchange(pack(turn)) for turn in range(per)]]
    dot_general x53 -> x0, matrix products: 105 us -> none  [the longest x16 36.3 us: place_columns(): jnp.dot(rows_placed[0], column_hot[0], precision=highest, preferred_eleme...]
    all_gather x2 -> x0, waiting for transfers between devices: 90.5 us -> none  [the longest x1 58.1 us: local(): lax.all_gather(lhat, 'row', axis=1, tiled=True)]
    pallas_call x0 -> x6, Pallas kernels: none -> 71.3 us  [the longest x2 46.4 us: whole_front(): pl.pallas_call(functools.partial(front_kernel, (n, held, planes, extra_ro...]
    another operation x5 -> x2, other arithmetic: 62.4 us -> 0.89 us  [whole_front(): turned = jnp.stack(turned)]
    psum x1, blocking collectives: 6.67 us -> 63.3 us  [local(): total = lax.psum(negatives, ('row', 'col'))]
    slice x128 -> x2, local copies, waits for them, and re-layouts: 22.7 us -> 1.28 us  [the longest x1 0.69 us: whole_front(): tail = twice[:, at + width // 2:at + width // 2 + held]]
    dynamic_slice x131 -> x0, local copies, waits for them, and re-layouts: 20.3 us -> none  [the longest x128 20.2 us: panel_step(): leading = lax.dynamic_index_in_dim(strip, place, 1, keepdims=False)]
  transfers between devices with their start and end apart: 4 -> 4, of which waited for: 4 -> 3; matrix products, arithmetic and copies ran while one was open for 2% -> 5% of each run, Pallas kernels for 0% -> 26%
where the time goes in v1:
time: 230 us; the launch traced here: 229 us
  Pallas kernels  71.3 us (31%)
  blocking collectives  63.3 us (28%)
  waiting for transfers between devices  56.3 us (24%)
  starting transfers between devices  18.3 us (8%)
  other arithmetic  8.67 us (4%)
  local copies, waits for them, and re-layouts  6.93 us (3%)
  between operations  3.77 us (2%)
    psum x1, blocking collectives, local(): total = lax.psum(negatives, ('row', 'col'))  63.3 us
    pallas_call x2, Pallas kernels, whole_front(): pl.pallas_call(functools.partial(front_kernel, (n, held, planes, extra_ro...  46.4 us
    all_to_all x2, waiting for transfers between devices, local(): arrived = [exchange(pack(turn)) for turn in range(per)]  40.8 us
    all_to_all x2, waiting for transfers between devices, local(): backs.append(exchange(rows_out.reshape(n, update_rows, order)))  15.5 us
    pallas_call x2, Pallas kernels, pack(): pl.pallas_call(functools.partial(pack_kernel, (n, held, planes, extra_row...  12.5 us
    pallas_call x2, Pallas kernels, finish(): pl.pallas_call(functools.partial(finish_kernel, size), grid=(n,), in_spec...  12.3 us
    all_to_all x2, starting transfers between devices, local(): arrived = [exchange(pack(turn)) for turn in range(per)]  10.9 us
    all_to_all x2, starting transfers between devices, local(): backs.append(exchange(rows_out.reshape(n, update_rows, order)))  7.38 us
  transfers between devices with their start and end apart: 4, of which 3 were waited for; matrix products, arithmetic and copies ran while one was open for 5% of the time, Pallas kernels for 26%

profile of v1, /device:TPU:0, one launch (start us, length us, event | category | flops | bytes accessed | tf_op | source)
XLA Modules:
  0.0 228.6 jit_solution(8461176307862130963)
XLA Ops:
  0.6 6.3 %pack.3 = f32[8,384,128]{2,1,0:T(8,128)} custom-call(s32[1]{0:T(128)} %bitcast.9.row_ref, f32[16,2,64,512]{3,2,1,0:T(8,128)} %child_ref.3, f32[16,80,768]{2,1,0:T(8,128)} %update_ref.7, f32[16,16,128]{2,1,0:T(8,128)} %pivot_ref.3), custom_call_target="tpu_custom_call" | custom-call | tf_op jit(solution)/shard_map/pack/pallas_call | solution.py:164
  6.9 7.3 %all-to-all-start.2 = ((f32[8,384,128]{2,1,0:T(8,128)}), f32[8,384,128]{2,1,0:T(8,128)S(1)}, u32[]{:S(2)}, u32[]{:S(2)}) async-start(f32[8,384,128]{2,1,0:T(8,128)} %pack.3), calls=%async_computation.2 | async-start | bytes 3145728 | tf_op jit(solution)/shard_map/all_to_all | solution.py:230
  14.2 6.2 %pack.2 = f32[8,384,128]{2,1,0:T(8,128)} custom-call(s32[1]{0:T(128)} %bitcast.9.row_ref, f32[16,2,64,512]{3,2,1,0:T(8,128)} %child_ref.3, f32[16,80,768]{2,1,0:T(8,128)} %update_ref.7, f32[16,16,128]{2,1,0:T(8,128)} %pivot_ref.3), custom_call_target="tpu_custom_call" | custom-call | tf_op jit(solution)/shard_map/pack/pallas_call | solution.py:164
  20.4 30.8 %all-to-all-done.2.in_ref = f32[8,384,128]{2,1,0:T(8,128)S(1)} async-done(((f32[8,384,128]{2,1,0:T(8,128)}), f32[8,384,128]{2,1,0:T(8,128)S(1)}, u32[]{:S(2)}, u32[]{:S(2)}) %all-to-all-start.2) | async-done | bytes 1572896 | tf_op jit(solution)/shard_map/all_to_all | solution.py:230
  51.2 3.6 %all-to-all-start = ((f32[8,384,128]{2,1,0:T(8,128)}), f32[8,384,128]{2,1,0:T(8,128)S(1)}, u32[]{:S(2)}, u32[]{:S(2)}) async-start(f32[8,384,128]{2,1,0:T(8,128)} %pack.2), calls=%async_computation | async-start | bytes 3145728 | tf_op jit(solution)/shard_map/all_to_all | solution.py:230
  58.7 23.2 %front.3 = (f32[640,768]{1,0:T(8,128)}, f32[1,128]{1,0:T(1,128)}) custom-call(s32[2,512]{1,0:T(2,128)} %copy-done.5, s32[8,2,384]{2,1,0:T(2,128)} %copy-done.6, f32[8,384,128]{2,1,0:T(8,128)} %copy-done.3), custom_call_target="tpu_custom_call" | custom-call | tf_op jit(solution)/shard_map/front/pallas_call | solution.py:190
  81.9 10.1 %all-to-all-done.in_ref = f32[8,384,128]{2,1,0:T(8,128)S(1)} async-done(((f32[8,384,128]{2,1,0:T(8,128)}), f32[8,384,128]{2,1,0:T(8,128)S(1)}, u32[]{:S(2)}, u32[]{:S(2)}) %all-to-all-start) | async-done | bytes 1572896 | tf_op jit(solution)/shard_map/all_to_all | solution.py:230
  92.0 1.2 copy-done.2
  93.2 3.8 %all-to-all-start.3 = ((f32[8,80,768]{2,1,0:T(8,128)}), f32[8,80,768]{2,1,0:T(8,128)S(1)}, u32[]{:S(2)}, u32[]{:S(2)}) async-start(f32[8,80,768]{2,1,0:T(8,128)} %bitcast.71), calls=%async_computation.3 | async-start | bytes 3932160 | tf_op jit(solution)/shard_map/all_to_all | solution.py:235
  96.9 0.8 constant_dynamic-update-slice_fusion.7
  97.7 0.7 constant_dynamic-update-slice_fusion.6
  99.1 0.7 constant_dynamic-update-slice_fusion.4
  99.9 0.8 constant_dynamic-update-slice_fusion.3
  100.7 0.8 constant_dynamic-update-slice_fusion.2
  101.5 0.8 constant_dynamic-update-slice_fusion.1
  102.3 0.8 constant_dynamic-update-slice_fusion.turned_ref
  103.7 23.2 %front.2 = (f32[640,768]{1,0:T(8,128)}, f32[1,128]{1,0:T(1,128)}) custom-call(s32[2,512]{1,0:T(2,128)} %copy-done.4, s32[8,2,384]{2,1,0:T(2,128)} %copy-done.7, f32[8,384,128]{2,1,0:T(8,128)} %copy-done.2), custom_call_target="tpu_custom_call" | custom-call | tf_op jit(solution)/shard_map/front/pallas_call | solution.py:190
  127.0 15.5 %all-to-all-done.3.back_ref = f32[8,80,768]{2,1,0:T(8,128)S(1)} async-done(((f32[8,80,768]{2,1,0:T(8,128)}), f32[8,80,768]{2,1,0:T(8,128)S(1)}, u32[]{:S(2)}, u32[]{:S(2)}) %all-to-all-start.3) | async-done | bytes 1966112 | tf_op jit(solution)/shard_map/all_to_all | solution.py:235
  142.5 1.3 copy-done.1
  143.7 3.6 %all-to-all-start.1 = ((f32[8,80,768]{2,1,0:T(8,128)}), f32[8,80,768]{2,1,0:T(8,128)S(1)}, u32[]{:S(2)}, u32[]{:S(2)}) async-start(f32[8,80,768]{2,1,0:T(8,128)} %bitcast.72), calls=%async_computation.1 | async-start | bytes 3932160 | tf_op jit(solution)/shard_map/all_to_all | solution.py:235
  149.8 63.3 %psum.7 = f32[]{:T(128)} all-reduce(f32[]{:T(128)S(6)} %add.20), channel_id=1, replica_groups=mesh['row'=8,'col'=4] {'row','col'}, use_global_device_ids=true, to_apply=%region_2.3 | all-reduce | flops 1 | bytes 8 | tf_op jit(solution)/shard_map/psum | solution.py:241
  213.8 6.2 %finish.2 = (f32[16,80,128]{2,1,0:T(8,128)}, f32[16,80,640]{2,1,0:T(8,128)}) custom-call(f32[16,80,768]{2,1,0:T(8,128)} %update_ref.7, f32[8,80,768]{2,1,0:T(8,128)} %copy-done.1), custom_call_target="tpu_custom_call" | custom-call | tf_op jit(solution)/shard_map/finish/pallas_call | solution.py:209
  220.0 1.3 copy-done
  221.3 6.2 %finish.3 = (f32[16,80,128]{2,1,0:T(8,128)}, f32[16,80,640]{2,1,0:T(8,128)}) custom-call(f32[16,80,768]{2,1,0:T(8,128)} %update_ref.7, f32[8,80,768]{2,1,0:T(8,128)} %copy-done, f32[16,80,128]{2,1,0:T(8,128)} %get-tuple-element.13.refs_0_, f32[16,80,640]{2,1,0:T(8,128)} %get-tuple-element.14.refs_1_), custom_call_target="tpu_custom_call", output_to_operand_aliasing={{0}: (2, {}), {1}: (3, {})} | custom-call | tf_op jit(solution)/shard_map/finish/pallas_call | solution.py:209
  (33 shorter events, 6.5 us)
Async XLA Ops:
  6.9 44.3 %all-to-all-start.2 = ((f32[8,384,128]{2,1,0:T(8,128)}), f32[8,384,128]{2,1,0:T(8,128)S(1)}, u32[]{:S(2)}, u32[]{:S(2)}) async-start(f32[8,384,128]{2,1,0:T(8,128)} %pack.3), calls=%async_computation.2 | async-start | bytes 3145728 | tf_op jit(solution)/shard_map/all_to_all | solution.py:230
  51.2 7.0 %copy-start.3 = (f32[8,384,128]{2,1,0:T(8,128)}, f32[8,384,128]{2,1,0:T(8,128)S(1)}, u32[]{:S(2)}) copy-start(f32[8,384,128]{2,1,0:T(8,128)S(1)} %all-to-all-done.2.in_ref) | copy-start | bytes 4718596
  51.2 40.8 %all-to-all-start = ((f32[8,384,128]{2,1,0:T(8,128)}), f32[8,384,128]{2,1,0:T(8,128)S(1)}, u32[]{:S(2)}, u32[]{:S(2)}) async-start(f32[8,384,128]{2,1,0:T(8,128)} %pack.2), calls=%async_computation | async-start | bytes 3145728 | tf_op jit(solution)/shard_map/all_to_all | solution.py:230
  55.5 2.6 %copy-start.5 = (s32[2,512]{1,0:T(2,128)}, s32[2,512]{1,0:T(2,128)S(1)}, u32[]{:S(2)}) copy-start(s32[2,512]{1,0:T(2,128)S(1)} %get-tuple-element.19.map_ref) | copy-start | bytes 12292
  55.5 36.5 %copy-start.4 = (s32[2,512]{1,0:T(2,128)}, s32[2,512]{1,0:T(2,128)S(1)}, u32[]{:S(2)}) copy-start(s32[2,512]{1,0:T(2,128)S(1)} %get-tuple-element.20.map_ref) | copy-start | bytes 12292
  58.1 0.6 copy-start.6
  92.0 1.2 copy-start.2
  93.2 49.3 %all-to-all-start.3 = ((f32[8,80,768]{2,1,0:T(8,128)}), f32[8,80,768]{2,1,0:T(8,128)S(1)}, u32[]{:S(2)}, u32[]{:S(2)}) async-start(f32[8,80,768]{2,1,0:T(8,128)} %bitcast.71), calls=%async_computation.3 | async-start | bytes 3932160 | tf_op jit(solution)/shard_map/all_to_all | solution.py:235
  103.1 0.6 copy-start.7
  142.4 1.3 copy-start.1
  142.4 4.9 %copy-start.8 = (f32[1,128]{1,0:T(1,128)S(1)}, f32[1,128]{1,0:T(1,128)}, u32[]{:S(2)}) copy-start(f32[1,128]{1,0:T(1,128)} %get-tuple-element.17) | copy-start | bytes 1540
  142.5 5.5 %copy-start.9 = (f32[1,128]{1,0:T(1,128)S(1)}, f32[1,128]{1,0:T(1,128)}, u32[]{:S(2)}) copy-start(f32[1,128]{1,0:T(1,128)} %get-tuple-element.18) | copy-start | bytes 1540
  143.7 76.3 %all-to-all-start.1 = ((f32[8,80,768]{2,1,0:T(8,128)}), f32[8,80,768]{2,1,0:T(8,128)S(1)}, u32[]{:S(2)}, u32[]{:S(2)}) async-start(f32[8,80,768]{2,1,0:T(8,128)} %bitcast.72), calls=%async_computation.1 | async-start | bytes 3932160 | tf_op jit(solution)/shard_map/all_to_all | solution.py:235
  220.0 1.3 copy-start

commit v2 on v1

v2 whole, which is shorter than its diff:
```python
import functools

import jax
import jax.numpy as jnp
from jax import lax
from jax.experimental import pallas as pl
from jax.experimental.pallas import tpu as pltpu
from jax.sharding import PartitionSpec as P

LANES = 128
highest = lax.Precision.HIGHEST


def split2(x):
    high = x.astype(jnp.bfloat16)
    low = (x - high.astype(jnp.float32)).astype(jnp.bfloat16)
    return high, low


def pack_kernel(dims, row_ref, child_ref, update_ref, pivot_ref, out_ref):
    n, held, extra_rows = dims
    row = row_ref[0]
    half = n // 2
    span = half * held
    place = lax.rem(row, half)
    lane = lax.broadcasted_iota(jnp.int32, (held, LANES), 1)
    lane_extra = lax.broadcasted_iota(jnp.int32, (extra_rows, LANES), 1)
    for front in range(child_ref.shape[0]):
        extras = []
        at = 0
        for child in range(2):
            rolled = pltpu.roll(child_ref[front, 0, child], lax.rem(span - place * held, span), 1)
            near = rolled[:, :LANES]
            out_ref[front, at : at + held, :] = jnp.where(lane < held, 0.5 * near, near)
            at += held
            extras.append(rolled[:, LANES:])
        extra = jnp.where(place < half // 2, extras[0], extras[1])
        packed = extra[:extra_rows]
        for piece in range(1, held // extra_rows):
            rows = pltpu.roll(extra[piece * extra_rows : (piece + 1) * extra_rows], piece * held, 1)
            packed = jnp.where(lane_extra // held == piece, rows, packed)
        out_ref[front, at : at + extra_rows, :] = packed
        at += extra_rows
        out_ref[front, at : at + update_ref.shape[2], :] = update_ref[front, 0]
        at += update_ref.shape[2]
        out_ref[front, at : at + pivot_ref.shape[2], :] = pivot_ref[front, 0]


def inner_kernel(dims, row_ref, child_ref, *refs):
    n, per, turn, span = dims
    outs, sem = refs[:-1], refs[-1]
    row = row_ref[0]
    half = n // 2
    columns = pl.ds(pl.multiple_of((1 - row // half) * span, LANES), span)
    copies = []
    for flip, out_ref in enumerate(outs):
        front = (row ^ flip) * per + turn
        copies.append(pltpu.make_async_copy(child_ref.at[front, :, :, columns], out_ref, sem.at[flip]))
    for copy in copies:
        copy.start()
    for copy in copies:
        copy.wait()


def front_kernel(dims, row_ref, map_ref, in_ref, *refs):
    n, held, extra_rows, update_rows, pivot_rows = dims
    half = n // 2
    inner_refs = refs[:half]
    out_ref, pivots_ref, hot_ref, half_ref, sum_ref, aug_ref, coup_ref = refs[half:]
    row = row_ref[0]
    width = map_ref.shape[-1]
    span = half * held
    order = sum_ref.shape[0]
    size = aug_ref.shape[0]
    f32, bf16 = jnp.float32, jnp.bfloat16

    def hot(indices):
        place = lax.broadcasted_iota(jnp.int32, (order, indices.shape[-1]), 0)
        return jnp.where(place == indices, 1.0, 0.0).astype(bf16)

    last = (((1,), (1,)), ((), ()))

    def spread(values, table):
        high, low = split2(values)
        both = jnp.concatenate([high, low], axis=0)
        return lax.dot_general(both, table, last, preferred_element_type=f32).astype(bf16)

    lane = lax.broadcasted_iota(jnp.int32, (extra_rows, LANES), 1)
    lane8 = lax.broadcasted_iota(jnp.int32, (8, LANES), 1)
    pieces = held // extra_rows
    for child in range(2):
        indices = map_ref[0, child : child + 1, :]
        hot_ref[:, child * width : (child + 1) * width] = hot(indices)
        for source in range(n):
            place = source % half
            start = source // half * span
            turned = jnp.broadcast_to(indices[:, start : start + span], (8, span))
            if place:
                turned = pltpu.roll(turned, span - place * held, 1)
            values = in_ref[source, child * held : (child + 1) * held, :]
            table = turned[:1, :LANES]
            if (place < half // 2) == (child == 0):
                extra = in_ref[source, 2 * held : 2 * held + extra_rows, :]
                values = jnp.concatenate(
                    [
                        values,
                        jnp.concatenate(
                            [jnp.where(lane // held == piece, extra, 0.0) for piece in range(pieces)], axis=0
                        ),
                    ],
                    axis=1,
                )
                far = turned[:, LANES : 2 * LANES]
                tiled = far
                for piece in range(1, pieces):
                    tiled = jnp.where(lane8 // held == piece, pltpu.roll(far, piece * held, 1), tiled)
                table = jnp.concatenate([table, tiled[:1]], axis=1)
            moved = spread(values, hot(table))
            at = child * width + source * held
            half_ref[at : at + held, :] = moved[:held]
            half_ref[2 * width + at : 2 * width + at + held, :] = moved[held:]
        other = hot(jnp.where(row // half == 0, indices[:, span:], indices[:, :span]))
        for flip in range(half):
            moved = spread(inner_refs[flip][child], other)
            at = pl.multiple_of(child * width + (row ^ flip) * held, held)
            half_ref[pl.ds(at, held), :] += moved[:held]
            half_ref[pl.ds(2 * width + at, held), :] += moved[held:]
    for block in range(order // LANES):
        rows = pl.ds(block * LANES, LANES)
        sum_ref[rows, :] = jnp.dot(
            hot_ref[rows, :], half_ref[: 2 * width, :], preferred_element_type=f32
        ) + jnp.dot(hot_ref[rows, :], half_ref[2 * width :, :], preferred_element_type=f32)

    at = 2 * held + extra_rows
    for source in range(n):
        coup_ref[source * update_rows : (source + 1) * update_rows, :] = in_ref[
            source, at : at + update_rows, :
        ]
        aug_ref[source * pivot_rows : (source + 1) * pivot_rows, :size] = in_ref[
            source, at + update_rows : at + update_rows + pivot_rows, :
        ]
    coup_ref[...] += sum_ref[size:, :size] + sum_ref[:size, size:].T
    aug_ref[:, :size] += sum_ref[:size, :size] + sum_ref[:size, :size].T
    square = (size, size)
    aug_ref[:, size:] = jnp.where(
        lax.broadcasted_iota(jnp.int32, square, 0) == lax.broadcasted_iota(jnp.int32, square, 1), 1.0, 0.0
    )

    lanes = lax.broadcasted_iota(jnp.int32, (1, size), 1)
    step = 32
    pivots = jnp.zeros((1, size), f32)
    for start in range(0, size, step):
        rest = size - start
        below = start + lax.broadcasted_iota(jnp.int32, (rest, 1), 0)

        def eliminate(k, pivots, start=start, below=below):
            row = aug_ref[pl.ds(k, 1), :]
            whole = aug_ref[start:, :]
            chosen = lanes == k
            column = jnp.sum(jnp.where(chosen, whole[:, :size], 0.0), axis=1, keepdims=True)
            pivot = jnp.sum(jnp.where(chosen, row[:, :size], 0.0), axis=1, keepdims=True)
            multiplier = jnp.where(below > k, column / pivot, 0.0)
            aug_ref[start:, :] = whole - multiplier * row
            return jnp.where(chosen, pivot, pivots)

        pivots = lax.fori_loop(start, start + step, eliminate, pivots)
    pivots_ref[...] = pivots

    lhat = lax.dot_general(coup_ref[...], aug_ref[:, size:], last, precision=highest, preferred_element_type=f32)
    out_ref[:, :size] = lhat
    coup_ref[...] = lhat / pivots
    for start in range(0, order - size, LANES):
        rows = pl.ds(start, LANES)
        correction = lax.dot_general(
            coup_ref[rows, :], out_ref[:, :size], last, precision=highest, preferred_element_type=f32
        )
        here = size + start
        out_ref[rows, size:] = (
            sum_ref[here : here + LANES, size:] + sum_ref[size:, here : here + LANES].T - correction
        )


def finish_kernel(size, update_ref, back_ref, *refs):
    lhat_ref, schur_ref = refs[-2:]
    count = update_ref.shape[0]
    rows = pl.ds(pl.program_id(0) * count, count)
    lhat_ref[:, 0] = back_ref[rows, :, :size]
    schur_ref[:, 0] = update_ref[:, 0, :, size:] + back_ref[rows, :, size:]


def local(front_pivot, front_update, child_blocks, child_map):
    f32 = jnp.float32
    n = lax.axis_size("row")
    half = n // 2
    my_row = lax.axis_index("row")
    fronts, pivot_rows, size = front_pivot.shape
    update_rows, order = front_update.shape[1:]
    held, width = child_blocks.shape[2:]
    per = fronts // n
    span = half * held
    extra_rows = held * held // LANES
    rows = 2 * held + extra_rows + update_rows + pivot_rows
    row_number = my_row.astype(jnp.int32).reshape(1)
    dims = (n, held, extra_rows)
    group = n // 2
    vmem = pl.BlockSpec(memory_space=pltpu.VMEM)
    whole = pl.BlockSpec(memory_space=pl.ANY)

    def pack(turn):
        return pl.pallas_call(
            functools.partial(pack_kernel, dims),
            grid_spec=pltpu.PrefetchScalarGridSpec(
                num_scalar_prefetch=1,
                grid=(n // group,),
                in_specs=[
                    pl.BlockSpec((group, 1, 2, held, span), lambda g, r: (g, turn, 0, 0, r[0] // half)),
                    pl.BlockSpec((group, 1, update_rows, size), lambda g, r: (g, turn, 0, 0)),
                    pl.BlockSpec((group, 1, pivot_rows, size), lambda g, r: (g, turn, 0, 0)),
                ],
                out_specs=pl.BlockSpec((group, rows, LANES), lambda g, r: (g, 0, 0)),
            ),
            out_shape=jax.ShapeDtypeStruct((n, rows, LANES), f32),
            name="pack",
        )(
            row_number,
            child_blocks.reshape(n, per, 2, held, width),
            front_update.reshape(n, per, update_rows, order),
            front_pivot.reshape(n, per, pivot_rows, size),
        )

    def inner(turn):
        return pl.pallas_call(
            functools.partial(inner_kernel, (n, per, turn, span)),
            in_specs=[pl.BlockSpec(memory_space=pltpu.SMEM), whole],
            out_specs=[whole] * half,
            out_shape=[jax.ShapeDtypeStruct((2, held, span), f32)] * half,
            scratch_shapes=[pltpu.SemaphoreType.DMA((half,))],
            name="inner",
        )(row_number, child_blocks)

    def whole_front(arrived, inners, turn):
        return pl.pallas_call(
            functools.partial(front_kernel, dims + (update_rows, pivot_rows)),
            grid_spec=pltpu.PrefetchScalarGridSpec(
                num_scalar_prefetch=1,
                grid=(1,),
                in_specs=[pl.BlockSpec((1, 2, width), lambda g, r: (r[0] * per + turn, 0, 0))]
                + [vmem] * (half + 1),
                out_specs=(vmem, vmem),
                scratch_shapes=[
                    pltpu.VMEM((order, 2 * width), jnp.bfloat16),
                    pltpu.VMEM((4 * width, order), jnp.bfloat16),
                    pltpu.VMEM((order, order), f32),
                    pltpu.VMEM((size, 2 * size), f32),
                    pltpu.VMEM((order - size, size), f32),
                ],
            ),
            out_shape=(
                jax.ShapeDtypeStruct((order - size, order), f32),
                jax.ShapeDtypeStruct((1, size), f32),
            ),
            name="front",
        )(row_number, child_map, arrived, *inners)

    def finish(back, turn, before):
        aliases = {2: 0, 3: 1} if before else {}
        group = 2
        place = lambda g: (g, turn, 0, 0)
        return pl.pallas_call(
            functools.partial(finish_kernel, size),
            grid=(n // group,),
            in_specs=[pl.BlockSpec((group, 1, update_rows, order), place), vmem] + [whole] * len(before),
            out_specs=(
                pl.BlockSpec((group, 1, update_rows, size), place),
                pl.BlockSpec((group, 1, update_rows, order - size), place),
            ),
            out_shape=(
                jax.ShapeDtypeStruct((n, per, update_rows, size), f32),
                jax.ShapeDtypeStruct((n, per, update_rows, order - size), f32),
            ),
            input_output_aliases=aliases,
            name="finish",
        )(front_update.reshape(n, per, update_rows, order), back, *before)

    exchange = functools.partial(lax.all_to_all, axis_name="row", split_axis=0, concat_axis=0, tiled=True)

    def near(parts):
        return [parts[0]] + [
            lax.ppermute(parts[flip], "row", [(i, i ^ flip) for i in range(n)]) for flip in range(1, half)
        ]

    packed = [pack(turn) for turn in range(per)]
    inners = [near(inner(turn)) for turn in range(per)]
    arrived = [exchange(packed[turn]) for turn in range(per)]
    total = jnp.zeros((), f32)
    backs = []
    for turn in range(per):
        rows_out, pivots = whole_front(arrived[turn], inners[turn], turn)
        total = total + jnp.sum(jnp.where(pivots < 0.0, 1.0, 0.0))
        if turn == per - 1:
            total = lax.psum(total, ("row", "col"))
            rows_out, total = lax.optimization_barrier((rows_out, total))
        backs.append(exchange(rows_out.reshape(n, update_rows, order)))
    done = ()
    for turn in range(per):
        done = finish(backs[turn], turn, done)
    lhat, schur = done
    negative_share = total / (fronts * lax.axis_size("col") * size)
    return (
        lhat.reshape(fronts, update_rows, size),
        schur.reshape(fronts, update_rows, order - size),
        negative_share,
    )


def solution(mesh):
    in_specs = (
        P("col", "row", None),
        P("col", "row", None),
        P("col", None, "row", None),
        P("col", None, None),
    )
    out_specs = (P("col", "row", None), P("col", "row", None), P())
    return jax.shard_map(local, mesh=mesh, in_specs=in_specs, out_specs=out_specs, check_vma=False)
```

time: 230 us -> 267 us (1.16)
  waiting for transfers between devices: 56.3 us -> 90 us
  Pallas kernels: 71.3 us -> 95.1 us
  blocking collectives: 63.3 us -> 42.7 us
  starting transfers between devices: 18.3 us -> 29.2 us
  other arithmetic: 8.67 us -> 1.86 us
  local copies, waits for them, and re-layouts: 6.93 us -> 3.88 us
    ppermute x0 -> x6, waiting for transfers between devices: none -> 27 us  [near(): lax.ppermute(parts[flip], 'row', [(i, i ^ flip) for i in range(n)])]
    all_to_all x2, waiting for transfers between devices: 15.5 us -> 39.8 us  [local(): backs.append(exchange(rows_out.reshape(n, update_rows, order)))]
    pallas_call x6 -> x8, Pallas kernels: 71.3 us -> 95.1 us  [the longest x2 47 us: whole_front(): pl.pallas_call(functools.partial(front_kernel, dims + (update_rows, pivot...]
    psum x1, blocking collectives: 63.3 us -> 42.7 us  [local(): total = lax.psum(total, ('row', 'col'))]
    all_to_all x2, waiting for transfers between devices: 40.8 us -> 23.2 us  [local(): arrived = [exchange(packed[turn]) for turn in range(per)]]
    ppermute x0 -> x6, starting transfers between devices: none -> 7.23 us  [near(): lax.ppermute(parts[flip], 'row', [(i, i ^ flip) for i in range(n)])]
    unnamed x14 -> x0, other arithmetic: 5.9 us -> none
    all_to_all x2, starting transfers between devices: 7.38 us -> 11 us  [local(): backs.append(exchange(rows_out.reshape(n, update_rows, order)))]
  transfers between devices with their start and end apart: 4 -> 10, of which waited for: 3 -> 8; matrix products, arithmetic and copies ran while one was open for 5% -> 1% of each run, Pallas kernels for 26% -> 33%
where the time goes in v2:
time: 267 us; the launch traced here: 266 us
  Pallas kernels  95.1 us (36%)
  waiting for transfers between devices  90 us (34%)
  blocking collectives  42.7 us (16%)
  starting transfers between devices  29.2 us (11%)
  local copies, waits for them, and re-layouts  3.88 us (1%)
  between operations  3.77 us (1%)
    pallas_call x2, Pallas kernels, whole_front(): pl.pallas_call(functools.partial(front_kernel, dims + (update_rows, pivot...  47 us
    psum x1, blocking collectives, local(): total = lax.psum(total, ('row', 'col'))  42.7 us
    all_to_all x2, waiting for transfers between devices, local(): backs.append(exchange(rows_out.reshape(n, update_rows, order)))  39.8 us
    pallas_call x2, Pallas kernels, inner(): pl.pallas_call(functools.partial(inner_kernel, (n, per, turn, span)), in_...  34 us
    ppermute x6, waiting for transfers between devices, near(): lax.ppermute(parts[flip], 'row', [(i, i ^ flip) for i in range(n)])  27 us
    all_to_all x2, waiting for transfers between devices, local(): arrived = [exchange(packed[turn]) for turn in range(per)]  23.2 us
    all_to_all x2, starting transfers between devices, local(): backs.append(exchange(rows_out.reshape(n, update_rows, order)))  11 us
    all_to_all x2, starting transfers between devices, local(): arrived = [exchange(packed[turn]) for turn in range(per)]  10.9 us
  transfers between devices with their start and end apart: 10, of which 8 were waited for; matrix products, arithmetic and copies ran while one was open for 1% of the time, Pallas kernels for 33%

profile of v2, /device:TPU:0, one launch (start us, length us, event | category | flops | bytes accessed | tf_op | source)
XLA Modules:
  0.0 266.4 jit_solution(12039247992603696529)
XLA Ops:
  0.6 2.5 pack.3
  3.2 7.3 %all-to-all-start.1 = ((f32[8,256,128]{2,1,0:T(8,128)}), f32[8,256,128]{2,1,0:T(8,128)S(1)}, u32[]{:S(2)}, u32[]{:S(2)}) async-start(f32[8,256,128]{2,1,0:T(8,128)} %pack.3), calls=%async_computation.1 | async-start | bytes 2097152 | tf_op jit(solution)/shard_map/all_to_all | solution.py:294
  10.5 2.5 pack.2
  13.0 23.2 %all-to-all-done.1.in_ref = f32[8,256,128]{2,1,0:T(8,128)S(1)} async-done(((f32[8,256,128]{2,1,0:T(8,128)}), f32[8,256,128]{2,1,0:T(8,128)S(1)}, u32[]{:S(2)}, u32[]{:S(2)}) %all-to-all-start.1) | async-done | bytes 1048608 | tf_op jit(solution)/shard_map/all_to_all | solution.py:294
  36.2 3.6 %all-to-all-start = ((f32[8,256,128]{2,1,0:T(8,128)}), f32[8,256,128]{2,1,0:T(8,128)S(1)}, u32[]{:S(2)}, u32[]{:S(2)}) async-start(f32[8,256,128]{2,1,0:T(8,128)} %pack.2), calls=%async_computation | async-start | bytes 2097152 | tf_op jit(solution)/shard_map/all_to_all | solution.py:294
  39.8 17.0 %inner.3 = (f32[2,64,256]{2,1,0:T(8,128)}, f32[2,64,256]{2,1,0:T(8,128)}, f32[2,64,256]{2,1,0:T(8,128)}, f32[2,64,256]{2,1,0:T(8,128)}) custom-call(s32[1]{0:T(128)} %bitcast.1.row_ref, f32[16,2,64,512]{3,2,1,0:T(8,128)} %child_ref.3), custom_call_target="tpu_custom_call" | custom-call | tf_op jit(solution)/shard_map/inner/pallas_call | solution.py:232
  56.9 2.1 collective-permute-start.3
  58.9 1.5 collective-permute-start.4
  60.5 2.9 %collective-permute-done.3.refs_1_ = f32[2,64,256]{2,1,0:T(8,128)S(1)} collective-permute-done((f32[2,64,256]{2,1,0:T(8,128)}, f32[2,64,256]{2,1,0:T(8,128)S(1)}, u32[]{:S(2)}, u32[]{:S(2)}) %collective-permute-start.3) | collective-permute-done | bytes 131104 | tf_op jit(solution)/shard_map/ppermute | solution.py:289
  63.3 5.3 %collective-permute-done.4.refs_2_ = f32[2,64,256]{2,1,0:T(8,128)S(1)} collective-permute-done((f32[2,64,256]{2,1,0:T(8,128)}, f32[2,64,256]{2,1,0:T(8,128)S(1)}, u32[]{:S(2)}, u32[]{:S(2)}) %collective-permute-start.4) | collective-permute-done | bytes 131104 | tf_op jit(solution)/shard_map/ppermute | solution.py:289
  69.9 23.5 %front.3 = (f32[640,768]{1,0:T(8,128)}, f32[1,128]{1,0:T(1,128)}) custom-call(s32[1]{0:T(128)} %bitcast.1.row_ref, s32[16,2,512]{2,1,0:T(2,128)} %map_ref.3, f32[8,256,128]{2,1,0:T(8,128)} %copy-done.3, f32[2,64,256]{2,1,0:T(8,128)} %get-tuple-element.26.refs_0_, f32[2,64,256]{2,1,0:T(8,128)} %copy-done.5, f32[2,64,256]{2,1,0:T(8,128)} %copy-done.7, ...), custom_call_target="tpu_custom_call" | custom-call | tf_op jit(solution)/shard_map/front/pallas_call | solution.py:242
  93.4 5.9 %all-to-all-start.3 = ((f32[8,80,768]{2,1,0:T(8,128)}), f32[8,80,768]{2,1,0:T(8,128)S(1)}, u32[]{:S(2)}, u32[]{:S(2)}) async-start(f32[8,80,768]{2,1,0:T(8,128)} %bitcast.15), calls=%async_computation.3 | async-start | bytes 3932160 | tf_op jit(solution)/shard_map/all_to_all | solution.py:303
  99.3 17.0 %inner.2 = (f32[2,64,256]{2,1,0:T(8,128)}, f32[2,64,256]{2,1,0:T(8,128)}, f32[2,64,256]{2,1,0:T(8,128)}, f32[2,64,256]{2,1,0:T(8,128)}) custom-call(s32[1]{0:T(128)} %bitcast.1.row_ref, f32[16,2,64,512]{3,2,1,0:T(8,128)} %child_ref.3), custom_call_target="tpu_custom_call" | custom-call | tf_op jit(solution)/shard_map/inner/pallas_call | solution.py:232
  116.3 2.1 collective-permute-start
  118.4 1.5 collective-permute-start.1
  120.0 5.7 %collective-permute-done.refs_1_ = f32[2,64,256]{2,1,0:T(8,128)S(1)} collective-permute-done((f32[2,64,256]{2,1,0:T(8,128)}, f32[2,64,256]{2,1,0:T(8,128)S(1)}, u32[]{:S(2)}, u32[]{:S(2)}) %collective-permute-start) | collective-permute-done | bytes 131104 | tf_op jit(solution)/shard_map/ppermute | solution.py:289
  125.6 10.7 %collective-permute-done.1.refs_2_ = f32[2,64,256]{2,1,0:T(8,128)S(1)} collective-permute-done((f32[2,64,256]{2,1,0:T(8,128)}, f32[2,64,256]{2,1,0:T(8,128)S(1)}, u32[]{:S(2)}, u32[]{:S(2)}) %collective-permute-start.1) | collective-permute-done | bytes 131104 | tf_op jit(solution)/shard_map/ppermute | solution.py:289
  136.3 1.9 collective-permute-done.2.refs_3_
  138.8 23.5 %front.2 = (f32[640,768]{1,0:T(8,128)}, f32[1,128]{1,0:T(1,128)}) custom-call(s32[1]{0:T(128)} %bitcast.1.row_ref, s32[16,2,512]{2,1,0:T(2,128)} %map_ref.3, f32[8,256,128]{2,1,0:T(8,128)} %copy-done.2, f32[2,64,256]{2,1,0:T(8,128)} %get-tuple-element.21.refs_0_, f32[2,64,256]{2,1,0:T(8,128)} %copy-done.4, f32[2,64,256]{2,1,0:T(8,128)} %copy-done.6, ...), custom_call_target="tpu_custom_call" | custom-call | tf_op jit(solution)/shard_map/front/pallas_call | solution.py:242
  165.5 42.7 %psum.7 = f32[]{:T(128)} all-reduce(f32[]{:T(128)S(6)} %add.5), channel_id=1, replica_groups=mesh['row'=8,'col'=4] {'row','col'}, use_global_device_ids=true, to_apply=%region_2.3 | all-reduce | flops 1 | bytes 8 | tf_op jit(solution)/shard_map/psum | solution.py:301
  209.5 5.2 %all-to-all-start.2 = ((f32[8,80,768]{2,1,0:T(8,128)}), f32[8,80,768]{2,1,0:T(8,128)S(1)}, u32[]{:S(2)}, u32[]{:S(2)}) async-start(f32[8,80,768]{2,1,0:T(8,128)} %bitcast.16), calls=%async_computation.2 | async-start | bytes 3932160 | tf_op jit(solution)/shard_map/all_to_all | solution.py:303
  215.3 4.5 %finish.2 = (f32[8,2,80,128]{3,2,1,0:T(8,128)}, f32[8,2,80,640]{3,2,1,0:T(8,128)}) custom-call(f32[8,2,80,768]{3,2,1,0:T(8,128)} %bitcast.12, f32[8,80,768]{2,1,0:T(8,128)} %copy-done.1), custom_call_target="tpu_custom_call" | custom-call | tf_op jit(solution)/shard_map/finish/pallas_call | solution.py:269
  219.8 39.8 %all-to-all-done.2.back_ref = f32[8,80,768]{2,1,0:T(8,128)S(1)} async-done(((f32[8,80,768]{2,1,0:T(8,128)}), f32[8,80,768]{2,1,0:T(8,128)S(1)}, u32[]{:S(2)}, u32[]{:S(2)}) %all-to-all-start.2) | async-done | bytes 1966112 | tf_op jit(solution)/shard_map/all_to_all | solution.py:303
  260.8 4.4 %finish.3 = (f32[8,2,80,128]{3,2,1,0:T(8,128)}, f32[8,2,80,640]{3,2,1,0:T(8,128)}) custom-call(f32[8,2,80,768]{3,2,1,0:T(8,128)} %bitcast.13, f32[8,80,768]{2,1,0:T(8,128)} %copy-done, f32[8,2,80,128]{3,2,1,0:T(8,128)} %get-tuple-element.34.refs_0_, f32[8,2,80,640]{3,2,1,0:T(8,128)} %get-tuple-element.35.refs_1_), custom_call_target="tpu_custom_call", output_to_operand_aliasing={{0}: (2, {}), {1}: (3, {})} | custom-call | tf_op jit(solution)/shard_map/finish/pallas_call | solution.py:269
  (29 shorter events, 6.5 us)
Async XLA Ops:
  3.2 33.0 %all-to-all-start.1 = ((f32[8,256,128]{2,1,0:T(8,128)}), f32[8,256,128]{2,1,0:T(8,128)S(1)}, u32[]{:S(2)}, u32[]{:S(2)}) async-start(f32[8,256,128]{2,1,0:T(8,128)} %pack.3), calls=%async_computation.1 | async-start | bytes 2097152 | tf_op jit(solution)/shard_map/all_to_all | solution.py:294
  36.2 33.0 %copy-start.3 = (f32[8,256,128]{2,1,0:T(8,128)}, f32[8,256,128]{2,1,0:T(8,128)S(1)}, u32[]{:S(2)}) copy-start(f32[8,256,128]{2,1,0:T(8,128)S(1)} %all-to-all-done.1.in_ref) | copy-start | bytes 3145732
  36.2 57.2 %all-to-all-start = ((f32[8,256,128]{2,1,0:T(8,128)}), f32[8,256,128]{2,1,0:T(8,128)S(1)}, u32[]{:S(2)}, u32[]{:S(2)}) async-start(f32[8,256,128]{2,1,0:T(8,128)} %pack.2), calls=%async_computation | async-start | bytes 2097152 | tf_op jit(solution)/shard_map/all_to_all | solution.py:294
  56.9 6.5 %collective-permute-start.3 = (f32[2,64,256]{2,1,0:T(8,128)}, f32[2,64,256]{2,1,0:T(8,128)S(1)}, u32[]{:S(2)}, u32[]{:S(2)}) collective-permute-start(f32[2,64,256]{2,1,0:T(8,128)} %get-tuple-element.27), channel_id=1, source_target_pairs={{0,4},{4,0},{8,12},{12,8},{16,20},{20,16},{24,28},{28,24},{1,5},{5... | collective-permute-start | bytes 393224 | tf_op jit(solution)/shard_map/ppermute | solution.py:289
  58.9 9.7 %collective-permute-start.4 = (f32[2,64,256]{2,1,0:T(8,128)}, f32[2,64,256]{2,1,0:T(8,128)S(1)}, u32[]{:S(2)}, u32[]{:S(2)}) collective-permute-start(f32[2,64,256]{2,1,0:T(8,128)} %get-tuple-element.28), channel_id=1, source_target_pairs={{0,8},{4,12},{8,0},{12,4},{16,24},{20,28},{24,16},{28,20},{1,9},{5... | collective-permute-start | bytes 393224 | tf_op jit(solution)/shard_map/ppermute | solution.py:289
  60.4 8.8 %collective-permute-start.5 = (f32[2,64,256]{2,1,0:T(8,128)}, f32[2,64,256]{2,1,0:T(8,128)S(1)}, u32[]{:S(2)}, u32[]{:S(2)}) collective-permute-start(f32[2,64,256]{2,1,0:T(8,128)} %get-tuple-element.29), channel_id=1, source_target_pairs={{0,12},{4,8},{8,4},{12,0},{16,28},{20,24},{24,20},{28,16},{1,13},{... | collective-permute-start | bytes 393224 | tf_op jit(solution)/shard_map/ppermute | solution.py:289
  63.3 5.9 %copy-start.5 = (f32[2,64,256]{2,1,0:T(8,128)}, f32[2,64,256]{2,1,0:T(8,128)S(1)}, u32[]{:S(2)}) copy-start(f32[2,64,256]{2,1,0:T(8,128)S(1)} %collective-permute-done.3.refs_1_) | copy-start | bytes 393220
  68.7 0.6 copy-start.7
  69.2 0.7 copy-start.9
  93.4 22.9 %copy-start.2 = (f32[8,256,128]{2,1,0:T(8,128)}, f32[8,256,128]{2,1,0:T(8,128)S(1)}, u32[]{:S(2)}) copy-start(f32[8,256,128]{2,1,0:T(8,128)S(1)} %all-to-all-done.in_ref) | copy-start | bytes 3145732
  93.4 114.8 %all-to-all-start.3 = ((f32[8,80,768]{2,1,0:T(8,128)}), f32[8,80,768]{2,1,0:T(8,128)S(1)}, u32[]{:S(2)}, u32[]{:S(2)}) async-start(f32[8,80,768]{2,1,0:T(8,128)} %bitcast.15), calls=%async_computation.3 | async-start | bytes 3932160 | tf_op jit(solution)/shard_map/all_to_all | solution.py:303
  99.3 63.1 %copy-start.10 = (f32[1,128]{1,0:T(1,128)S(1)}, f32[1,128]{1,0:T(1,128)}, u32[]{:S(2)}) copy-start(f32[1,128]{1,0:T(1,128)} %get-tuple-element.30) | copy-start | bytes 1540
  116.3 9.3 %collective-permute-start = (f32[2,64,256]{2,1,0:T(8,128)}, f32[2,64,256]{2,1,0:T(8,128)S(1)}, u32[]{:S(2)}, u32[]{:S(2)}) collective-permute-start(f32[2,64,256]{2,1,0:T(8,128)} %get-tuple-element.22), channel_id=1, source_target_pairs={{0,4},{4,0},{8,12},{12,8},{16,20},{20,16},{24,28},{28,24},{1,5},{5... | collective-permute-start | bytes 393224 | tf_op jit(solution)/shard_map/ppermute | solution.py:289
  118.4 17.9 %collective-permute-start.1 = (f32[2,64,256]{2,1,0:T(8,128)}, f32[2,64,256]{2,1,0:T(8,128)S(1)}, u32[]{:S(2)}, u32[]{:S(2)}) collective-permute-start(f32[2,64,256]{2,1,0:T(8,128)} %get-tuple-element.23), channel_id=1, source_target_pairs={{0,8},{4,12},{8,0},{12,4},{16,24},{20,28},{24,16},{28,20},{1,9},{5... | collective-permute-start | bytes 393224 | tf_op jit(solution)/shard_map/ppermute | solution.py:289
  119.9 18.3 %collective-permute-start.2 = (f32[2,64,256]{2,1,0:T(8,128)}, f32[2,64,256]{2,1,0:T(8,128)S(1)}, u32[]{:S(2)}, u32[]{:S(2)}) collective-permute-start(f32[2,64,256]{2,1,0:T(8,128)} %get-tuple-element.24), channel_id=1, source_target_pairs={{0,12},{4,8},{8,4},{12,0},{16,28},{20,24},{24,20},{28,16},{1,13},{... | collective-permute-start | bytes 393224 | tf_op jit(solution)/shard_map/ppermute | solution.py:289
  125.6 12.6 %copy-start.4 = (f32[2,64,256]{2,1,0:T(8,128)}, f32[2,64,256]{2,1,0:T(8,128)S(1)}, u32[]{:S(2)}) copy-start(f32[2,64,256]{2,1,0:T(8,128)S(1)} %collective-permute-done.refs_1_) | copy-start | bytes 393220
  136.3 1.9 copy-start.6
  138.2 0.6 copy-start.8
  208.2 1.3 copy-start.1
  209.5 50.0 %all-to-all-start.2 = ((f32[8,80,768]{2,1,0:T(8,128)}), f32[8,80,768]{2,1,0:T(8,128)S(1)}, u32[]{:S(2)}, u32[]{:S(2)}) async-start(f32[8,80,768]{2,1,0:T(8,128)} %bitcast.16), calls=%async_computation.2 | async-start | bytes 3932160 | tf_op jit(solution)/shard_map/all_to_all | solution.py:303
  259.5 1.3 copy-start

commit v3 on v2

--- a/solution.py
+++ b/solution.py
@@ -6,6 +6,7 @@
 from jax.experimental import pallas as pl
 from jax.experimental.pallas import tpu as pltpu
 from jax.sharding import PartitionSpec as P
+
 
 LANES = 128
 highest = lax.Precision.HIGHEST
@@ -46,28 +47,15 @@
         out_ref[front, at : at + pivot_ref.shape[2], :] = pivot_ref[front, 0]
 
 
-def inner_kernel(dims, row_ref, child_ref, *refs):
-    n, per, turn, span = dims
-    outs, sem = refs[:-1], refs[-1]
-    row = row_ref[0]
-    half = n // 2
-    columns = pl.ds(pl.multiple_of((1 - row // half) * span, LANES), span)
-    copies = []
-    for flip, out_ref in enumerate(outs):
-        front = (row ^ flip) * per + turn
-        copies.append(pltpu.make_async_copy(child_ref.at[front, :, :, columns], out_ref, sem.at[flip]))
-    for copy in copies:
-        copy.start()
-    for copy in copies:
-        copy.wait()
-
-
-def front_kernel(dims, row_ref, map_ref, in_ref, *refs):
+def inner_kernel(*refs):
+    count = (len(refs) - 1) // 2
+    for in_ref, out_ref in zip(refs[1 : 1 + count], refs[1 + count :]):
+        out_ref[...] = in_ref[0]
+
+
+def assemble(dims, row, map_ref, in_ref, inner_refs, hot_ref, half_ref, sum_ref, aug_ref, coup_ref):
     n, held, extra_rows, update_rows, pivot_rows = dims
     half = n // 2
-    inner_refs = refs[:half]
-    out_ref, pivots_ref, hot_ref, half_ref, sum_ref, aug_ref, coup_ref = refs[half:]
-    row = row_ref[0]
     width = map_ref.shape[-1]
     span = half * held
     order = sum_ref.shape[0]
@@ -146,14 +134,17 @@
         lax.broadcasted_iota(jnp.int32, square, 0) == lax.broadcasted_iota(jnp.int32, square, 1), 1.0, 0.0
     )
 
+
+def eliminate(aug_ref):
+    size = aug_ref.shape[0]
     lanes = lax.broadcasted_iota(jnp.int32, (1, size), 1)
     step = 32
-    pivots = jnp.zeros((1, size), f32)
+    pivots = jnp.zeros((1, size), jnp.float32)
     for start in range(0, size, step):
         rest = size - start
         below = start + lax.broadcasted_iota(jnp.int32, (rest, 1), 0)
 
-        def eliminate(k, pivots, start=start, below=below):
+        def one(k, pivots, start=start, below=below):
             row = aug_ref[pl.ds(k, 1), :]
             whole = aug_ref[start:, :]
             chosen = lanes == k
@@ -163,21 +154,71 @@
             aug_ref[start:, :] = whole - multiplier * row
             return jnp.where(chosen, pivot, pivots)
 
-        pivots = lax.fori_loop(start, start + step, eliminate, pivots)
-    pivots_ref[...] = pivots
-
-    lhat = lax.dot_general(coup_ref[...], aug_ref[:, size:], last, precision=highest, preferred_element_type=f32)
+        pivots = lax.fori_loop(start, start + step, one, pivots)
+    return pivots
+
+
+def trailing(sum_ref, size, start):
+    here = size + start
+    return sum_ref[here : here + LANES, size:] + sum_ref[size:, here : here + LANES].T
+
+
+LAST = (((1,), (1,)), ((), ()))
+
+
+def update(out_ref, coup_ref, inverse, pivots, trailing_rows):
+    size = inverse.shape[0]
+    f32 = jnp.float32
+    lhat = lax.dot_general(coup_ref[...], inverse, LAST, precision=highest, preferred_element_type=f32)
     out_ref[:, :size] = lhat
     coup_ref[...] = lhat / pivots
-    for start in range(0, order - size, LANES):
+    for start in range(0, out_ref.shape[0], LANES):
         rows = pl.ds(start, LANES)
         correction = lax.dot_general(
-            coup_ref[rows, :], out_ref[:, :size], last, precision=highest, preferred_element_type=f32
+            coup_ref[rows, :], out_ref[:, :size], LAST, precision=highest, preferred_element_type=f32
         )
-        here = size + start
-        out_ref[rows, size:] = (
-            sum_ref[here : here + LANES, size:] + sum_ref[size:, here : here + LANES].T - correction
-        )
+        out_ref[rows, size:] = trailing_rows(start) - correction
+
+
+def front_kernel(dims, row_ref, map_ref, in_ref, *refs):
+    half = dims[0] // 2
+    out_ref, pivots_ref, hot_ref, half_ref, sum_ref, aug_ref, coup_ref = refs[half:]
+    assemble(dims, row_ref[0], map_ref, in_ref, refs[:half], hot_ref, half_ref, sum_ref, aug_ref, coup_ref)
+    size = aug_ref.shape[0]
+    pivots = eliminate(aug_ref)
+    pivots_ref[...] = pivots
+    update(out_ref, coup_ref, aug_ref[:, size:], pivots, functools.partial(trailing, sum_ref, size))
+
+
+def factor_kernel(dims, row_ref, map_ref, in_ref, *refs):
+    half = dims[0] // 2
+    trail_ref, coup_ref, inverse_ref, pivots_ref, hot_ref, half_ref, sum_ref, aug_ref = refs[half:]
+    assemble(dims, row_ref[0], map_ref, in_ref, refs[:half], hot_ref, half_ref, sum_ref, aug_ref, coup_ref)
+    size = aug_ref.shape[0]
+    pivots_ref[...] = eliminate(aug_ref)
+    inverse_ref[...] = aug_ref[:, size:]
+    for start in range(0, trail_ref.shape[0], LANES):
+        trail_ref[pl.ds(start, LANES), :] = trailing(sum_ref, size, start)
+
+
+def schur_kernel(row_ref, count_ref, trail_ref, coup_in_ref, inverse_ref, pivots_ref, *refs):
+    out_refs = refs[:-2]
+    full_ref, coup_ref = refs[-2:]
+    coup_ref[...] = coup_in_ref[...]
+    update(
+        full_ref, coup_ref, inverse_ref[...], pivots_ref[...], lambda start: trail_ref[pl.ds(start, LANES), :]
+    )
+    update_rows, order = out_refs[0].shape
+    size = inverse_ref.shape[0]
+    shape = (8, order)
+    first = lax.broadcasted_iota(jnp.int32, shape, 0)
+    second = lax.broadcasted_iota(jnp.int32, shape, 1)
+    for flip, out_ref in enumerate(out_refs):
+        home = row_ref[0] ^ flip
+        at = pl.multiple_of(home * update_rows, 8)
+        out_ref[...] = full_ref[pl.ds(at, update_rows), :]
+        chosen = (first == 1) & (second == size + at)
+        out_ref[:8, :] = jnp.where(chosen, count_ref[0], full_ref[pl.ds(at, 8), :])
 
 
 def finish_kernel(size, update_ref, back_ref, *refs):
@@ -188,7 +229,35 @@
     schur_ref[:, 0] = update_ref[:, 0, :, size:] + back_ref[rows, :, size:]
 
 
-def local(front_pivot, front_update, child_blocks, child_map):
+def last_kernel(size, count, row_ref, update_ref, *refs):
+    back_refs, seen_ref = refs[:count], refs[count]
+    lhat_ref, schur_ref, total_ref = refs[-3:]
+    step = pl.program_id(0)
+    update_rows, order = back_refs[0].shape
+    shape = (8, order - size)
+    first = lax.broadcasted_iota(jnp.int32, shape, 0)
+    second = lax.broadcasted_iota(jnp.int32, shape, 1)
+    at = row_ref[0] * update_rows
+
+    @pl.when(step == 0)
+    def _():
+        total_ref[...] = seen_ref[...]
+
+    for which in range(count):
+
+        @pl.when(step == which)
+        def _(which=which):
+            back = back_refs[which]
+            lhat_ref[0] = back[:, :size]
+            schur_ref[0] = update_ref[0, :, size:] + back[:, size:]
+            head = back[:8, size:]
+            marked = (first == 1) & (second == at)
+            twin = jnp.sum(jnp.where((first == 0) & (second == at + 1), head, 0.0))
+            total_ref[...] += jnp.sum(jnp.where(marked, head, 0.0))
+            schur_ref[0, :8, :] = update_ref[0, :8, size:] + jnp.where(marked, twin, head)
+
+
+def local_body(front_pivot, front_update, child_blocks, child_map):
     f32 = jnp.float32
     n = lax.axis_size("row")
     half = n // 2
@@ -205,6 +274,8 @@
     group = n // 2
     vmem = pl.BlockSpec(memory_space=pltpu.VMEM)
     whole = pl.BlockSpec(memory_space=pl.ANY)
+    updates = front_update.reshape(n, per, update_rows, order)
+    flat = jax.ShapeDtypeStruct
 
     def pack(turn):
         return pl.pallas_call(
@@ -219,48 +290,73 @@
                 ],
                 out_specs=pl.BlockSpec((group, rows, LANES), lambda g, r: (g, 0, 0)),
             ),
-            out_shape=jax.ShapeDtypeStruct((n, rows, LANES), f32),
+            out_shape=flat((n, rows, LANES), f32),
             name="pack",
         )(
             row_number,
             child_blocks.reshape(n, per, 2, held, width),
-            front_update.reshape(n, per, update_rows, order),
+            updates,
             front_pivot.reshape(n, per, pivot_rows, size),
         )
 
     def inner(turn):
-        return pl.pallas_call(
-            functools.partial(inner_kernel, (n, per, turn, span)),
-            in_specs=[pl.BlockSpec(memory_space=pltpu.SMEM), whole],
-            out_specs=[whole] * half,
-            out_shape=[jax.ShapeDtypeStruct((2, held, span), f32)] * half,
-            scratch_shapes=[pltpu.SemaphoreType.DMA((half,))],
+        def spec(flip):
+            return pl.BlockSpec(
+                (1, 2, held, span), lambda g, r: ((r[0] ^ flip) * per + turn, 0, 0, 1 - r[0] // half)
+            )
+
+        return pl.pallas_call(
+            inner_kernel,
+            grid_spec=pltpu.PrefetchScalarGridSpec(
+                num_scalar_prefetch=1,
+                grid=(1,),
+                in_specs=[spec(flip) for flip in range(half)],
+                out_specs=[vmem] * half,
+            ),
+            out_shape=[flat((2, held, span), f32)] * half,
             name="inner",
-        )(row_number, child_blocks)
-
-    def whole_front(arrived, inners, turn):
-        return pl.pallas_call(
-            functools.partial(front_kernel, dims + (update_rows, pivot_rows)),
+        )(row_number, *[child_blocks] * half)
+
+    def from_arrived(kernel, arrived, inners, turn, outs, scratch):
+        return pl.pallas_call(
+            functools.partial(kernel, dims + (update_rows, pivot_rows)),
             grid_spec=pltpu.PrefetchScalarGridSpec(
                 num_scalar_prefetch=1,
                 grid=(1,),
                 in_specs=[pl.BlockSpec((1, 2, width), lambda g, r: (r[0] * per + turn, 0, 0))]
                 + [vmem] * (half + 1),
-                out_specs=(vmem, vmem),
+                out_specs=(vmem,) * len(outs),
                 scratch_shapes=[
                     pltpu.VMEM((order, 2 * width), jnp.bfloat16),
                     pltpu.VMEM((4 * width, order), jnp.bfloat16),
                     pltpu.VMEM((order, order), f32),
                     pltpu.VMEM((size, 2 * size), f32),
-                    pltpu.VMEM((order - size, size), f32),
-                ],
-            ),
-            out_shape=(
-                jax.ShapeDtypeStruct((order - size, order), f32),
-                jax.ShapeDtypeStruct((1, size), f32),
-            ),
+                ]
+                + scratch,
+            ),
+            out_shape=tuple(flat(shape, f32) for shape in outs),
             name="front",
         )(row_number, child_map, arrived, *inners)
+
+    def whole_front(arrived, inners, turn):
+        outs = [(order - size, order), (1, size)]
+        scratch = [pltpu.VMEM((order - size, size), f32)]
+        return from_arrived(front_kernel, arrived, inners, turn, outs, scratch)
+
+    def factored(arrived, inners, turn):
+        outs = [(order - size, order - size), (order - size, size), (size, size), (1, size)]
+        return from_arrived(factor_kernel, arrived, inners, turn, outs, [])
+
+    def schur_rows(count, parts):
+        smem = pl.BlockSpec(memory_space=pltpu.SMEM)
+        return pl.pallas_call(
+            schur_kernel,
+            in_specs=[smem, smem] + [vmem] * 4,
+            out_specs=[vmem] * n,
+            out_shape=[flat((update_rows, order), f32)] * n,
+            scratch_shapes=[pltpu.VMEM((order - size, order), f32), pltpu.VMEM((order - size, size), f32)],
+            name="schur",
+        )(row_number, count.reshape(1), *parts)
 
     def finish(back, turn, before):
         aliases = {2: 0, 3: 1} if before else {}
@@ -275,42 +371,73 @@
                 pl.BlockSpec((group, 1, update_rows, order - size), place),
             ),
             out_shape=(
-                jax.ShapeDtypeStruct((n, per, update_rows, size), f32),
-                jax.ShapeDtypeStruct((n, per, update_rows, order - size), f32),
+                flat((n, per, update_rows, size), f32),
+                flat((n, per, update_rows, order - size), f32),
             ),
             input_output_aliases=aliases,
             name="finish",
-        )(front_update.reshape(n, per, update_rows, order), back, *before)
+        )(updates, back, *before)
+
+    def last(backs, flips, turn, before, seen):
+        count = len(backs)
+        place = lambda g, r: ((r[0] ^ (flips[0] + g)) * per + turn, 0, 0)
+        before = [part.reshape(fronts, update_rows, -1) for part in before]
+        aliases = {3 + count: 0, 4 + count: 1} if before else {}
+        return pl.pallas_call(
+            functools.partial(last_kernel, size, count),
+            grid_spec=pltpu.PrefetchScalarGridSpec(
+                num_scalar_prefetch=1,
+                grid=(count,),
+                in_specs=[pl.BlockSpec((1, update_rows, order), place)]
+                + [vmem] * (count + 1)
+                + [whole] * len(before),
+                out_specs=(
+                    pl.BlockSpec((1, update_rows, size), place),
+                    pl.BlockSpec((1, update_rows, order - size), place),
+                    pl.BlockSpec((1, size), lambda g, r: (0, 0)),
+                ),
+            ),
+            out_shape=(
+                flat((fronts, update_rows, size), f32),
+                flat((fronts, update_rows, order - size), f32),
+                flat((1, size), f32),
+            ),
+            input_output_aliases=aliases,
+            name="last",
+        )(row_number, front_update, *backs, seen, *before)
 
     exchange = functools.partial(lax.all_to_all, axis_name="row", split_axis=0, concat_axis=0, tiled=True)
 
-    def near(parts):
-        return [parts[0]] + [
-            lax.ppermute(parts[flip], "row", [(i, i ^ flip) for i in range(n)]) for flip in range(1, half)
-        ]
-
-    packed = [pack(turn) for turn in range(per)]
-    inners = [near(inner(turn)) for turn in range(per)]
-    arrived = [exchange(packed[turn]) for turn in range(per)]
+    def send(part, flip):
+        return lax.ppermute(part, "row", [(i, i ^ flip) for i in range(n)])
+
+    arrived, inners = [], []
+    for turn in range(per):
+        packed = pack(turn)
+        arrived.append(exchange(packed))
+        parts = inner(turn)
+        inners.append([parts[0]] + [send(parts[flip], flip) for flip in range(1, half)])
     total = jnp.zeros((), f32)
     backs = []
-    for turn in range(per):
+    for turn in range(per - 1):
         rows_out, pivots = whole_front(arrived[turn], inners[turn], turn)
         total = total + jnp.sum(jnp.where(pivots < 0.0, 1.0, 0.0))
-        if turn == per - 1:
-            total = lax.psum(total, ("row", "col"))
-            rows_out, total = lax.optimization_barrier((rows_out, total))
         backs.append(exchange(rows_out.reshape(n, update_rows, order)))
+    turn = per - 1
+    parts = factored(arrived[turn], inners[turn], turn)
+    total = lax.psum(total + jnp.sum(jnp.where(parts[3] < 0.0, 1.0, 0.0)), "col")
+    homes = schur_rows(total, parts)
+    homes = [homes[0]] + [send(homes[flip], flip) for flip in range(1, n)]
     done = ()
-    for turn in range(per):
+    for turn in range(per - 1):
         done = finish(backs[turn], turn, done)
-    lhat, schur = done
-    negative_share = total / (fronts * lax.axis_size("col") * size)
-    return (
-        lhat.reshape(fronts, update_rows, size),
-        schur.reshape(fronts, update_rows, order - size),
-        negative_share,
-    )
+    seen = jnp.zeros((1, size), f32)
+    for begin in (0, half):
+        flips = range(begin, begin + half)
+        lhat, schur, seen = last([homes[flip] for flip in flips], flips, per - 1, done, seen)
+        done = (lhat, schur)
+    negative_share = seen[0, 0] / (fronts * lax.axis_size("col") * size)
+    return (lhat, schur, negative_share)
 
 
 def solution(mesh):
@@ -321,4 +448,4 @@
         P("col", None, None),
     )
     out_specs = (P("col", "row", None), P("col", "row", None), P())
-    return jax.shard_map(local, mesh=mesh, in_specs=in_specs, out_specs=out_specs, check_vma=False)
+    return jax.shard_map(local_body, mesh=mesh, in_specs=in_specs, out_specs=out_specs, check_vma=False)

time: 267 us -> 225 us (0.84)
  the two profiles are of different devices: /device:TPU:0 before, /device:TPU:14 now
where the time goes in v3:
time: 225 us
  waiting for transfers between devices  98.8 us (44%)
  Pallas kernels  72.2 us (32%)
  starting transfers between devices  37 us (16%)
  blocking collectives  7.03 us (3%)
  local copies, waits for them, and re-layouts  3.85 us (2%)
  between operations  3.68 us (2%)
    ppermute x13, waiting for transfers between devices, send(): return lax.ppermute(part, 'row', [(i, i ^ flip) for i in range(n)])  78.8 us
    pallas_call x2, Pallas kernels, from_arrived(): pl.pallas_call(functools.partial(kernel, dims + (update_rows, pivot_rows)...  44.7 us
    all_to_all x2, waiting for transfers between devices, local_body(): arrived.append(exchange(packed))  19.9 us
    ppermute x13, starting transfers between devices, send(): return lax.ppermute(part, 'row', [(i, i ^ flip) for i in range(n)])  18 us
    all_to_all x2, starting transfers between devices, local_body(): arrived.append(exchange(packed))  13.1 us
    pallas_call x2, Pallas kernels, last(): pl.pallas_call(functools.partial(last_kernel, size, count), grid_spec=plt...  8.11 us
    psum x1, blocking collectives, local_body(): lax.psum(total + jnp.sum(jnp.where(parts[3] < 0.0, 1.0, 0.0)), 'col')  7.03 us
    pallas_call x1, Pallas kernels, schur_rows(): pl.pallas_call(schur_kernel, in_specs=[smem, smem] + [vmem] * 4, out_spec...  6.13 us
  transfers between devices with their start and end apart: 16, of which 12 were waited for; matrix products, arithmetic and copies ran while one was open for 1% of the time, Pallas kernels for 29%

profile of v3, /device:TPU:14, one launch (start us, length us, event | category | flops | bytes accessed | tf_op | source)
XLA Modules:
  0.0 224.5 jit_solution(15877238095602739057)
XLA Ops:
  0.6 2.5 %pack.2 = f32[8,256,128]{2,1,0:T(8,128)} custom-call(s32[1]{0:T(128)} %bitcast.row_ref.refs_0_, f32[8,2,2,64,512]{4,3,2,1,0:T(8,128)} %bitcast.10, f32[8,2,80,768]{3,2,1,0:T(8,128)} %bitcast.12, f32[8,2,16,128]{3,2,1,0:T(8,128)} %bitcast.18), custom_call_target="tpu_custom_call" | custom-call | tf_op jit(solution)/shard_map/pack/pallas_call | solution.py:281
  3.2 6.2 %all-to-all-start = ((f32[8,256,128]{2,1,0:T(8,128)}), f32[8,256,128]{2,1,0:T(8,128)S(1)}, u32[]{:S(2)}, u32[]{:S(2)}) async-start(f32[8,256,128]{2,1,0:T(8,128)} %pack.2), calls=%async_computation | async-start | bytes 2097152 | tf_op jit(solution)/shard_map/all_to_all | solution.py:417
  9.4 2.5 %pack.3 = f32[8,256,128]{2,1,0:T(8,128)} custom-call(s32[1]{0:T(128)} %bitcast.row_ref.refs_0_, f32[8,2,2,64,512]{4,3,2,1,0:T(8,128)} %bitcast.11, f32[8,2,80,768]{3,2,1,0:T(8,128)} %bitcast.13, f32[8,2,16,128]{3,2,1,0:T(8,128)} %bitcast.19), custom_call_target="tpu_custom_call" | custom-call | tf_op jit(solution)/shard_map/pack/pallas_call | solution.py:281
  11.9 19.9 %all-to-all-done.in_ref = f32[8,256,128]{2,1,0:T(8,128)S(1)} async-done(((f32[8,256,128]{2,1,0:T(8,128)}), f32[8,256,128]{2,1,0:T(8,128)S(1)}, u32[]{:S(2)}, u32[]{:S(2)}) %all-to-all-start) | async-done | bytes 1048608 | tf_op jit(solution)/shard_map/all_to_all | solution.py:417
  31.9 6.9 %all-to-all-start.1 = ((f32[8,256,128]{2,1,0:T(8,128)}), f32[8,256,128]{2,1,0:T(8,128)S(1)}, u32[]{:S(2)}, u32[]{:S(2)}) async-start(f32[8,256,128]{2,1,0:T(8,128)} %pack.3), calls=%async_computation.1 | async-start | bytes 2097152 | tf_op jit(solution)/shard_map/all_to_all | solution.py:417
  41.3 2.9 %collective-permute-start.2 = (f32[2,64,256]{2,1,0:T(8,128)}, f32[2,64,256]{2,1,0:T(8,128)S(1)}, u32[]{:S(2)}, u32[]{:S(2)}) collective-permute-start(f32[2,64,256]{2,1,0:T(8,128)} %get-tuple-element.36), channel_id=1, source_target_pairs={{0,12},{4,8},{8,4},{12,0},{16,28},{20,24},{24,20},{28,16},{1,13},{... | collective-permute-start | bytes 393224 | tf_op jit(solution)/shard_map/ppermute | solution.py:412
  44.1 6.9 %collective-permute-done.refs_1_ = f32[2,64,256]{2,1,0:T(8,128)S(1)} collective-permute-done((f32[2,64,256]{2,1,0:T(8,128)}, f32[2,64,256]{2,1,0:T(8,128)S(1)}, u32[]{:S(2)}, u32[]{:S(2)}) %collective-permute-start) | collective-permute-done | bytes 131104 | tf_op jit(solution)/shard_map/ppermute | solution.py:412
  51.1 9.7 %collective-permute-done.1.refs_2_ = f32[2,64,256]{2,1,0:T(8,128)S(1)} collective-permute-done((f32[2,64,256]{2,1,0:T(8,128)}, f32[2,64,256]{2,1,0:T(8,128)S(1)}, u32[]{:S(2)}, u32[]{:S(2)}) %collective-permute-start.1) | collective-permute-done | bytes 131104 | tf_op jit(solution)/shard_map/ppermute | solution.py:412
  63.2 23.5 %front.2 = (f32[640,768]{1,0:T(8,128)}, f32[1,128]{1,0:T(1,128)}) custom-call(s32[1]{0:T(128)} %bitcast.row_ref.refs_0_, s32[16,2,512]{2,1,0:T(2,128)} %map_ref.3, f32[8,256,128]{2,1,0:T(8,128)} %copy-done.2, f32[2,64,256]{2,1,0:T(8,128)} %get-tuple-element.33.refs_0_, f32[2,64,256]{2,1,0:T(8,128)} %copy-done.10, f32[2,64,256]{2,1,0:T(8,128)} %copy-done.12, ...), custom_call_target="tpu_custom_call" | custom-call | tf_op jit(solution)/shard_map/front/pallas_call | solution.py:321
  86.7 5.9 %all-to-all-start.2 = ((f32[8,80,768]{2,1,0:T(8,128)}), f32[8,80,768]{2,1,0:T(8,128)S(1)}, u32[]{:S(2)}, u32[]{:S(2)}) async-start(f32[8,80,768]{2,1,0:T(8,128)} %bitcast.17), calls=%async_computation.2 | async-start | bytes 3932160 | tf_op jit(solution)/shard_map/all_to_all | solution.py:425
  95.1 2.9 %collective-permute-start.5 = (f32[2,64,256]{2,1,0:T(8,128)}, f32[2,64,256]{2,1,0:T(8,128)S(1)}, u32[]{:S(2)}, u32[]{:S(2)}) collective-permute-start(f32[2,64,256]{2,1,0:T(8,128)} %get-tuple-element.41), channel_id=1, source_target_pairs={{0,12},{4,8},{8,4},{12,0},{16,28},{20,24},{24,20},{28,16},{1,13},{... | collective-permute-start | bytes 393224 | tf_op jit(solution)/shard_map/ppermute | solution.py:412
  98.0 13.2 %collective-permute-done.3.refs_1_ = f32[2,64,256]{2,1,0:T(8,128)S(1)} collective-permute-done((f32[2,64,256]{2,1,0:T(8,128)}, f32[2,64,256]{2,1,0:T(8,128)S(1)}, u32[]{:S(2)}, u32[]{:S(2)}) %collective-permute-start.3) | collective-permute-done | bytes 131104 | tf_op jit(solution)/shard_map/ppermute | solution.py:412
  111.2 17.2 %collective-permute-done.4.refs_2_ = f32[2,64,256]{2,1,0:T(8,128)S(1)} collective-permute-done((f32[2,64,256]{2,1,0:T(8,128)}, f32[2,64,256]{2,1,0:T(8,128)S(1)}, u32[]{:S(2)}, u32[]{:S(2)}) %collective-permute-start.4) | collective-permute-done | bytes 131104 | tf_op jit(solution)/shard_map/ppermute | solution.py:412
  130.3 21.2 %front.3 = (f32[640,640]{1,0:T(8,128)}, f32[640,128]{1,0:T(8,128)}, f32[128,128]{1,0:T(8,128)}, f32[1,128]{1,0:T(1,128)}) custom-call(s32[1]{0:T(128)} %bitcast.row_ref.refs_0_, s32[16,2,512]{2,1,0:T(2,128)} %map_ref.3, f32[8,256,128]{2,1,0:T(8,128)} %copy-done.1, f32[2,64,256]{2,1,0:T(8,128)} %get-tuple-element.38.refs_0_, f32[2,64,256]{2,1,0:T(8,128)} %copy-done.9, ...), custom_call_target="tpu_custom_call" | custom-call | tf_op jit(solution)/shard_map/front/pallas_call | solution.py:321
  154.8 7.0 %psum.7.count_ref = f32[1]{0:T(128)} all-reduce(f32[1]{0:T(128)} %bitcast.4), channel_id=1, replica_groups=mesh['row'=8,'col'=4] {'col'}, use_global_device_ids=true, to_apply=%region_2.3 | all-reduce | flops 1 | bytes 8 | tf_op jit(solution)/shard_map/psum | solution.py:428
  161.8 6.1 %schur.1 = (f32[80,768]{1,0:T(8,128)}, f32[80,768]{1,0:T(8,128)}, f32[80,768]{1,0:T(8,128)}, f32[80,768]{1,0:T(8,128)}, f32[80,768]{1,0:T(8,128)}, /*index=5*/f3...) custom-call(s32[1]{0:T(128)} %bitcast.row_ref.refs_0_, f32[1]{0:T(128)} %psum.7.count_ref, ...), custom_call_target="tpu_custom_call" | custom-call | tf_op jit(solution)/shard_map/schur/pallas_call | solution.py:352
  167.9 3.0 %collective-permute-start.10 = (f32[80,768]{1,0:T(8,128)}, f32[80,768]{1,0:T(8,128)S(1)}, u32[]{:S(2)}, u32[]{:S(2)}) collective-permute-start(f32[80,768]{1,0:T(8,128)} %get-tuple-element.51), channel_id=1, source_target_pairs={{0,4},{4,0},{8,12},{12,8},{16,20},{20,16},{24,28},{28,24},{1,5},{5... | collective-permute-start | bytes 737288 | tf_op jit(solution)/shard_map/ppermute | solution.py:412
  179.2 8.2 %collective-permute-done.11.refs_2_ = f32[80,768]{1,0:T(8,128)S(1)} collective-permute-done((f32[80,768]{1,0:T(8,128)}, f32[80,768]{1,0:T(8,128)S(1)}, u32[]{:S(2)}, u32[]{:S(2)}) %collective-permute-start.11) | collective-permute-done | bytes 245792 | tf_op jit(solution)/shard_map/ppermute | solution.py:412
  188.7 4.4 %finish.1 = (f32[8,2,80,128]{3,2,1,0:T(8,128)}, f32[8,2,80,640]{3,2,1,0:T(8,128)}) custom-call(f32[8,2,80,768]{3,2,1,0:T(8,128)} %bitcast.14, f32[8,80,768]{2,1,0:T(8,128)} %copy-done), custom_call_target="tpu_custom_call" | custom-call | tf_op jit(solution)/shard_map/finish/pallas_call | solution.py:365
  193.6 4.1 %last.2 = (f32[16,80,128]{2,1,0:T(8,128)}, f32[16,80,640]{2,1,0:T(8,128)}, f32[1,128]{1,0:T(1,128)}) custom-call(s32[1]{0:T(128)} %bitcast.row_ref.refs_0_, f32[16,80,768]{2,1,0:T(8,128)} %update_ref.3, f32[80,768]{1,0:T(8,128)} %get-tuple-element.50.refs_0_, f32[80,768]{1,0:T(8,128)} %copy-done.6, ...), custom_call_target="tpu_custom_call", output_to_operand_aliasing={{0}: (7, {}), {1}: (8, {})} | custom-call | tf_op jit(solution)/shard_map/last/pallas_call | solution.py:386
  197.7 9.8 %collective-permute-done.7.refs_1_ = f32[80,768]{1,0:T(8,128)S(1)} collective-permute-done((f32[80,768]{1,0:T(8,128)}, f32[80,768]{1,0:T(8,128)S(1)}, u32[]{:S(2)}, u32[]{:S(2)}) %collective-permute-start.7) | collective-permute-done | bytes 245792 | tf_op jit(solution)/shard_map/ppermute | solution.py:412
  207.5 5.6 %collective-permute-done.8.refs_2_ = f32[80,768]{1,0:T(8,128)S(1)} collective-permute-done((f32[80,768]{1,0:T(8,128)}, f32[80,768]{1,0:T(8,128)S(1)}, u32[]{:S(2)}, u32[]{:S(2)}) %collective-permute-start.8) | collective-permute-done | bytes 245792 | tf_op jit(solution)/shard_map/ppermute | solution.py:412
  213.2 4.9 %collective-permute-done.9.refs_3_ = f32[80,768]{1,0:T(8,128)S(1)} collective-permute-done((f32[80,768]{1,0:T(8,128)}, f32[80,768]{1,0:T(8,128)S(1)}, u32[]{:S(2)}, u32[]{:S(2)}) %collective-permute-start.9) | collective-permute-done | bytes 245792 | tf_op jit(solution)/shard_map/ppermute | solution.py:412
  218.8 4.0 %last.3 = (f32[16,80,128]{2,1,0:T(8,128)}, f32[16,80,640]{2,1,0:T(8,128)}, f32[1,128]{1,0:T(1,128)}) custom-call(s32[1]{0:T(128)} %bitcast.row_ref.refs_0_, f32[16,80,768]{2,1,0:T(8,128)} %update_ref.3, f32[80,768]{1,0:T(8,128)} %copy-done.3, f32[80,768]{1,0:T(8,128)} %copy-done.4, ...), custom_call_target="tpu_custom_call", output_to_operand_aliasing={{0}: (7, {}), {1}: (8, {})} | custom-call | tf_op jit(solution)/shard_map/last/pallas_call | solution.py:386
  (54 shorter events, 22.1 us)
Async XLA Ops:
  3.2 28.7 %all-to-all-start = ((f32[8,256,128]{2,1,0:T(8,128)}), f32[8,256,128]{2,1,0:T(8,128)S(1)}, u32[]{:S(2)}, u32[]{:S(2)}) async-start(f32[8,256,128]{2,1,0:T(8,128)} %pack.2), calls=%async_computation | async-start | bytes 2097152 | tf_op jit(solution)/shard_map/all_to_all | solution.py:417
  31.9 8.8 %copy-start.2 = (f32[8,256,128]{2,1,0:T(8,128)}, f32[8,256,128]{2,1,0:T(8,128)S(1)}, u32[]{:S(2)}) copy-start(f32[8,256,128]{2,1,0:T(8,128)S(1)} %all-to-all-done.in_ref) | copy-start | bytes 3145732
  31.9 54.8 %all-to-all-start.1 = ((f32[8,256,128]{2,1,0:T(8,128)}), f32[8,256,128]{2,1,0:T(8,128)S(1)}, u32[]{:S(2)}, u32[]{:S(2)}) async-start(f32[8,256,128]{2,1,0:T(8,128)} %pack.3), calls=%async_computation.1 | async-start | bytes 2097152 | tf_op jit(solution)/shard_map/all_to_all | solution.py:417
  40.7 10.4 %collective-permute-start = (f32[2,64,256]{2,1,0:T(8,128)}, f32[2,64,256]{2,1,0:T(8,128)S(1)}, u32[]{:S(2)}, u32[]{:S(2)}) collective-permute-start(f32[2,64,256]{2,1,0:T(8,128)} %get-tuple-element.34), channel_id=1, source_target_pairs={{0,4},{4,0},{8,12},{12,8},{16,20},{20,16},{24,28},{28,24},{1,5},{5... | collective-permute-start | bytes 393224 | tf_op jit(solution)/shard_map/ppermute | solution.py:412
  41.2 19.6 %collective-permute-start.1 = (f32[2,64,256]{2,1,0:T(8,128)}, f32[2,64,256]{2,1,0:T(8,128)S(1)}, u32[]{:S(2)}, u32[]{:S(2)}) collective-permute-start(f32[2,64,256]{2,1,0:T(8,128)} %get-tuple-element.35), channel_id=1, source_target_pairs={{0,8},{4,12},{8,0},{12,4},{16,24},{20,28},{24,16},{28,20},{1,9},{5... | collective-permute-start | bytes 393224 | tf_op jit(solution)/shard_map/ppermute | solution.py:412
  41.3 21.2 %collective-permute-start.2 = (f32[2,64,256]{2,1,0:T(8,128)}, f32[2,64,256]{2,1,0:T(8,128)S(1)}, u32[]{:S(2)}, u32[]{:S(2)}) collective-permute-start(f32[2,64,256]{2,1,0:T(8,128)} %get-tuple-element.36), channel_id=1, source_target_pairs={{0,12},{4,8},{8,4},{12,0},{16,28},{20,24},{24,20},{28,16},{1,13},{... | collective-permute-start | bytes 393224 | tf_op jit(solution)/shard_map/ppermute | solution.py:412
  51.1 11.5 %copy-start.10 = (f32[2,64,256]{2,1,0:T(8,128)}, f32[2,64,256]{2,1,0:T(8,128)S(1)}, u32[]{:S(2)}) copy-start(f32[2,64,256]{2,1,0:T(8,128)S(1)} %collective-permute-done.refs_1_) | copy-start | bytes 393220
  86.7 7.8 %copy-start.1 = (f32[8,256,128]{2,1,0:T(8,128)}, f32[8,256,128]{2,1,0:T(8,128)S(1)}, u32[]{:S(2)}) copy-start(f32[8,256,128]{2,1,0:T(8,128)S(1)} %all-to-all-done.1.in_ref) | copy-start | bytes 3145732
  86.7 100.7 %all-to-all-start.2 = ((f32[8,80,768]{2,1,0:T(8,128)}), f32[8,80,768]{2,1,0:T(8,128)S(1)}, u32[]{:S(2)}, u32[]{:S(2)}) async-start(f32[8,80,768]{2,1,0:T(8,128)} %bitcast.17), calls=%async_computation.2 | async-start | bytes 3932160 | tf_op jit(solution)/shard_map/all_to_all | solution.py:425
  92.6 60.2 %copy-start.15 = (f32[1,128]{1,0:T(1,128)S(1)}, f32[1,128]{1,0:T(1,128)}, u32[]{:S(2)}) copy-start(f32[1,128]{1,0:T(1,128)} %get-tuple-element.37) | copy-start | bytes 1540
  94.5 16.7 %collective-permute-start.3 = (f32[2,64,256]{2,1,0:T(8,128)}, f32[2,64,256]{2,1,0:T(8,128)S(1)}, u32[]{:S(2)}, u32[]{:S(2)}) collective-permute-start(f32[2,64,256]{2,1,0:T(8,128)} %get-tuple-element.39), channel_id=1, source_target_pairs={{0,4},{4,0},{8,12},{12,8},{16,20},{20,16},{24,28},{28,24},{1,5},{5... | collective-permute-start | bytes 393224 | tf_op jit(solution)/shard_map/ppermute | solution.py:412
  95.0 33.4 %collective-permute-start.4 = (f32[2,64,256]{2,1,0:T(8,128)}, f32[2,64,256]{2,1,0:T(8,128)S(1)}, u32[]{:S(2)}, u32[]{:S(2)}) collective-permute-start(f32[2,64,256]{2,1,0:T(8,128)} %get-tuple-element.40), channel_id=1, source_target_pairs={{0,8},{4,12},{8,0},{12,4},{16,24},{20,28},{24,16},{28,20},{1,9},{5... | collective-permute-start | bytes 393224 | tf_op jit(solution)/shard_map/ppermute | solution.py:412
  95.1 34.6 %collective-permute-start.5 = (f32[2,64,256]{2,1,0:T(8,128)}, f32[2,64,256]{2,1,0:T(8,128)S(1)}, u32[]{:S(2)}, u32[]{:S(2)}) collective-permute-start(f32[2,64,256]{2,1,0:T(8,128)} %get-tuple-element.41), channel_id=1, source_target_pairs={{0,12},{4,8},{8,4},{12,0},{16,28},{20,24},{24,20},{28,16},{1,13},{... | collective-permute-start | bytes 393224 | tf_op jit(solution)/shard_map/ppermute | solution.py:412
  111.2 18.5 %copy-start.9 = (f32[2,64,256]{2,1,0:T(8,128)}, f32[2,64,256]{2,1,0:T(8,128)S(1)}, u32[]{:S(2)}) copy-start(f32[2,64,256]{2,1,0:T(8,128)S(1)} %collective-permute-done.3.refs_1_) | copy-start | bytes 393220
  167.9 9.1 %collective-permute-start.10 = (f32[80,768]{1,0:T(8,128)}, f32[80,768]{1,0:T(8,128)S(1)}, u32[]{:S(2)}, u32[]{:S(2)}) collective-permute-start(f32[80,768]{1,0:T(8,128)} %get-tuple-element.51), channel_id=1, source_target_pairs={{0,4},{4,0},{8,12},{12,8},{16,20},{20,16},{24,28},{28,24},{1,5},{5... | collective-permute-start | bytes 737288 | tf_op jit(solution)/shard_map/ppermute | solution.py:412
  170.9 16.4 %collective-permute-start.11 = (f32[80,768]{1,0:T(8,128)}, f32[80,768]{1,0:T(8,128)S(1)}, u32[]{:S(2)}, u32[]{:S(2)}) collective-permute-start(f32[80,768]{1,0:T(8,128)} %get-tuple-element.52), channel_id=1, source_target_pairs={{0,8},{4,12},{8,0},{12,4},{16,24},{20,28},{24,16},{28,20},{1,9},{5... | collective-permute-start | bytes 737288 | tf_op jit(solution)/shard_map/ppermute | solution.py:412
  170.9 22.2 %collective-permute-start.12 = (f32[80,768]{1,0:T(8,128)}, f32[80,768]{1,0:T(8,128)}, u32[]{:S(2)}, u32[]{:S(2)}) collective-permute-start(f32[80,768]{1,0:T(8,128)} %get-tuple-element.53), channel_id=1, source_target_pairs={{0,12},{4,8},{8,4},{12,0},{16,28},{20,24},{24,20},{28,16},{1,13},{... | collective-permute-start | bytes 737288 | tf_op jit(solution)/shard_map/ppermute | solution.py:412
  172.4 25.3 %collective-permute-start.6 = (f32[80,768]{1,0:T(8,128)}, f32[80,768]{1,0:T(8,128)S(1)}, u32[]{:S(2)}, u32[]{:S(2)}) collective-permute-start(f32[80,768]{1,0:T(8,128)} %get-tuple-element.46), channel_id=1, source_target_pairs={{0,16},{4,20},{8,24},{12,28},{16,0},{20,4},{24,8},{28,12},{1,17},{... | collective-permute-start | bytes 737288 | tf_op jit(solution)/shard_map/ppermute | solution.py:412
  174.6 33.0 %collective-permute-start.7 = (f32[80,768]{1,0:T(8,128)}, f32[80,768]{1,0:T(8,128)S(1)}, u32[]{:S(2)}, u32[]{:S(2)}) collective-permute-start(f32[80,768]{1,0:T(8,128)} %get-tuple-element.47), channel_id=1, source_target_pairs={{0,20},{4,16},{8,28},{12,24},{16,4},{20,0},{24,12},{28,8},{1,21},{... | collective-permute-start | bytes 737288 | tf_op jit(solution)/shard_map/ppermute | solution.py:412
  177.0 16.6 %copy-start.6 = (f32[80,768]{1,0:T(8,128)}, f32[80,768]{1,0:T(8,128)S(1)}, u32[]{:S(2)}) copy-start(f32[80,768]{1,0:T(8,128)S(1)} %collective-permute-done.10.refs_1_) | copy-start | bytes 737284
  177.0 36.2 %collective-permute-start.8 = (f32[80,768]{1,0:T(8,128)}, f32[80,768]{1,0:T(8,128)S(1)}, u32[]{:S(2)}, u32[]{:S(2)}) collective-permute-start(f32[80,768]{1,0:T(8,128)} %get-tuple-element.48), channel_id=1, source_target_pairs={{0,24},{4,28},{8,16},{12,20},{16,8},{20,12},{24,0},{28,4},{1,25},{... | collective-permute-start | bytes 737288 | tf_op jit(solution)/shard_map/ppermute | solution.py:412
  187.4 30.7 %collective-permute-start.9 = (f32[80,768]{1,0:T(8,128)}, f32[80,768]{1,0:T(8,128)S(1)}, u32[]{:S(2)}, u32[]{:S(2)}) collective-permute-start(f32[80,768]{1,0:T(8,128)} %get-tuple-element.49), channel_id=1, source_target_pairs={{0,28},{4,24},{8,20},{12,16},{16,12},{20,8},{24,4},{28,0},{1,29},{... | collective-permute-start | bytes 737288 | tf_op jit(solution)/shard_map/ppermute | solution.py:412
  197.7 20.4 %copy-start.3 = (f32[80,768]{1,0:T(8,128)}, f32[80,768]{1,0:T(8,128)S(1)}, u32[]{:S(2)}) copy-start(f32[80,768]{1,0:T(8,128)S(1)} %collective-permute-done.6.refs_0_) | copy-start | bytes 737284
  207.5 10.5 %copy-start.4 = (f32[80,768]{1,0:T(8,128)}, f32[80,768]{1,0:T(8,128)S(1)}, u32[]{:S(2)}) copy-start(f32[80,768]{1,0:T(8,128)S(1)} %collective-permute-done.7.refs_1_) | copy-start | bytes 737284
  (8 other events, 17.5 us)

commit v4 on v3

--- a/solution.py
+++ b/solution.py
@@ -18,33 +18,51 @@
     return high, low
 
 
-def pack_kernel(dims, row_ref, child_ref, update_ref, pivot_ref, out_ref):
+def fill(dims, row, children, coupling, pivots, out_ref):
     n, held, extra_rows = dims
-    row = row_ref[0]
     half = n // 2
     span = half * held
     place = lax.rem(row, half)
     lane = lax.broadcasted_iota(jnp.int32, (held, LANES), 1)
     lane_extra = lax.broadcasted_iota(jnp.int32, (extra_rows, LANES), 1)
+    extras = []
+    at = 0
+    for child in range(2):
+        rolled = pltpu.roll(children[child], lax.rem(span - place * held, span), 1)
+        near = rolled[:, :LANES]
+        out_ref[at : at + held, :] = jnp.where(lane < held, 0.5 * near, near)
+        at += held
+        extras.append(rolled[:, LANES:])
+    extra = jnp.where(place < half // 2, extras[0], extras[1])
+    packed = extra[:extra_rows]
+    for piece in range(1, held // extra_rows):
+        rows = pltpu.roll(extra[piece * extra_rows : (piece + 1) * extra_rows], piece * held, 1)
+        packed = jnp.where(lane_extra // held == piece, rows, packed)
+    for part in (packed, coupling, pivots):
+        out_ref[at : at + part.shape[0], :] = part
+        at += part.shape[0]
+    return at
+
+
+def pack_kernel(dims, row_ref, child_ref, update_ref, pivot_ref, out_ref):
     for front in range(child_ref.shape[0]):
-        extras = []
-        at = 0
-        for child in range(2):
-            rolled = pltpu.roll(child_ref[front, 0, child], lax.rem(span - place * held, span), 1)
-            near = rolled[:, :LANES]
-            out_ref[front, at : at + held, :] = jnp.where(lane < held, 0.5 * near, near)
-            at += held
-            extras.append(rolled[:, LANES:])
-        extra = jnp.where(place < half // 2, extras[0], extras[1])
-        packed = extra[:extra_rows]
-        for piece in range(1, held // extra_rows):
-            rows = pltpu.roll(extra[piece * extra_rows : (piece + 1) * extra_rows], piece * held, 1)
-            packed = jnp.where(lane_extra // held == piece, rows, packed)
-        out_ref[front, at : at + extra_rows, :] = packed
-        at += extra_rows
-        out_ref[front, at : at + update_ref.shape[2], :] = update_ref[front, 0]
-        at += update_ref.shape[2]
-        out_ref[front, at : at + pivot_ref.shape[2], :] = pivot_ref[front, 0]
+        fill(
+            dims, row_ref[0], child_ref.at[front, 0], update_ref[front, 0], pivot_ref[front, 0], out_ref.at[front]
+        )
+
+
+def part_kernel(dims, count, row_ref, *refs):
+    inputs, outs = refs[:-count], refs[-count:]
+    groups = [inputs[at : at + count] for at in range(0, len(inputs), count)]
+    for which, out_ref in enumerate(outs):
+        children, coupling, pivots = (group[which] for group in groups[:3])
+        at = fill(dims, row_ref[0], children.at[0], coupling[0], pivots[0], out_ref)
+        for other in groups[3:]:
+            held = dims[1]
+            for child in range(2):
+                for plane in range(other[which].shape[-1] // LANES):
+                    out_ref[at : at + held, :] = other[which][0, child, :, plane * LANES : (plane + 1) * LANES]
+                    at += held
 
 
 def inner_kernel(*refs):
@@ -53,7 +71,7 @@
         out_ref[...] = in_ref[0]
 
 
-def assemble(dims, row, map_ref, in_ref, inner_refs, hot_ref, half_ref, sum_ref, aug_ref, coup_ref):
+def assemble(dims, row, map_ref, in_ref, inners, hot_ref, half_ref, sum_ref, aug_ref, coup_ref):
     n, held, extra_rows, update_rows, pivot_rows = dims
     half = n // 2
     width = map_ref.shape[-1]
@@ -109,7 +127,7 @@
             half_ref[2 * width + at : 2 * width + at + held, :] = moved[held:]
         other = hot(jnp.where(row // half == 0, indices[:, span:], indices[:, :span]))
         for flip in range(half):
-            moved = spread(inner_refs[flip][child], other)
+            moved = spread(inners(flip, child), other)
             at = pl.multiple_of(child * width + (row ^ flip) * held, held)
             half_ref[pl.ds(at, held), :] += moved[:held]
             half_ref[pl.ds(2 * width + at, held), :] += moved[held:]
@@ -180,10 +198,21 @@
         out_ref[rows, size:] = trailing_rows(start) - correction
 
 
-def front_kernel(dims, row_ref, map_ref, in_ref, *refs):
-    half = dims[0] // 2
-    out_ref, pivots_ref, hot_ref, half_ref, sum_ref, aug_ref, coup_ref = refs[half:]
-    assemble(dims, row_ref[0], map_ref, in_ref, refs[:half], hot_ref, half_ref, sum_ref, aug_ref, coup_ref)
+def front_kernel(dims, row_ref, map_ref, *refs):
+    n, held = dims[:2]
+    out_ref, pivots_ref, hot_ref, half_ref, sum_ref, aug_ref, coup_ref, in_ref = refs[n:]
+    rows = in_ref.shape[1]
+    for flip in range(n):
+        in_ref[row_ref[0] ^ flip] = refs[flip][:rows, :]
+
+    def inners(flip, child):
+        planes = (refs[flip].shape[0] - rows) // (2 * held)
+        start = rows + child * planes * held
+        return jnp.concatenate(
+            [refs[flip][start + plane * held : start + (plane + 1) * held, :] for plane in range(planes)], axis=1
+        )
+
+    assemble(dims, row_ref[0], map_ref, in_ref, inners, hot_ref, half_ref, sum_ref, aug_ref, coup_ref)
     size = aug_ref.shape[0]
     pivots = eliminate(aug_ref)
     pivots_ref[...] = pivots
@@ -193,7 +222,8 @@
 def factor_kernel(dims, row_ref, map_ref, in_ref, *refs):
     half = dims[0] // 2
     trail_ref, coup_ref, inverse_ref, pivots_ref, hot_ref, half_ref, sum_ref, aug_ref = refs[half:]
-    assemble(dims, row_ref[0], map_ref, in_ref, refs[:half], hot_ref, half_ref, sum_ref, aug_ref, coup_ref)
+    inners = lambda flip, child: refs[flip][child]
+    assemble(dims, row_ref[0], map_ref, in_ref, inners, hot_ref, half_ref, sum_ref, aug_ref, coup_ref)
     size = aug_ref.shape[0]
     pivots_ref[...] = eliminate(aug_ref)
     inverse_ref[...] = aug_ref[:, size:]
@@ -299,6 +329,34 @@
             front_pivot.reshape(n, per, pivot_rows, size),
         )
 
+    def parts_for(turn, flips):
+        near = flips[0] < half
+
+        def front(r, flip):
+            return (r[0] ^ flip) * per + turn
+
+        specs = [
+            pl.BlockSpec((1, 2, held, span), lambda g, r, f=f: (front(r, f), 0, 0, r[0] // half)) for f in flips
+        ]
+        specs += [pl.BlockSpec((1, update_rows, size), lambda g, r, f=f: (front(r, f), 0, 0)) for f in flips]
+        specs += [pl.BlockSpec((1, pivot_rows, size), lambda g, r, f=f: (front(r, f), 0, 0)) for f in flips]
+        if near:
+            specs += [
+                pl.BlockSpec((1, 2, held, span), lambda g, r, f=f: (front(r, f), 0, 0, 1 - r[0] // half))
+                for f in flips
+            ]
+        count = len(flips)
+        operands = [child_blocks] * count + [front_update] * count + [front_pivot] * count
+        operands += [child_blocks] * count if near else []
+        return pl.pallas_call(
+            functools.partial(part_kernel, dims, count),
+            grid_spec=pltpu.PrefetchScalarGridSpec(
+                num_scalar_prefetch=1, grid=(1,), in_specs=specs, out_specs=[vmem] * count
+            ),
+            out_shape=[flat((rows + (2 * held * span // LANES if near else 0), LANES), f32)] * count,
+            name="parts",
+        )(row_number, *operands)
+
     def inner(turn):
         def spec(flip):
             return pl.BlockSpec(
@@ -317,14 +375,14 @@
             name="inner",
         )(row_number, *[child_blocks] * half)
 
-    def from_arrived(kernel, arrived, inners, turn, outs, scratch):
+    def from_arrived(kernel, arrays, turn, outs, scratch):
         return pl.pallas_call(
             functools.partial(kernel, dims + (update_rows, pivot_rows)),
             grid_spec=pltpu.PrefetchScalarGridSpec(
                 num_scalar_prefetch=1,
                 grid=(1,),
                 in_specs=[pl.BlockSpec((1, 2, width), lambda g, r: (r[0] * per + turn, 0, 0))]
-                + [vmem] * (half + 1),
+                + [vmem] * len(arrays),
                 out_specs=(vmem,) * len(outs),
                 scratch_shapes=[
                     pltpu.VMEM((order, 2 * width), jnp.bfloat16),
@@ -336,16 +394,16 @@
             ),
             out_shape=tuple(flat(shape, f32) for shape in outs),
             name="front",
-        )(row_number, child_map, arrived, *inners)
-
-    def whole_front(arrived, inners, turn):
+        )(row_number, child_map, *arrays)
+
+    def whole_front(arrays, turn):
         outs = [(order - size, order), (1, size)]
-        scratch = [pltpu.VMEM((order - size, size), f32)]
-        return from_arrived(front_kernel, arrived, inners, turn, outs, scratch)
-
-    def factored(arrived, inners, turn):
+        scratch = [pltpu.VMEM((order - size, size), f32), pltpu.VMEM((n, rows, LANES), f32)]
+        return from_arrived(front_kernel, arrays, turn, outs, scratch)
+
+    def factored(arrays, turn):
         outs = [(order - size, order - size), (order - size, size), (size, size), (1, size)]
-        return from_arrived(factor_kernel, arrived, inners, turn, outs, [])
+        return from_arrived(factor_kernel, arrays, turn, outs, [])
 
     def schur_rows(count, parts):
         smem = pl.BlockSpec(memory_space=pltpu.SMEM)
@@ -411,20 +469,26 @@
     def send(part, flip):
         return lax.ppermute(part, "row", [(i, i ^ flip) for i in range(n)])
 
-    arrived, inners = [], []
-    for turn in range(per):
-        packed = pack(turn)
-        arrived.append(exchange(packed))
-        parts = inner(turn)
-        inners.append([parts[0]] + [send(parts[flip], flip) for flip in range(1, half)])
+    arrays = []
+    for turn in range(per - 1):
+        far = parts_for(turn, range(half, n))
+        far = [send(part, half + flip) for flip, part in enumerate(far)]
+        near = parts_for(turn, range(half))
+        near = [near[0]] + [send(near[flip], flip) for flip in range(1, half)]
+        arrays.append(near + far)
+    turn = per - 1
+    packed = pack(turn)
+    arrived = exchange(packed)
+    parts = inner(turn)
+    arrays.append([arrived, parts[0]] + [send(parts[flip], flip) for flip in range(1, half)])
     total = jnp.zeros((), f32)
     backs = []
     for turn in range(per - 1):
-        rows_out, pivots = whole_front(arrived[turn], inners[turn], turn)
+        rows_out, pivots = whole_front(arrays[turn], turn)
         total = total + jnp.sum(jnp.where(pivots < 0.0, 1.0, 0.0))
         backs.append(exchange(rows_out.reshape(n, update_rows, order)))
     turn = per - 1
-    parts = factored(arrived[turn], inners[turn], turn)
+    parts = factored(arrays[turn], turn)
     total = lax.psum(total + jnp.sum(jnp.where(parts[3] < 0.0, 1.0, 0.0)), "col")
     homes = schur_rows(total, parts)
     homes = [homes[0]] + [send(homes[flip], flip) for flip in range(1, n)]
@@ -432,8 +496,8 @@
     for turn in range(per - 1):
         done = finish(backs[turn], turn, done)
     seen = jnp.zeros((1, size), f32)
-    for begin in (0, half):
-        flips = range(begin, begin + half)
+    for begin, end in [(0, half)] + [(flip, flip + 1) for flip in range(half, n)]:
+        flips = range(begin, end)
         lhat, schur, seen = last([homes[flip] for flip in flips], flips, per - 1, done, seen)
         done = (lhat, schur)
     negative_share = seen[0, 0] / (fronts * lax.axis_size("col") * size)

time: 225 us -> 215 us (0.956)
  the two profiles are of different devices: /device:TPU:14 before, /device:TPU:0 now
where the time goes in v4:
time: 215 us; the launch traced here: 213 us
  waiting for transfers between devices  77.7 us (36%)
  Pallas kernels  76.2 us (35%)
  starting transfers between devices  40.3 us (19%)
  blocking collectives  6.81 us (3%)
  local copies, waits for them, and re-layouts  6.11 us (3%)
  between operations  3.67 us (2%)
    ppermute x17, waiting for transfers between devices, send(): return lax.ppermute(part, 'row', [(i, i ^ flip) for i in range(n)])  77.7 us
    pallas_call x2, Pallas kernels, from_arrived(): pl.pallas_call(functools.partial(kernel, dims + (update_rows, pivot_rows)...  44.7 us
    ppermute x17, starting transfers between devices, send(): return lax.ppermute(part, 'row', [(i, i ^ flip) for i in range(n)])  28.9 us
    pallas_call x5, Pallas kernels, last(): pl.pallas_call(functools.partial(last_kernel, size, count), grid_spec=plt...  11.5 us
    all_to_all x1, starting transfers between devices, local_body(): arrived = exchange(packed)  7.28 us
    psum x1, blocking collectives, local_body(): lax.psum(total + jnp.sum(jnp.where(parts[3] < 0.0, 1.0, 0.0)), 'col')  6.81 us
    pallas_call x1, Pallas kernels, schur_rows(): pl.pallas_call(schur_kernel, in_specs=[smem, smem] + [vmem] * 4, out_spec...  6.17 us
    unnamed x42, local copies, waits for them, and re-layouts  5.57 us
  transfers between devices with their start and end apart: 19, of which 9 were waited for; matrix products, arithmetic and copies ran while one was open for 1% of the time, Pallas kernels for 34%

profile of v4, /device:TPU:0, one launch (start us, length us, event | category | flops | bytes accessed | tf_op | source)
XLA Modules:
  0.0 212.6 jit_solution(5814384288877758876)
XLA Ops:
  0.6 2.6 %pack.1 = f32[8,256,128]{2,1,0:T(8,128)} custom-call(s32[1]{0:T(128)} %bitcast.row_ref.refs_0_, f32[8,2,2,64,512]{4,3,2,1,0:T(8,128)} %bitcast.10, f32[8,2,80,768]{3,2,1,0:T(8,128)} %bitcast.11, f32[8,2,16,128]{3,2,1,0:T(8,128)} %bitcast.15), custom_call_target="tpu_custom_call" | custom-call | tf_op jit(solution)/shard_map/pack/pallas_call | solution.py:311
  3.2 7.3 %all-to-all-start = ((f32[8,256,128]{2,1,0:T(8,128)}), f32[8,256,128]{2,1,0:T(8,128)S(1)}, u32[]{:S(2)}, u32[]{:S(2)}) async-start(f32[8,256,128]{2,1,0:T(8,128)} %pack.1), calls=%async_computation | async-start | bytes 2097152 | tf_op jit(solution)/shard_map/all_to_all | solution.py:481
  10.5 2.2 %parts.3 = (f32[256,128]{1,0:T(8,128)}, f32[256,128]{1,0:T(8,128)}, f32[256,128]{1,0:T(8,128)}, f32[256,128]{1,0:T(8,128)}) custom-call(s32[1]{0:T(128)} %bitcast.row_ref.refs_0_, f32[16,2,64,512]{3,2,1,0:T(8,128)} %refs_4_.5, f32[16,2,64,512]{3,2,1,0:T(8,128)} %refs_4_.5, f32[16,2,64,512]{3,2,1,0:T(8,128)} %refs_4_.5, f32[16,2,64,512]{3,2,1,0:T(8,128)} %refs_4_.5, ...), custom_call_target="tpu_custom_call" | custom-call | tf_op jit(solution)/shard_map/parts/pallas_call | solution.py:351
  12.7 2.9 %collective-permute-start.3 = (f32[256,128]{1,0:T(8,128)}, f32[256,128]{1,0:T(8,128)S(1)}, u32[]{:S(2)}, u32[]{:S(2)}) collective-permute-start(f32[256,128]{1,0:T(8,128)} %get-tuple-element.50), channel_id=1, source_target_pairs={{0,16},{4,20},{8,24},{12,28},{16,0},{20,4},{24,8},{28,12},{1,17},{... | collective-permute-start | bytes 393224 | tf_op jit(solution)/shard_map/ppermute | solution.py:470
  17.1 2.6 %parts.2 = (f32[512,128]{1,0:T(8,128)}, f32[512,128]{1,0:T(8,128)}, f32[512,128]{1,0:T(8,128)}, f32[512,128]{1,0:T(8,128)}) custom-call(s32[1]{0:T(128)} %bitcast.row_ref.refs_0_, f32[16,2,64,512]{3,2,1,0:T(8,128)} %refs_4_.5, f32[16,2,64,512]{3,2,1,0:T(8,128)} %refs_4_.5, f32[16,2,64,512]{3,2,1,0:T(8,128)} %refs_4_.5, f32[16,2,64,512]{3,2,1,0:T(8,128)} %refs_4_.5, ...), custom_call_target="tpu_custom_call" | custom-call | tf_op jit(solution)/shard_map/parts/pallas_call | solution.py:351
  23.2 22.8 %collective-permute-done.3.refs_4_ = f32[256,128]{1,0:T(8,128)S(1)} collective-permute-done((f32[256,128]{1,0:T(8,128)}, f32[256,128]{1,0:T(8,128)S(1)}, u32[]{:S(2)}, u32[]{:S(2)}) %collective-permute-start.3) | collective-permute-done | bytes 131104 | tf_op jit(solution)/shard_map/ppermute | solution.py:470
  46.1 3.5 %collective-permute-done.4.refs_5_ = f32[256,128]{1,0:T(8,128)S(1)} collective-permute-done((f32[256,128]{1,0:T(8,128)}, f32[256,128]{1,0:T(8,128)S(1)}, u32[]{:S(2)}, u32[]{:S(2)}) %collective-permute-start.4) | collective-permute-done | bytes 131104 | tf_op jit(solution)/shard_map/ppermute | solution.py:470
  50.4 3.8 %collective-permute-done.5.refs_6_ = f32[256,128]{1,0:T(8,128)S(1)} collective-permute-done((f32[256,128]{1,0:T(8,128)S(1)}, f32[256,128]{1,0:T(8,128)S(1)}, u32[]{:S(2)}, u32[]{:S(2)}) %collective-permute-start.5) | collective-permute-done | bytes 131104 | tf_op jit(solution)/shard_map/ppermute | solution.py:470
  54.2 3.2 %collective-permute-done.6.refs_7_ = f32[256,128]{1,0:T(8,128)S(1)} collective-permute-done((f32[256,128]{1,0:T(8,128)S(1)}, f32[256,128]{1,0:T(8,128)S(1)}, u32[]{:S(2)}, u32[]{:S(2)}) %collective-permute-start.6) | collective-permute-done | bytes 131104 | tf_op jit(solution)/shard_map/ppermute | solution.py:470
  58.3 23.5 %front.2 = (f32[640,768]{1,0:T(8,128)}, f32[1,128]{1,0:T(1,128)}) custom-call(s32[1]{0:T(128)} %bitcast.row_ref.refs_0_, s32[16,2,512]{2,1,0:T(2,128)} %map_ref.3, f32[512,128]{1,0:T(8,128)} %get-tuple-element.46.refs_0_, f32[512,128]{1,0:T(8,128)} %copy-done.2, f32[512,128]{1,0:T(8,128)} %copy-done.3, f32[512,128]{1,0:T(8,128)} %copy-done.4, ...), custom_call_target="tpu_custom_call" | custom-call | tf_op jit(solution)/shard_map/front/pallas_call | solution.py:379
  81.8 4.1 %all-to-all-start.1 = ((f32[8,80,768]{2,1,0:T(8,128)}), f32[8,80,768]{2,1,0:T(8,128)S(1)}, u32[]{:S(2)}, u32[]{:S(2)}) async-start(f32[8,80,768]{2,1,0:T(8,128)} %bitcast.16), calls=%async_computation.1 | async-start | bytes 3932160 | tf_op jit(solution)/shard_map/all_to_all | solution.py:489
  92.3 13.0 %collective-permute-done.7.refs_1_ = f32[2,64,256]{2,1,0:T(8,128)S(1)} collective-permute-done((f32[2,64,256]{2,1,0:T(8,128)}, f32[2,64,256]{2,1,0:T(8,128)S(1)}, u32[]{:S(2)}, u32[]{:S(2)}) %collective-permute-start.7) | collective-permute-done | bytes 131104 | tf_op jit(solution)/shard_map/ppermute | solution.py:470
  105.3 16.5 %collective-permute-done.8.refs_2_ = f32[2,64,256]{2,1,0:T(8,128)S(1)} collective-permute-done((f32[2,64,256]{2,1,0:T(8,128)}, f32[2,64,256]{2,1,0:T(8,128)S(1)}, u32[]{:S(2)}, u32[]{:S(2)}) %collective-permute-start.8) | collective-permute-done | bytes 131104 | tf_op jit(solution)/shard_map/ppermute | solution.py:470
  123.9 21.2 %front.3 = (f32[640,640]{1,0:T(8,128)}, f32[640,128]{1,0:T(8,128)}, f32[128,128]{1,0:T(8,128)}, f32[1,128]{1,0:T(1,128)}) custom-call(s32[1]{0:T(128)} %bitcast.row_ref.refs_0_, s32[16,2,512]{2,1,0:T(2,128)} %map_ref.3, f32[8,256,128]{2,1,0:T(8,128)} %copy-done.1, f32[2,64,256]{2,1,0:T(8,128)} %get-tuple-element.55.refs_0_, f32[2,64,256]{2,1,0:T(8,128)} %copy-done.15, ...), custom_call_target="tpu_custom_call" | custom-call | tf_op jit(solution)/shard_map/front/pallas_call | solution.py:379
  147.6 6.8 %psum.7.count_ref = f32[1]{0:T(128)} all-reduce(f32[1]{0:T(128)} %bitcast.4), channel_id=1, replica_groups=mesh['row'=8,'col'=4] {'col'}, use_global_device_ids=true, to_apply=%region_2.3 | all-reduce | flops 1 | bytes 8 | tf_op jit(solution)/shard_map/psum | solution.py:492
  154.4 6.2 %schur.1 = (f32[80,768]{1,0:T(8,128)}, f32[80,768]{1,0:T(8,128)}, f32[80,768]{1,0:T(8,128)}, f32[80,768]{1,0:T(8,128)}, f32[80,768]{1,0:T(8,128)}, /*index=5*/f3...) custom-call(s32[1]{0:T(128)} %bitcast.row_ref.refs_0_, f32[1]{0:T(128)} %psum.7.count_ref, ...), custom_call_target="tpu_custom_call" | custom-call | tf_op jit(solution)/shard_map/schur/pallas_call | solution.py:410
  162.4 2.8 %collective-permute-start.15 = (f32[80,768]{1,0:T(8,128)}, f32[80,768]{1,0:T(8,128)S(1)}, u32[]{:S(2)}, u32[]{:S(2)}) collective-permute-start(f32[80,768]{1,0:T(8,128)} %get-tuple-element.69), channel_id=1, source_target_pairs={{0,8},{4,12},{8,0},{12,4},{16,24},{20,28},{24,16},{28,20},{1,9},{5... | collective-permute-start | bytes 737288 | tf_op jit(solution)/shard_map/ppermute | solution.py:470
  166.6 3.8 %collective-permute-start.13 = (f32[80,768]{1,0:T(8,128)}, f32[80,768]{1,0:T(8,128)S(1)}, u32[]{:S(2)}, u32[]{:S(2)}) collective-permute-start(f32[80,768]{1,0:T(8,128)} %get-tuple-element.66), channel_id=1, source_target_pairs={{0,16},{4,20},{8,24},{12,28},{16,0},{20,4},{24,8},{28,12},{1,17},{... | collective-permute-start | bytes 737288 | tf_op jit(solution)/shard_map/ppermute | solution.py:470
  170.4 2.4 %collective-permute-start.11 = (f32[80,768]{1,0:T(8,128)}, f32[80,768]{1,0:T(8,128)S(1)}, u32[]{:S(2)}, u32[]{:S(2)}) collective-permute-start(f32[80,768]{1,0:T(8,128)} %get-tuple-element.64), channel_id=1, source_target_pairs={{0,24},{4,28},{8,16},{12,20},{16,8},{20,12},{24,0},{28,4},{1,25},{... | collective-permute-start | bytes 737288 | tf_op jit(solution)/shard_map/ppermute | solution.py:470
  172.7 8.5 %collective-permute-done.15.refs_2_ = f32[80,768]{1,0:T(8,128)S(1)} collective-permute-done((f32[80,768]{1,0:T(8,128)}, f32[80,768]{1,0:T(8,128)S(1)}, u32[]{:S(2)}, u32[]{:S(2)}) %collective-permute-start.15) | collective-permute-done | bytes 245792 | tf_op jit(solution)/shard_map/ppermute | solution.py:470
  181.2 4.1 %collective-permute-start.10 = (f32[80,768]{1,0:T(8,128)}, f32[80,768]{1,0:T(8,128)S(1)}, u32[]{:S(2)}, u32[]{:S(2)}) collective-permute-start(f32[80,768]{1,0:T(8,128)} %get-tuple-element.63), channel_id=1, source_target_pairs={{0,28},{4,24},{8,20},{12,16},{16,12},{20,8},{24,4},{28,0},{1,29},{... | collective-permute-start | bytes 737288 | tf_op jit(solution)/shard_map/ppermute | solution.py:470
  186.7 4.4 %finish.1 = (f32[8,2,80,128]{3,2,1,0:T(8,128)}, f32[8,2,80,640]{3,2,1,0:T(8,128)}) custom-call(f32[8,2,80,768]{3,2,1,0:T(8,128)} %bitcast.12, f32[8,80,768]{2,1,0:T(8,128)} %copy-done), custom_call_target="tpu_custom_call" | custom-call | tf_op jit(solution)/shard_map/finish/pallas_call | solution.py:423
  191.6 4.1 %last.5 = (f32[16,80,128]{2,1,0:T(8,128)}, f32[16,80,640]{2,1,0:T(8,128)}, f32[1,128]{1,0:T(1,128)}) custom-call(s32[1]{0:T(128)} %bitcast.row_ref.refs_0_, f32[16,80,768]{2,1,0:T(8,128)} %update_ref.9, f32[80,768]{1,0:T(8,128)} %get-tuple-element.67.refs_0_, f32[80,768]{1,0:T(8,128)} %copy-done.9, ...), custom_call_target="tpu_custom_call", output_to_operand_aliasing={{0}: (7, {}), {1}: (8, {})} | custom-call | tf_op jit(solution)/shard_map/last/pallas_call | solution.py:444
  198.3 4.9 %collective-permute-done.12.refs_0_ = f32[80,768]{1,0:T(8,128)S(1)} collective-permute-done((f32[80,768]{1,0:T(8,128)}, f32[80,768]{1,0:T(8,128)S(1)}, u32[]{:S(2)}, u32[]{:S(2)}) %collective-permute-start.12) | collective-permute-done | bytes 245792 | tf_op jit(solution)/shard_map/ppermute | solution.py:470
  (73 shorter events, 31.7 us)
Async XLA Ops:
  3.2 78.6 %all-to-all-start = ((f32[8,256,128]{2,1,0:T(8,128)}), f32[8,256,128]{2,1,0:T(8,128)S(1)}, u32[]{:S(2)}, u32[]{:S(2)}) async-start(f32[8,256,128]{2,1,0:T(8,128)} %pack.1), calls=%async_computation | async-start | bytes 2097152 | tf_op jit(solution)/shard_map/all_to_all | solution.py:481
  12.7 33.3 %collective-permute-start.3 = (f32[256,128]{1,0:T(8,128)}, f32[256,128]{1,0:T(8,128)S(1)}, u32[]{:S(2)}, u32[]{:S(2)}) collective-permute-start(f32[256,128]{1,0:T(8,128)} %get-tuple-element.50), channel_id=1, source_target_pairs={{0,16},{4,20},{8,24},{12,28},{16,0},{20,4},{24,8},{28,12},{1,17},{... | collective-permute-start | bytes 393224 | tf_op jit(solution)/shard_map/ppermute | solution.py:470
  15.6 30.4 %copy-start.19 = (f32[256,128]{1,0:T(8,128)S(1)}, f32[256,128]{1,0:T(8,128)}, u32[]{:S(2)}) copy-start(f32[256,128]{1,0:T(8,128)} %get-tuple-element.52) | copy-start | bytes 393220
  15.7 34.0 %copy-start.18 = (f32[256,128]{1,0:T(8,128)S(1)}, f32[256,128]{1,0:T(8,128)}, u32[]{:S(2)}) copy-start(f32[256,128]{1,0:T(8,128)} %get-tuple-element.53) | copy-start | bytes 393220
  15.7 34.0 %collective-permute-start.4 = (f32[256,128]{1,0:T(8,128)}, f32[256,128]{1,0:T(8,128)S(1)}, u32[]{:S(2)}, u32[]{:S(2)}) collective-permute-start(f32[256,128]{1,0:T(8,128)} %get-tuple-element.51), channel_id=1, source_target_pairs={{0,20},{4,16},{8,28},{12,24},{16,4},{20,0},{24,12},{28,8},{1,21},{... | collective-permute-start | bytes 393224 | tf_op jit(solution)/shard_map/ppermute | solution.py:470
  19.7 37.7 %collective-permute-start = (f32[512,128]{1,0:T(8,128)}, f32[512,128]{1,0:T(8,128)S(1)}, u32[]{:S(2)}, u32[]{:S(2)}) collective-permute-start(f32[512,128]{1,0:T(8,128)} %get-tuple-element.47), channel_id=1, source_target_pairs={{0,4},{4,0},{8,12},{12,8},{16,20},{20,16},{24,28},{28,24},{1,5},{5... | collective-permute-start | bytes 786440 | tf_op jit(solution)/shard_map/ppermute | solution.py:470
  19.8 37.6 %collective-permute-start.1 = (f32[512,128]{1,0:T(8,128)}, f32[512,128]{1,0:T(8,128)S(1)}, u32[]{:S(2)}, u32[]{:S(2)}) collective-permute-start(f32[512,128]{1,0:T(8,128)} %get-tuple-element.48), channel_id=1, source_target_pairs={{0,8},{4,12},{8,0},{12,4},{16,24},{20,28},{24,16},{28,20},{1,9},{5... | collective-permute-start | bytes 786440 | tf_op jit(solution)/shard_map/ppermute | solution.py:470
  21.8 35.7 %collective-permute-start.2 = (f32[512,128]{1,0:T(8,128)}, f32[512,128]{1,0:T(8,128)S(1)}, u32[]{:S(2)}, u32[]{:S(2)}) collective-permute-start(f32[512,128]{1,0:T(8,128)} %get-tuple-element.49), channel_id=1, source_target_pairs={{0,12},{4,8},{8,4},{12,0},{16,28},{20,24},{24,20},{28,16},{1,13},{... | collective-permute-start | bytes 786440 | tf_op jit(solution)/shard_map/ppermute | solution.py:470
  46.1 11.4 %copy-start.11 = (f32[256,128]{1,0:T(8,128)}, f32[256,128]{1,0:T(8,128)S(1)}, u32[]{:S(2)}) copy-start(f32[256,128]{1,0:T(8,128)S(1)} %collective-permute-done.3.refs_4_) | copy-start | bytes 393220
  46.1 8.2 %collective-permute-start.5 = (f32[256,128]{1,0:T(8,128)S(1)}, f32[256,128]{1,0:T(8,128)S(1)}, u32[]{:S(2)}, u32[]{:S(2)}) collective-permute-start(f32[256,128]{1,0:T(8,128)S(1)} %copy-done.19), channel_id=1, source_target_pairs={{0,24},{4,28},{8,16},{12,20},{16,8},{20,12},{24,0},{28,4},{1,25},{... | collective-permute-start | bytes 393224 | tf_op jit(solution)/shard_map/ppermute | solution.py:470
  49.6 7.8 %collective-permute-start.6 = (f32[256,128]{1,0:T(8,128)S(1)}, f32[256,128]{1,0:T(8,128)S(1)}, u32[]{:S(2)}, u32[]{:S(2)}) collective-permute-start(f32[256,128]{1,0:T(8,128)S(1)} %copy-done.18), channel_id=1, source_target_pairs={{0,28},{4,24},{8,20},{12,16},{16,12},{20,8},{24,4},{28,0},{1,29},{... | collective-permute-start | bytes 393224 | tf_op jit(solution)/shard_map/ppermute | solution.py:470
  81.8 103.5 %all-to-all-start.1 = ((f32[8,80,768]{2,1,0:T(8,128)}), f32[8,80,768]{2,1,0:T(8,128)S(1)}, u32[]{:S(2)}, u32[]{:S(2)}) async-start(f32[8,80,768]{2,1,0:T(8,128)} %bitcast.16), calls=%async_computation.1 | async-start | bytes 3932160 | tf_op jit(solution)/shard_map/all_to_all | solution.py:489
  87.8 17.5 %collective-permute-start.7 = (f32[2,64,256]{2,1,0:T(8,128)}, f32[2,64,256]{2,1,0:T(8,128)S(1)}, u32[]{:S(2)}, u32[]{:S(2)}) collective-permute-start(f32[2,64,256]{2,1,0:T(8,128)} %get-tuple-element.56), channel_id=1, source_target_pairs={{0,4},{4,0},{8,12},{12,8},{16,20},{20,16},{24,28},{28,24},{1,5},{5... | collective-permute-start | bytes 393224 | tf_op jit(solution)/shard_map/ppermute | solution.py:470
  89.8 32.0 %collective-permute-start.8 = (f32[2,64,256]{2,1,0:T(8,128)}, f32[2,64,256]{2,1,0:T(8,128)S(1)}, u32[]{:S(2)}, u32[]{:S(2)}) collective-permute-start(f32[2,64,256]{2,1,0:T(8,128)} %get-tuple-element.57), channel_id=1, source_target_pairs={{0,8},{4,12},{8,0},{12,4},{16,24},{20,28},{24,16},{28,20},{1,9},{5... | collective-permute-start | bytes 393224 | tf_op jit(solution)/shard_map/ppermute | solution.py:470
  91.3 32.0 %collective-permute-start.9 = (f32[2,64,256]{2,1,0:T(8,128)}, f32[2,64,256]{2,1,0:T(8,128)S(1)}, u32[]{:S(2)}, u32[]{:S(2)}) collective-permute-start(f32[2,64,256]{2,1,0:T(8,128)} %get-tuple-element.58), channel_id=1, source_target_pairs={{0,12},{4,8},{8,4},{12,0},{16,28},{20,24},{24,20},{28,16},{1,13},{... | collective-permute-start | bytes 393224 | tf_op jit(solution)/shard_map/ppermute | solution.py:470
  105.3 17.9 %copy-start.15 = (f32[2,64,256]{2,1,0:T(8,128)}, f32[2,64,256]{2,1,0:T(8,128)S(1)}, u32[]{:S(2)}) copy-start(f32[2,64,256]{2,1,0:T(8,128)S(1)} %collective-permute-done.7.refs_1_) | copy-start | bytes 393220
  160.6 9.8 %collective-permute-start.14 = (f32[80,768]{1,0:T(8,128)}, f32[80,768]{1,0:T(8,128)S(1)}, u32[]{:S(2)}, u32[]{:S(2)}) collective-permute-start(f32[80,768]{1,0:T(8,128)} %get-tuple-element.68), channel_id=1, source_target_pairs={{0,4},{4,0},{8,12},{12,8},{16,20},{20,16},{24,28},{28,24},{1,5},{5... | collective-permute-start | bytes 737288 | tf_op jit(solution)/shard_map/ppermute | solution.py:470
  162.4 18.8 %collective-permute-start.15 = (f32[80,768]{1,0:T(8,128)}, f32[80,768]{1,0:T(8,128)S(1)}, u32[]{:S(2)}, u32[]{:S(2)}) collective-permute-start(f32[80,768]{1,0:T(8,128)} %get-tuple-element.69), channel_id=1, source_target_pairs={{0,8},{4,12},{8,0},{12,4},{16,24},{20,28},{24,16},{28,20},{1,9},{5... | collective-permute-start | bytes 737288 | tf_op jit(solution)/shard_map/ppermute | solution.py:470
  165.1 26.0 %collective-permute-start.16 = (f32[80,768]{1,0:T(8,128)}, f32[80,768]{1,0:T(8,128)}, u32[]{:S(2)}, u32[]{:S(2)}) collective-permute-start(f32[80,768]{1,0:T(8,128)} %get-tuple-element.70), channel_id=1, source_target_pairs={{0,12},{4,8},{8,4},{12,0},{16,28},{20,24},{24,20},{28,16},{1,13},{... | collective-permute-start | bytes 737288 | tf_op jit(solution)/shard_map/ppermute | solution.py:470
  166.6 29.1 %collective-permute-start.13 = (f32[80,768]{1,0:T(8,128)}, f32[80,768]{1,0:T(8,128)S(1)}, u32[]{:S(2)}, u32[]{:S(2)}) collective-permute-start(f32[80,768]{1,0:T(8,128)} %get-tuple-element.66), channel_id=1, source_target_pairs={{0,16},{4,20},{8,24},{12,28},{16,0},{20,4},{24,8},{28,12},{1,17},{... | collective-permute-start | bytes 737288 | tf_op jit(solution)/shard_map/ppermute | solution.py:470
  170.4 32.8 %collective-permute-start.12 = (f32[80,768]{1,0:T(8,128)}, f32[80,768]{1,0:T(8,128)S(1)}, u32[]{:S(2)}, u32[]{:S(2)}) collective-permute-start(f32[80,768]{1,0:T(8,128)} %get-tuple-element.65), channel_id=1, source_target_pairs={{0,20},{4,16},{8,28},{12,24},{16,4},{20,0},{24,12},{28,8},{1,21},{... | collective-permute-start | bytes 737288 | tf_op jit(solution)/shard_map/ppermute | solution.py:470
  170.4 21.3 %copy-start.9 = (f32[80,768]{1,0:T(8,128)}, f32[80,768]{1,0:T(8,128)S(1)}, u32[]{:S(2)}) copy-start(f32[80,768]{1,0:T(8,128)S(1)} %collective-permute-done.14.refs_1_) | copy-start | bytes 737284
  170.4 35.4 %collective-permute-start.11 = (f32[80,768]{1,0:T(8,128)}, f32[80,768]{1,0:T(8,128)S(1)}, u32[]{:S(2)}, u32[]{:S(2)}) collective-permute-start(f32[80,768]{1,0:T(8,128)} %get-tuple-element.64), channel_id=1, source_target_pairs={{0,24},{4,28},{8,16},{12,20},{16,8},{20,12},{24,0},{28,4},{1,25},{... | collective-permute-start | bytes 737288 | tf_op jit(solution)/shard_map/ppermute | solution.py:470
  181.2 27.1 %collective-permute-start.10 = (f32[80,768]{1,0:T(8,128)}, f32[80,768]{1,0:T(8,128)S(1)}, u32[]{:S(2)}, u32[]{:S(2)}) collective-permute-start(f32[80,768]{1,0:T(8,128)} %get-tuple-element.63), channel_id=1, source_target_pairs={{0,28},{4,24},{8,20},{12,16},{16,12},{20,8},{24,4},{28,0},{1,29},{... | collective-permute-start | bytes 737288 | tf_op jit(solution)/shard_map/ppermute | solution.py:470
  (16 other events, 42.5 us)

commit v5 on v4

--- a/solution.py
+++ b/solution.py
@@ -155,25 +155,38 @@
 
 def eliminate(aug_ref):
     size = aug_ref.shape[0]
-    lanes = lax.broadcasted_iota(jnp.int32, (1, size), 1)
-    step = 32
-    pivots = jnp.zeros((1, size), jnp.float32)
-    for start in range(0, size, step):
-        rest = size - start
-        below = start + lax.broadcasted_iota(jnp.int32, (rest, 1), 0)
-
-        def one(k, pivots, start=start, below=below):
-            row = aug_ref[pl.ds(k, 1), :]
-            whole = aug_ref[start:, :]
-            chosen = lanes == k
-            column = jnp.sum(jnp.where(chosen, whole[:, :size], 0.0), axis=1, keepdims=True)
-            pivot = jnp.sum(jnp.where(chosen, row[:, :size], 0.0), axis=1, keepdims=True)
-            multiplier = jnp.where(below > k, column / pivot, 0.0)
-            aug_ref[start:, :] = whole - multiplier * row
-            return jnp.where(chosen, pivot, pivots)
-
-        pivots = lax.fori_loop(start, start + step, one, pivots)
-    return pivots
+    panel = 16
+    shape = (panel, size)
+    sub = lax.broadcasted_iota(jnp.int32, shape, 0)
+    lane = lax.broadcasted_iota(jnp.int32, shape, 1)
+
+    def one(block, pivots):
+        base = pl.multiple_of(block * panel, panel)
+        left = aug_ref[pl.ds(base, panel), :size]
+        right = aug_ref[pl.ds(base, panel), size:]
+        turned = pltpu.roll(left, lax.rem(size - base, size), 1)
+        columns = [jnp.broadcast_to(turned[:, j : j + 1], shape) for j in range(panel)]
+        scale = jnp.zeros(shape, jnp.float32)
+        for j in range(panel):
+            pivot = columns[j][j : j + 1, :]
+            inverse = 1.0 / pivot
+            multiplier = jnp.where(sub > j, columns[j] * inverse, 0.0)
+            for k in range(j + 1, panel):
+                columns[k] = columns[k] - multiplier * columns[k][j : j + 1, :]
+            left = left - multiplier * left[j : j + 1, :]
+            right = right - multiplier * right[j : j + 1, :]
+            scale = jnp.where(sub == j, inverse, scale)
+            pivots = jnp.where(lane[:1] == base + j, pivot, pivots)
+        aug_ref[pl.ds(base, panel), :size] = left
+        aug_ref[pl.ds(base, panel), size:] = right
+        lower = jnp.where(lane >= base + panel, left * scale, 0.0)
+        both = jnp.concatenate([left, right], axis=1)
+        aug_ref[...] -= lax.dot_general(
+            lower, both, (((0,), (0,)), ((), ())), precision=highest, preferred_element_type=jnp.float32
+        )
+        return pivots
+
+    return lax.fori_loop(0, size // panel, one, jnp.zeros((1, size), jnp.float32))
 
 
 def trailing(sum_ref, size, start):
@@ -472,7 +485,8 @@
     arrays = []
     for turn in range(per - 1):
         far = parts_for(turn, range(half, n))
-        far = [send(part, half + flip) for flip, part in enumerate(far)]
+        sent = [send(part, half + flip) for flip, part in enumerate(far[:-1])]
+        far = sent + [send(far[-1], n - 1)]
         near = parts_for(turn, range(half))
         near = [near[0]] + [send(near[flip], flip) for flip in range(1, half)]
         arrays.append(near + far)

time: 215 us -> 200 us (0.930)
  Pallas kernels: 76.2 us -> 61.4 us
    pallas_call x2, Pallas kernels: 44.7 us -> 29.9 us  [from_arrived(): pl.pallas_call(functools.partial(kernel, dims + (update_rows, pivot_rows)...]
  transfers between devices with their start and end apart: 19 -> 19, of which waited for: 9 -> 9; matrix products, arithmetic and copies ran while one was open for 1% -> 1% of each run, Pallas kernels for 34% -> 29%
where the time goes in v5:
time: 200 us; the launch traced here: 198 us
  waiting for transfers between devices  77.7 us (39%)
  Pallas kernels  61.4 us (31%)
  starting transfers between devices  40.3 us (20%)
  blocking collectives  6.81 us (3%)
  local copies, waits for them, and re-layouts  6.11 us (3%)
  between operations  3.67 us (2%)
    ppermute x17, waiting for transfers between devices, send(): return lax.ppermute(part, 'row', [(i, i ^ flip) for i in range(n)])  77.7 us
    pallas_call x2, Pallas kernels, from_arrived(): pl.pallas_call(functools.partial(kernel, dims + (update_rows, pivot_rows)...  29.9 us
    ppermute x17, starting transfers between devices, send(): return lax.ppermute(part, 'row', [(i, i ^ flip) for i in range(n)])  28.9 us
    pallas_call x5, Pallas kernels, last(): pl.pallas_call(functools.partial(last_kernel, size, count), grid_spec=plt...  11.5 us
    all_to_all x1, starting transfers between devices, local_body(): arrived = exchange(packed)  7.28 us
    psum x1, blocking collectives, local_body(): lax.psum(total + jnp.sum(jnp.where(parts[3] < 0.0, 1.0, 0.0)), 'col')  6.81 us
    pallas_call x1, Pallas kernels, schur_rows(): pl.pallas_call(schur_kernel, in_specs=[smem, smem] + [vmem] * 4, out_spec...  6.17 us
    unnamed x42, local copies, waits for them, and re-layouts  5.57 us
  transfers between devices with their start and end apart: 19, of which 9 were waited for; matrix products, arithmetic and copies ran while one was open for 1% of the time, Pallas kernels for 29%

profile of v5, /device:TPU:0, one launch (start us, length us, event | category | flops | bytes accessed | tf_op | source)
XLA Modules:
  0.0 197.8 jit_solution(12779649414457694406)
XLA Ops:
  0.6 2.6 %pack.1 = f32[8,256,128]{2,1,0:T(8,128)} custom-call(s32[1]{0:T(128)} %bitcast.row_ref.refs_0_, f32[8,2,2,64,512]{4,3,2,1,0:T(8,128)} %bitcast.10, f32[8,2,80,768]{3,2,1,0:T(8,128)} %bitcast.11, f32[8,2,16,128]{3,2,1,0:T(8,128)} %bitcast.15), custom_call_target="tpu_custom_call" | custom-call | tf_op jit(solution)/shard_map/pack/pallas_call | solution.py:324
  3.2 7.3 %all-to-all-start = ((f32[8,256,128]{2,1,0:T(8,128)}), f32[8,256,128]{2,1,0:T(8,128)S(1)}, u32[]{:S(2)}, u32[]{:S(2)}) async-start(f32[8,256,128]{2,1,0:T(8,128)} %pack.1), calls=%async_computation | async-start | bytes 2097152 | tf_op jit(solution)/shard_map/all_to_all | solution.py:495
  10.5 2.2 %parts.3 = (f32[256,128]{1,0:T(8,128)}, f32[256,128]{1,0:T(8,128)}, f32[256,128]{1,0:T(8,128)}, f32[256,128]{1,0:T(8,128)}) custom-call(s32[1]{0:T(128)} %bitcast.row_ref.refs_0_, f32[16,2,64,512]{3,2,1,0:T(8,128)} %refs_4_.5, f32[16,2,64,512]{3,2,1,0:T(8,128)} %refs_4_.5, f32[16,2,64,512]{3,2,1,0:T(8,128)} %refs_4_.5, f32[16,2,64,512]{3,2,1,0:T(8,128)} %refs_4_.5, ...), custom_call_target="tpu_custom_call" | custom-call | tf_op jit(solution)/shard_map/parts/pallas_call | solution.py:364
  12.7 2.9 %collective-permute-start.3 = (f32[256,128]{1,0:T(8,128)}, f32[256,128]{1,0:T(8,128)S(1)}, u32[]{:S(2)}, u32[]{:S(2)}) collective-permute-start(f32[256,128]{1,0:T(8,128)} %get-tuple-element.50), channel_id=1, source_target_pairs={{0,16},{4,20},{8,24},{12,28},{16,0},{20,4},{24,8},{28,12},{1,17},{... | collective-permute-start | bytes 393224 | tf_op jit(solution)/shard_map/ppermute | solution.py:483
  17.1 2.6 %parts.2 = (f32[512,128]{1,0:T(8,128)}, f32[512,128]{1,0:T(8,128)}, f32[512,128]{1,0:T(8,128)}, f32[512,128]{1,0:T(8,128)}) custom-call(s32[1]{0:T(128)} %bitcast.row_ref.refs_0_, f32[16,2,64,512]{3,2,1,0:T(8,128)} %refs_4_.5, f32[16,2,64,512]{3,2,1,0:T(8,128)} %refs_4_.5, f32[16,2,64,512]{3,2,1,0:T(8,128)} %refs_4_.5, f32[16,2,64,512]{3,2,1,0:T(8,128)} %refs_4_.5, ...), custom_call_target="tpu_custom_call" | custom-call | tf_op jit(solution)/shard_map/parts/pallas_call | solution.py:364
  23.2 22.8 %collective-permute-done.3.refs_4_ = f32[256,128]{1,0:T(8,128)S(1)} collective-permute-done((f32[256,128]{1,0:T(8,128)}, f32[256,128]{1,0:T(8,128)S(1)}, u32[]{:S(2)}, u32[]{:S(2)}) %collective-permute-start.3) | collective-permute-done | bytes 131104 | tf_op jit(solution)/shard_map/ppermute | solution.py:483
  46.1 3.5 %collective-permute-done.4.refs_5_ = f32[256,128]{1,0:T(8,128)S(1)} collective-permute-done((f32[256,128]{1,0:T(8,128)}, f32[256,128]{1,0:T(8,128)S(1)}, u32[]{:S(2)}, u32[]{:S(2)}) %collective-permute-start.4) | collective-permute-done | bytes 131104 | tf_op jit(solution)/shard_map/ppermute | solution.py:483
  50.4 3.8 %collective-permute-done.5.refs_6_ = f32[256,128]{1,0:T(8,128)S(1)} collective-permute-done((f32[256,128]{1,0:T(8,128)S(1)}, f32[256,128]{1,0:T(8,128)S(1)}, u32[]{:S(2)}, u32[]{:S(2)}) %collective-permute-start.5) | collective-permute-done | bytes 131104 | tf_op jit(solution)/shard_map/ppermute | solution.py:483
  54.2 3.2 %collective-permute-done.6.refs_7_ = f32[256,128]{1,0:T(8,128)S(1)} collective-permute-done((f32[256,128]{1,0:T(8,128)S(1)}, f32[256,128]{1,0:T(8,128)S(1)}, u32[]{:S(2)}, u32[]{:S(2)}) %collective-permute-start.6) | collective-permute-done | bytes 131104 | tf_op jit(solution)/shard_map/ppermute | solution.py:483
  58.3 16.1 %front.2 = (f32[640,768]{1,0:T(8,128)}, f32[1,128]{1,0:T(1,128)}) custom-call(s32[1]{0:T(128)} %bitcast.row_ref.refs_0_, s32[16,2,512]{2,1,0:T(2,128)} %map_ref.3, f32[512,128]{1,0:T(8,128)} %get-tuple-element.46.refs_0_, f32[512,128]{1,0:T(8,128)} %copy-done.2, f32[512,128]{1,0:T(8,128)} %copy-done.3, f32[512,128]{1,0:T(8,128)} %copy-done.4, ...), custom_call_target="tpu_custom_call" | custom-call | tf_op jit(solution)/shard_map/front/pallas_call | solution.py:392
  74.4 4.1 %all-to-all-start.1 = ((f32[8,80,768]{2,1,0:T(8,128)}), f32[8,80,768]{2,1,0:T(8,128)S(1)}, u32[]{:S(2)}, u32[]{:S(2)}) async-start(f32[8,80,768]{2,1,0:T(8,128)} %bitcast.16), calls=%async_computation.1 | async-start | bytes 3932160 | tf_op jit(solution)/shard_map/all_to_all | solution.py:503
  84.9 13.0 %collective-permute-done.7.refs_1_ = f32[2,64,256]{2,1,0:T(8,128)S(1)} collective-permute-done((f32[2,64,256]{2,1,0:T(8,128)}, f32[2,64,256]{2,1,0:T(8,128)S(1)}, u32[]{:S(2)}, u32[]{:S(2)}) %collective-permute-start.7) | collective-permute-done | bytes 131104 | tf_op jit(solution)/shard_map/ppermute | solution.py:483
  97.9 16.5 %collective-permute-done.8.refs_2_ = f32[2,64,256]{2,1,0:T(8,128)S(1)} collective-permute-done((f32[2,64,256]{2,1,0:T(8,128)}, f32[2,64,256]{2,1,0:T(8,128)S(1)}, u32[]{:S(2)}, u32[]{:S(2)}) %collective-permute-start.8) | collective-permute-done | bytes 131104 | tf_op jit(solution)/shard_map/ppermute | solution.py:483
  116.5 13.8 %front.3 = (f32[640,640]{1,0:T(8,128)}, f32[640,128]{1,0:T(8,128)}, f32[128,128]{1,0:T(8,128)}, f32[1,128]{1,0:T(1,128)}) custom-call(s32[1]{0:T(128)} %bitcast.row_ref.refs_0_, s32[16,2,512]{2,1,0:T(2,128)} %map_ref.3, f32[8,256,128]{2,1,0:T(8,128)} %copy-done.1, f32[2,64,256]{2,1,0:T(8,128)} %get-tuple-element.55.refs_0_, f32[2,64,256]{2,1,0:T(8,128)} %copy-done.15, ...), custom_call_target="tpu_custom_call" | custom-call | tf_op jit(solution)/shard_map/front/pallas_call | solution.py:392
  132.8 6.8 %psum.7.count_ref = f32[1]{0:T(128)} all-reduce(f32[1]{0:T(128)} %bitcast.4), channel_id=1, replica_groups=mesh['row'=8,'col'=4] {'col'}, use_global_device_ids=true, to_apply=%region_2.3 | all-reduce | flops 1 | bytes 8 | tf_op jit(solution)/shard_map/psum | solution.py:506
  139.6 6.2 %schur.1 = (f32[80,768]{1,0:T(8,128)}, f32[80,768]{1,0:T(8,128)}, f32[80,768]{1,0:T(8,128)}, f32[80,768]{1,0:T(8,128)}, f32[80,768]{1,0:T(8,128)}, /*index=5*/f3...) custom-call(s32[1]{0:T(128)} %bitcast.row_ref.refs_0_, f32[1]{0:T(128)} %psum.7.count_ref, ...), custom_call_target="tpu_custom_call" | custom-call | tf_op jit(solution)/shard_map/schur/pallas_call | solution.py:423
  147.6 2.8 %collective-permute-start.15 = (f32[80,768]{1,0:T(8,128)}, f32[80,768]{1,0:T(8,128)S(1)}, u32[]{:S(2)}, u32[]{:S(2)}) collective-permute-start(f32[80,768]{1,0:T(8,128)} %get-tuple-element.69), channel_id=1, source_target_pairs={{0,8},{4,12},{8,0},{12,4},{16,24},{20,28},{24,16},{28,20},{1,9},{5... | collective-permute-start | bytes 737288 | tf_op jit(solution)/shard_map/ppermute | solution.py:483
  151.8 3.8 %collective-permute-start.13 = (f32[80,768]{1,0:T(8,128)}, f32[80,768]{1,0:T(8,128)S(1)}, u32[]{:S(2)}, u32[]{:S(2)}) collective-permute-start(f32[80,768]{1,0:T(8,128)} %get-tuple-element.66), channel_id=1, source_target_pairs={{0,16},{4,20},{8,24},{12,28},{16,0},{20,4},{24,8},{28,12},{1,17},{... | collective-permute-start | bytes 737288 | tf_op jit(solution)/shard_map/ppermute | solution.py:483
  155.6 2.4 %collective-permute-start.11 = (f32[80,768]{1,0:T(8,128)}, f32[80,768]{1,0:T(8,128)S(1)}, u32[]{:S(2)}, u32[]{:S(2)}) collective-permute-start(f32[80,768]{1,0:T(8,128)} %get-tuple-element.64), channel_id=1, source_target_pairs={{0,24},{4,28},{8,16},{12,20},{16,8},{20,12},{24,0},{28,4},{1,25},{... | collective-permute-start | bytes 737288 | tf_op jit(solution)/shard_map/ppermute | solution.py:483
  158.0 8.4 %collective-permute-done.15.refs_2_ = f32[80,768]{1,0:T(8,128)S(1)} collective-permute-done((f32[80,768]{1,0:T(8,128)}, f32[80,768]{1,0:T(8,128)S(1)}, u32[]{:S(2)}, u32[]{:S(2)}) %collective-permute-start.15) | collective-permute-done | bytes 245792 | tf_op jit(solution)/shard_map/ppermute | solution.py:483
  166.4 4.1 %collective-permute-start.10 = (f32[80,768]{1,0:T(8,128)}, f32[80,768]{1,0:T(8,128)S(1)}, u32[]{:S(2)}, u32[]{:S(2)}) collective-permute-start(f32[80,768]{1,0:T(8,128)} %get-tuple-element.63), channel_id=1, source_target_pairs={{0,28},{4,24},{8,20},{12,16},{16,12},{20,8},{24,4},{28,0},{1,29},{... | collective-permute-start | bytes 737288 | tf_op jit(solution)/shard_map/ppermute | solution.py:483
  171.9 4.4 %finish.1 = (f32[8,2,80,128]{3,2,1,0:T(8,128)}, f32[8,2,80,640]{3,2,1,0:T(8,128)}) custom-call(f32[8,2,80,768]{3,2,1,0:T(8,128)} %bitcast.12, f32[8,80,768]{2,1,0:T(8,128)} %copy-done), custom_call_target="tpu_custom_call" | custom-call | tf_op jit(solution)/shard_map/finish/pallas_call | solution.py:436
  176.9 4.1 %last.5 = (f32[16,80,128]{2,1,0:T(8,128)}, f32[16,80,640]{2,1,0:T(8,128)}, f32[1,128]{1,0:T(1,128)}) custom-call(s32[1]{0:T(128)} %bitcast.row_ref.refs_0_, f32[16,80,768]{2,1,0:T(8,128)} %update_ref.9, f32[80,768]{1,0:T(8,128)} %get-tuple-element.67.refs_0_, f32[80,768]{1,0:T(8,128)} %copy-done.9, ...), custom_call_target="tpu_custom_call", output_to_operand_aliasing={{0}: (7, {}), {1}: (8, {})} | custom-call | tf_op jit(solution)/shard_map/last/pallas_call | solution.py:457
  183.5 4.9 %collective-permute-done.12.refs_0_ = f32[80,768]{1,0:T(8,128)S(1)} collective-permute-done((f32[80,768]{1,0:T(8,128)}, f32[80,768]{1,0:T(8,128)S(1)}, u32[]{:S(2)}, u32[]{:S(2)}) %collective-permute-start.12) | collective-permute-done | bytes 245792 | tf_op jit(solution)/shard_map/ppermute | solution.py:483
  (73 shorter events, 31.7 us)
Async XLA Ops:
  3.2 71.2 %all-to-all-start = ((f32[8,256,128]{2,1,0:T(8,128)}), f32[8,256,128]{2,1,0:T(8,128)S(1)}, u32[]{:S(2)}, u32[]{:S(2)}) async-start(f32[8,256,128]{2,1,0:T(8,128)} %pack.1), calls=%async_computation | async-start | bytes 2097152 | tf_op jit(solution)/shard_map/all_to_all | solution.py:495
  12.7 33.3 %collective-permute-start.3 = (f32[256,128]{1,0:T(8,128)}, f32[256,128]{1,0:T(8,128)S(1)}, u32[]{:S(2)}, u32[]{:S(2)}) collective-permute-start(f32[256,128]{1,0:T(8,128)} %get-tuple-element.50), channel_id=1, source_target_pairs={{0,16},{4,20},{8,24},{12,28},{16,0},{20,4},{24,8},{28,12},{1,17},{... | collective-permute-start | bytes 393224 | tf_op jit(solution)/shard_map/ppermute | solution.py:483
  15.6 30.4 %copy-start.19 = (f32[256,128]{1,0:T(8,128)S(1)}, f32[256,128]{1,0:T(8,128)}, u32[]{:S(2)}) copy-start(f32[256,128]{1,0:T(8,128)} %get-tuple-element.52) | copy-start | bytes 393220
  15.7 34.0 %copy-start.18 = (f32[256,128]{1,0:T(8,128)S(1)}, f32[256,128]{1,0:T(8,128)}, u32[]{:S(2)}) copy-start(f32[256,128]{1,0:T(8,128)} %get-tuple-element.53) | copy-start | bytes 393220
  15.7 34.0 %collective-permute-start.4 = (f32[256,128]{1,0:T(8,128)}, f32[256,128]{1,0:T(8,128)S(1)}, u32[]{:S(2)}, u32[]{:S(2)}) collective-permute-start(f32[256,128]{1,0:T(8,128)} %get-tuple-element.51), channel_id=1, source_target_pairs={{0,20},{4,16},{8,28},{12,24},{16,4},{20,0},{24,12},{28,8},{1,21},{... | collective-permute-start | bytes 393224 | tf_op jit(solution)/shard_map/ppermute | solution.py:483
  19.7 37.7 %collective-permute-start = (f32[512,128]{1,0:T(8,128)}, f32[512,128]{1,0:T(8,128)S(1)}, u32[]{:S(2)}, u32[]{:S(2)}) collective-permute-start(f32[512,128]{1,0:T(8,128)} %get-tuple-element.47), channel_id=1, source_target_pairs={{0,4},{4,0},{8,12},{12,8},{16,20},{20,16},{24,28},{28,24},{1,5},{5... | collective-permute-start | bytes 786440 | tf_op jit(solution)/shard_map/ppermute | solution.py:483
  19.8 37.6 %collective-permute-start.1 = (f32[512,128]{1,0:T(8,128)}, f32[512,128]{1,0:T(8,128)S(1)}, u32[]{:S(2)}, u32[]{:S(2)}) collective-permute-start(f32[512,128]{1,0:T(8,128)} %get-tuple-element.48), channel_id=1, source_target_pairs={{0,8},{4,12},{8,0},{12,4},{16,24},{20,28},{24,16},{28,20},{1,9},{5... | collective-permute-start | bytes 786440 | tf_op jit(solution)/shard_map/ppermute | solution.py:483
  21.8 35.7 %collective-permute-start.2 = (f32[512,128]{1,0:T(8,128)}, f32[512,128]{1,0:T(8,128)S(1)}, u32[]{:S(2)}, u32[]{:S(2)}) collective-permute-start(f32[512,128]{1,0:T(8,128)} %get-tuple-element.49), channel_id=1, source_target_pairs={{0,12},{4,8},{8,4},{12,0},{16,28},{20,24},{24,20},{28,16},{1,13},{... | collective-permute-start | bytes 786440 | tf_op jit(solution)/shard_map/ppermute | solution.py:483
  46.1 11.4 %copy-start.11 = (f32[256,128]{1,0:T(8,128)}, f32[256,128]{1,0:T(8,128)S(1)}, u32[]{:S(2)}) copy-start(f32[256,128]{1,0:T(8,128)S(1)} %collective-permute-done.3.refs_4_) | copy-start | bytes 393220
  46.1 8.2 %collective-permute-start.5 = (f32[256,128]{1,0:T(8,128)S(1)}, f32[256,128]{1,0:T(8,128)S(1)}, u32[]{:S(2)}, u32[]{:S(2)}) collective-permute-start(f32[256,128]{1,0:T(8,128)S(1)} %copy-done.19), channel_id=1, source_target_pairs={{0,24},{4,28},{8,16},{12,20},{16,8},{20,12},{24,0},{28,4},{1,25},{... | collective-permute-start | bytes 393224 | tf_op jit(solution)/shard_map/ppermute | solution.py:483
  49.6 7.8 %collective-permute-start.6 = (f32[256,128]{1,0:T(8,128)S(1)}, f32[256,128]{1,0:T(8,128)S(1)}, u32[]{:S(2)}, u32[]{:S(2)}) collective-permute-start(f32[256,128]{1,0:T(8,128)S(1)} %copy-done.18), channel_id=1, source_target_pairs={{0,28},{4,24},{8,20},{12,16},{16,12},{20,8},{24,4},{28,0},{1,29},{... | collective-permute-start | bytes 393224 | tf_op jit(solution)/shard_map/ppermute | solution.py:483
  74.4 96.2 %all-to-all-start.1 = ((f32[8,80,768]{2,1,0:T(8,128)}), f32[8,80,768]{2,1,0:T(8,128)S(1)}, u32[]{:S(2)}, u32[]{:S(2)}) async-start(f32[8,80,768]{2,1,0:T(8,128)} %bitcast.16), calls=%async_computation.1 | async-start | bytes 3932160 | tf_op jit(solution)/shard_map/all_to_all | solution.py:503
  80.4 17.5 %collective-permute-start.7 = (f32[2,64,256]{2,1,0:T(8,128)}, f32[2,64,256]{2,1,0:T(8,128)S(1)}, u32[]{:S(2)}, u32[]{:S(2)}) collective-permute-start(f32[2,64,256]{2,1,0:T(8,128)} %get-tuple-element.56), channel_id=1, source_target_pairs={{0,4},{4,0},{8,12},{12,8},{16,20},{20,16},{24,28},{28,24},{1,5},{5... | collective-permute-start | bytes 393224 | tf_op jit(solution)/shard_map/ppermute | solution.py:483
  82.4 32.0 %collective-permute-start.8 = (f32[2,64,256]{2,1,0:T(8,128)}, f32[2,64,256]{2,1,0:T(8,128)S(1)}, u32[]{:S(2)}, u32[]{:S(2)}) collective-permute-start(f32[2,64,256]{2,1,0:T(8,128)} %get-tuple-element.57), channel_id=1, source_target_pairs={{0,8},{4,12},{8,0},{12,4},{16,24},{20,28},{24,16},{28,20},{1,9},{5... | collective-permute-start | bytes 393224 | tf_op jit(solution)/shard_map/ppermute | solution.py:483
  83.9 32.0 %collective-permute-start.9 = (f32[2,64,256]{2,1,0:T(8,128)}, f32[2,64,256]{2,1,0:T(8,128)S(1)}, u32[]{:S(2)}, u32[]{:S(2)}) collective-permute-start(f32[2,64,256]{2,1,0:T(8,128)} %get-tuple-element.58), channel_id=1, source_target_pairs={{0,12},{4,8},{8,4},{12,0},{16,28},{20,24},{24,20},{28,16},{1,13},{... | collective-permute-start | bytes 393224 | tf_op jit(solution)/shard_map/ppermute | solution.py:483
  97.9 17.9 %copy-start.15 = (f32[2,64,256]{2,1,0:T(8,128)}, f32[2,64,256]{2,1,0:T(8,128)S(1)}, u32[]{:S(2)}) copy-start(f32[2,64,256]{2,1,0:T(8,128)S(1)} %collective-permute-done.7.refs_1_) | copy-start | bytes 393220
  145.8 9.8 %collective-permute-start.14 = (f32[80,768]{1,0:T(8,128)}, f32[80,768]{1,0:T(8,128)S(1)}, u32[]{:S(2)}, u32[]{:S(2)}) collective-permute-start(f32[80,768]{1,0:T(8,128)} %get-tuple-element.68), channel_id=1, source_target_pairs={{0,4},{4,0},{8,12},{12,8},{16,20},{20,16},{24,28},{28,24},{1,5},{5... | collective-permute-start | bytes 737288 | tf_op jit(solution)/shard_map/ppermute | solution.py:483
  147.6 18.8 %collective-permute-start.15 = (f32[80,768]{1,0:T(8,128)}, f32[80,768]{1,0:T(8,128)S(1)}, u32[]{:S(2)}, u32[]{:S(2)}) collective-permute-start(f32[80,768]{1,0:T(8,128)} %get-tuple-element.69), channel_id=1, source_target_pairs={{0,8},{4,12},{8,0},{12,4},{16,24},{20,28},{24,16},{28,20},{1,9},{5... | collective-permute-start | bytes 737288 | tf_op jit(solution)/shard_map/ppermute | solution.py:483
  150.4 26.0 %collective-permute-start.16 = (f32[80,768]{1,0:T(8,128)}, f32[80,768]{1,0:T(8,128)}, u32[]{:S(2)}, u32[]{:S(2)}) collective-permute-start(f32[80,768]{1,0:T(8,128)} %get-tuple-element.70), channel_id=1, source_target_pairs={{0,12},{4,8},{8,4},{12,0},{16,28},{20,24},{24,20},{28,16},{1,13},{... | collective-permute-start | bytes 737288 | tf_op jit(solution)/shard_map/ppermute | solution.py:483
  151.8 29.1 %collective-permute-start.13 = (f32[80,768]{1,0:T(8,128)}, f32[80,768]{1,0:T(8,128)S(1)}, u32[]{:S(2)}, u32[]{:S(2)}) collective-permute-start(f32[80,768]{1,0:T(8,128)} %get-tuple-element.66), channel_id=1, source_target_pairs={{0,16},{4,20},{8,24},{12,28},{16,0},{20,4},{24,8},{28,12},{1,17},{... | collective-permute-start | bytes 737288 | tf_op jit(solution)/shard_map/ppermute | solution.py:483
  155.6 32.8 %collective-permute-start.12 = (f32[80,768]{1,0:T(8,128)}, f32[80,768]{1,0:T(8,128)S(1)}, u32[]{:S(2)}, u32[]{:S(2)}) collective-permute-start(f32[80,768]{1,0:T(8,128)} %get-tuple-element.65), channel_id=1, source_target_pairs={{0,20},{4,16},{8,28},{12,24},{16,4},{20,0},{24,12},{28,8},{1,21},{... | collective-permute-start | bytes 737288 | tf_op jit(solution)/shard_map/ppermute | solution.py:483
  155.6 21.3 %copy-start.9 = (f32[80,768]{1,0:T(8,128)}, f32[80,768]{1,0:T(8,128)S(1)}, u32[]{:S(2)}) copy-start(f32[80,768]{1,0:T(8,128)S(1)} %collective-permute-done.14.refs_1_) | copy-start | bytes 737284
  155.6 35.4 %collective-permute-start.11 = (f32[80,768]{1,0:T(8,128)}, f32[80,768]{1,0:T(8,128)S(1)}, u32[]{:S(2)}, u32[]{:S(2)}) collective-permute-start(f32[80,768]{1,0:T(8,128)} %get-tuple-element.64), channel_id=1, source_target_pairs={{0,24},{4,28},{8,16},{12,20},{16,8},{20,12},{24,0},{28,4},{1,25},{... | collective-permute-start | bytes 737288 | tf_op jit(solution)/shard_map/ppermute | solution.py:483
  166.4 27.1 %collective-permute-start.10 = (f32[80,768]{1,0:T(8,128)}, f32[80,768]{1,0:T(8,128)S(1)}, u32[]{:S(2)}, u32[]{:S(2)}) collective-permute-start(f32[80,768]{1,0:T(8,128)} %get-tuple-element.63), channel_id=1, source_target_pairs={{0,28},{4,24},{8,20},{12,16},{16,12},{20,8},{24,4},{28,0},{1,29},{... | collective-permute-start | bytes 737288 | tf_op jit(solution)/shard_map/ppermute | solution.py:483
  (16 other events, 42.5 us)

commit v6 on v5

--- a/solution.py
+++ b/solution.py
@@ -213,7 +213,8 @@
 
 def front_kernel(dims, row_ref, map_ref, *refs):
     n, held = dims[:2]
-    out_ref, pivots_ref, hot_ref, half_ref, sum_ref, aug_ref, coup_ref, in_ref = refs[n:]
+    outs, pivots_ref = refs[n : 2 * n], refs[2 * n]
+    hot_ref, half_ref, sum_ref, aug_ref, coup_ref, in_ref, full_ref = refs[2 * n + 1 :]
     rows = in_ref.shape[1]
     for flip in range(n):
         in_ref[row_ref[0] ^ flip] = refs[flip][:rows, :]
@@ -229,7 +230,11 @@
     size = aug_ref.shape[0]
     pivots = eliminate(aug_ref)
     pivots_ref[...] = pivots
-    update(out_ref, coup_ref, aug_ref[:, size:], pivots, functools.partial(trailing, sum_ref, size))
+    update(full_ref, coup_ref, aug_ref[:, size:], pivots, functools.partial(trailing, sum_ref, size))
+    update_rows = outs[0].shape[0]
+    for flip, out_ref in enumerate(outs):
+        at = pl.multiple_of((row_ref[0] ^ flip) * update_rows, 8)
+        out_ref[...] = full_ref[pl.ds(at, update_rows), :]
 
 
 def factor_kernel(dims, row_ref, map_ref, in_ref, *refs):
@@ -264,15 +269,7 @@
         out_ref[:8, :] = jnp.where(chosen, count_ref[0], full_ref[pl.ds(at, 8), :])
 
 
-def finish_kernel(size, update_ref, back_ref, *refs):
-    lhat_ref, schur_ref = refs[-2:]
-    count = update_ref.shape[0]
-    rows = pl.ds(pl.program_id(0) * count, count)
-    lhat_ref[:, 0] = back_ref[rows, :, :size]
-    schur_ref[:, 0] = update_ref[:, 0, :, size:] + back_ref[rows, :, size:]
-
-
-def last_kernel(size, count, row_ref, update_ref, *refs):
+def last_kernel(size, count, stamped, row_ref, update_ref, *refs):
     back_refs, seen_ref = refs[:count], refs[count]
     lhat_ref, schur_ref, total_ref = refs[-3:]
     step = pl.program_id(0)
@@ -293,6 +290,8 @@
             back = back_refs[which]
             lhat_ref[0] = back[:, :size]
             schur_ref[0] = update_ref[0, :, size:] + back[:, size:]
+            if not stamped:
+                return
             head = back[:8, size:]
             marked = (first == 1) & (second == at)
             twin = jnp.sum(jnp.where((first == 0) & (second == at + 1), head, 0.0))
@@ -410,8 +409,12 @@
         )(row_number, child_map, *arrays)
 
     def whole_front(arrays, turn):
-        outs = [(order - size, order), (1, size)]
-        scratch = [pltpu.VMEM((order - size, size), f32), pltpu.VMEM((n, rows, LANES), f32)]
+        outs = [(update_rows, order)] * n + [(1, size)]
+        scratch = [
+            pltpu.VMEM((order - size, size), f32),
+            pltpu.VMEM((n, rows, LANES), f32),
+            pltpu.VMEM((order - size, order), f32),
+        ]
         return from_arrived(front_kernel, arrays, turn, outs, scratch)
 
     def factored(arrays, turn):
@@ -429,33 +432,12 @@
             name="schur",
         )(row_number, count.reshape(1), *parts)
 
-    def finish(back, turn, before):
-        aliases = {2: 0, 3: 1} if before else {}
-        group = 2
-        place = lambda g: (g, turn, 0, 0)
-        return pl.pallas_call(
-            functools.partial(finish_kernel, size),
-            grid=(n // group,),
-            in_specs=[pl.BlockSpec((group, 1, update_rows, order), place), vmem] + [whole] * len(before),
-            out_specs=(
-                pl.BlockSpec((group, 1, update_rows, size), place),
-                pl.BlockSpec((group, 1, update_rows, order - size), place),
-            ),
-            out_shape=(
-                flat((n, per, update_rows, size), f32),
-                flat((n, per, update_rows, order - size), f32),
-            ),
-            input_output_aliases=aliases,
-            name="finish",
-        )(updates, back, *before)
-
-    def last(backs, flips, turn, before, seen):
+    def last(backs, flips, turn, before, seen, stamped):
         count = len(backs)
         place = lambda g, r: ((r[0] ^ (flips[0] + g)) * per + turn, 0, 0)
-        before = [part.reshape(fronts, update_rows, -1) for part in before]
         aliases = {3 + count: 0, 4 + count: 1} if before else {}
         return pl.pallas_call(
-            functools.partial(last_kernel, size, count),
+            functools.partial(last_kernel, size, count, stamped),
             grid_spec=pltpu.PrefetchScalarGridSpec(
                 num_scalar_prefetch=1,
                 grid=(count,),
@@ -497,23 +479,32 @@
     arrays.append([arrived, parts[0]] + [send(parts[flip], flip) for flip in range(1, half)])
     total = jnp.zeros((), f32)
     backs = []
+
+    def home(parts):
+        far = [send(parts[flip], flip) for flip in range(half, n)]
+        return [parts[0]] + [send(parts[flip], flip) for flip in range(1, half)] + far
+
     for turn in range(per - 1):
-        rows_out, pivots = whole_front(arrays[turn], turn)
+        *parts, pivots = whole_front(arrays[turn], turn)
         total = total + jnp.sum(jnp.where(pivots < 0.0, 1.0, 0.0))
-        backs.append(exchange(rows_out.reshape(n, update_rows, order)))
+        backs.append(home(parts))
     turn = per - 1
     parts = factored(arrays[turn], turn)
     total = lax.psum(total + jnp.sum(jnp.where(parts[3] < 0.0, 1.0, 0.0)), "col")
-    homes = schur_rows(total, parts)
-    homes = [homes[0]] + [send(homes[flip], flip) for flip in range(1, n)]
+    parts = schur_rows(total, parts)
+    backs.append(home(parts))
     done = ()
-    for turn in range(per - 1):
-        done = finish(backs[turn], turn, done)
     seen = jnp.zeros((1, size), f32)
-    for begin, end in [(0, half)] + [(flip, flip + 1) for flip in range(half, n)]:
-        flips = range(begin, end)
-        lhat, schur, seen = last([homes[flip] for flip in flips], flips, per - 1, done, seen)
-        done = (lhat, schur)
+    singles = [range(flip, flip + 1) for flip in range(half, n)]
+    cut = len(singles) // 2
+    for turn in range(per):
+        stamped = turn == per - 1
+        groups = [range(half), range(half, n)]
+        if stamped:
+            groups = singles[:cut] + [range(half)] + singles[cut:]
+        for flips in groups:
+            lhat, schur, seen = last([backs[turn][flip] for flip in flips], flips, turn, done, seen, stamped)
+            done = (lhat, schur)
     negative_share = seen[0, 0] / (fronts * lax.axis_size("col") * size)
     return (lhat, schur, negative_share)
 

time: 200 us -> 203 us (1.015)
  starting transfers between devices: 40.3 us -> 60.2 us
  waiting for transfers between devices: 77.7 us -> 59.1 us
  Pallas kernels: 61.4 us -> 64.7 us
    ppermute x17 -> x24, starting transfers between devices: 28.9 us -> 53 us  [send(): return lax.ppermute(part, 'row', [(i, i ^ flip) for i in range(n)])]
    ppermute x17 -> x24, waiting for transfers between devices: 77.7 us -> 59.1 us  [send(): return lax.ppermute(part, 'row', [(i, i ^ flip) for i in range(n)])]
    all_to_all x1 -> x0, starting transfers between devices: 4.1 us -> none  [local_body(): backs.append(exchange(rows_out.reshape(n, update_rows, order)))]
    pallas_call x6 -> x7, Pallas kernels: 16 us -> 19.2 us  [last(): pl.pallas_call(functools.partial(last_kernel, size, count, stamped), grid...]
    unnamed x42 -> x54, local copies, waits for them, and re-layouts: 5.57 us -> 4.19 us
  transfers between devices with their start and end apart: 19 -> 25, of which waited for: 9 -> 7; matrix products, arithmetic and copies ran while one was open for 1% -> 2% of each run, Pallas kernels for 29% -> 30%
where the time goes in v6:
time: 203 us; the launch traced here: 202 us
  Pallas kernels  64.7 us (32%)
  starting transfers between devices  60.2 us (30%)
  waiting for transfers between devices  59.1 us (29%)
  blocking collectives  7.01 us (3%)
  local copies, waits for them, and re-layouts  4.77 us (2%)
  between operations  3.74 us (2%)
  other arithmetic  2.52 us (1%)
    ppermute x24, waiting for transfers between devices, send(): return lax.ppermute(part, 'row', [(i, i ^ flip) for i in range(n)])  59.1 us
    ppermute x24, starting transfers between devices, send(): return lax.ppermute(part, 'row', [(i, i ^ flip) for i in range(n)])  53 us
    pallas_call x2, Pallas kernels, from_arrived(): pl.pallas_call(functools.partial(kernel, dims + (update_rows, pivot_rows)...  30.1 us
    pallas_call x7, Pallas kernels, last(): pl.pallas_call(functools.partial(last_kernel, size, count, stamped), grid...  19.2 us
    all_to_all x1, starting transfers between devices, local_body(): arrived = exchange(packed)  7.28 us
    psum x1, blocking collectives, local_body(): lax.psum(total + jnp.sum(jnp.where(parts[3] < 0.0, 1.0, 0.0)), 'col')  7.01 us
    pallas_call x1, Pallas kernels, schur_rows(): pl.pallas_call(schur_kernel, in_specs=[smem, smem] + [vmem] * 4, out_spec...  6.15 us
    pallas_call x2, Pallas kernels, parts_for(): pl.pallas_call(functools.partial(part_kernel, dims, count), grid_spec=plt...  4.86 us
  transfers between devices with their start and end apart: 25, of which 7 were waited for; matrix products, arithmetic and copies ran while one was open for 2% of the time, Pallas kernels for 30%

profile of v6, /device:TPU:0, one launch (start us, length us, event | category | flops | bytes accessed | tf_op | source)
XLA Modules:
  0.0 202.1 jit_solution(15442928785468630681)
XLA Ops:
  0.6 2.6 %pack.1 = f32[8,256,128]{2,1,0:T(8,128)} custom-call(s32[1]{0:T(128)} %bitcast.row_ref.refs_0_, f32[8,2,2,64,512]{4,3,2,1,0:T(8,128)} %bitcast.7, f32[8,2,80,768]{3,2,1,0:T(8,128)} %bitcast.8, f32[8,2,16,128]{3,2,1,0:T(8,128)} %bitcast.9), custom_call_target="tpu_custom_call" | custom-call | tf_op jit(solution)/shard_map/pack/pallas_call | solution.py:323
  3.2 7.3 %all-to-all-start = ((f32[8,256,128]{2,1,0:T(8,128)}), f32[8,256,128]{2,1,0:T(8,128)S(1)}, u32[]{:S(2)}, u32[]{:S(2)}) async-start(f32[8,256,128]{2,1,0:T(8,128)} %pack.1), calls=%async_computation | async-start | bytes 2097152 | tf_op jit(solution)/shard_map/all_to_all | solution.py:477
  10.5 2.2 %parts.3 = (f32[256,128]{1,0:T(8,128)}, f32[256,128]{1,0:T(8,128)}, f32[256,128]{1,0:T(8,128)}, f32[256,128]{1,0:T(8,128)}) custom-call(s32[1]{0:T(128)} %bitcast.row_ref.refs_0_, f32[16,2,64,512]{3,2,1,0:T(8,128)} %refs_4_.5, f32[16,2,64,512]{3,2,1,0:T(8,128)} %refs_4_.5, f32[16,2,64,512]{3,2,1,0:T(8,128)} %refs_4_.5, f32[16,2,64,512]{3,2,1,0:T(8,128)} %refs_4_.5, ...), custom_call_target="tpu_custom_call" | custom-call | tf_op jit(solution)/shard_map/parts/pallas_call | solution.py:363
  12.7 2.9 %collective-permute-start.3 = (f32[256,128]{1,0:T(8,128)}, f32[256,128]{1,0:T(8,128)S(1)}, u32[]{:S(2)}, u32[]{:S(2)}) collective-permute-start(f32[256,128]{1,0:T(8,128)} %get-tuple-element.61), channel_id=1, source_target_pairs={{0,16},{4,20},{8,24},{12,28},{16,0},{20,4},{24,8},{28,12},{1,17},{... | collective-permute-start | bytes 393224 | tf_op jit(solution)/shard_map/ppermute | solution.py:465
  17.1 2.6 %parts.2 = (f32[512,128]{1,0:T(8,128)}, f32[512,128]{1,0:T(8,128)}, f32[512,128]{1,0:T(8,128)}, f32[512,128]{1,0:T(8,128)}) custom-call(s32[1]{0:T(128)} %bitcast.row_ref.refs_0_, f32[16,2,64,512]{3,2,1,0:T(8,128)} %refs_4_.5, f32[16,2,64,512]{3,2,1,0:T(8,128)} %refs_4_.5, f32[16,2,64,512]{3,2,1,0:T(8,128)} %refs_4_.5, f32[16,2,64,512]{3,2,1,0:T(8,128)} %refs_4_.5, ...), custom_call_target="tpu_custom_call" | custom-call | tf_op jit(solution)/shard_map/parts/pallas_call | solution.py:363
  23.2 22.8 %collective-permute-done.3.refs_4_ = f32[256,128]{1,0:T(8,128)S(1)} collective-permute-done((f32[256,128]{1,0:T(8,128)}, f32[256,128]{1,0:T(8,128)S(1)}, u32[]{:S(2)}, u32[]{:S(2)}) %collective-permute-start.3) | collective-permute-done | bytes 131104 | tf_op jit(solution)/shard_map/ppermute | solution.py:465
  46.0 3.5 %collective-permute-done.4.refs_5_ = f32[256,128]{1,0:T(8,128)S(1)} collective-permute-done((f32[256,128]{1,0:T(8,128)}, f32[256,128]{1,0:T(8,128)S(1)}, u32[]{:S(2)}, u32[]{:S(2)}) %collective-permute-start.4) | collective-permute-done | bytes 131104 | tf_op jit(solution)/shard_map/ppermute | solution.py:465
  54.5 2.9 %collective-permute-done.6.refs_7_ = f32[256,128]{1,0:T(8,128)S(1)} collective-permute-done((f32[256,128]{1,0:T(8,128)S(1)}, f32[256,128]{1,0:T(8,128)S(1)}, u32[]{:S(2)}, u32[]{:S(2)}) %collective-permute-start.6) | collective-permute-done | bytes 131104 | tf_op jit(solution)/shard_map/ppermute | solution.py:465
  57.4 2.8 %collective-permute-start.8 = (f32[2,64,256]{2,1,0:T(8,128)}, f32[2,64,256]{2,1,0:T(8,128)S(1)}, u32[]{:S(2)}, u32[]{:S(2)}) collective-permute-start(f32[2,64,256]{2,1,0:T(8,128)} %get-tuple-element.68), channel_id=1, source_target_pairs={{0,8},{4,12},{8,0},{12,4},{16,24},{20,28},{24,16},{28,20},{1,9},{5... | collective-permute-start | bytes 393224 | tf_op jit(solution)/shard_map/ppermute | solution.py:465
  61.0 16.3 %front.2 = (f32[80,768]{1,0:T(8,128)}, f32[80,768]{1,0:T(8,128)}, f32[80,768]{1,0:T(8,128)}, f32[80,768]{1,0:T(8,128)}, f32[80,768]{1,0:T(8,128)}, /*index=5*/f3...) custom-call(s32[1]{0:T(128)} %bitcast.row_ref.refs_0_, s32[16,2,512]{2,1,0:T(2,128)} %map_ref.3, ...), custom_call_target="tpu_custom_call" | custom-call | tf_op jit(solution)/shard_map/front/pallas_call | solution.py:391
  84.1 14.7 %collective-permute-done.9.refs_3_ = f32[2,64,256]{2,1,0:T(8,128)S(1)} collective-permute-done((f32[2,64,256]{2,1,0:T(8,128)}, f32[2,64,256]{2,1,0:T(8,128)S(1)}, u32[]{:S(2)}, u32[]{:S(2)}) %collective-permute-start.9) | collective-permute-done | bytes 131104 | tf_op jit(solution)/shard_map/ppermute | solution.py:465
  100.0 13.8 %front.3 = (f32[640,640]{1,0:T(8,128)}, f32[640,128]{1,0:T(8,128)}, f32[128,128]{1,0:T(8,128)}, f32[1,128]{1,0:T(1,128)}) custom-call(s32[1]{0:T(128)} %bitcast.row_ref.refs_0_, s32[16,2,512]{2,1,0:T(2,128)} %map_ref.3, f32[8,256,128]{2,1,0:T(8,128)} %copy-done, f32[2,64,256]{2,1,0:T(8,128)} %get-tuple-element.66.refs_0_, f32[2,64,256]{2,1,0:T(8,128)} %copy-done.18, ...), custom_call_target="tpu_custom_call" | custom-call | tf_op jit(solution)/shard_map/front/pallas_call | solution.py:391
  116.2 7.0 %psum.7.count_ref = f32[1]{0:T(128)} all-reduce(f32[1]{0:T(128)} %bitcast.4), channel_id=1, replica_groups=mesh['row'=8,'col'=4] {'col'}, use_global_device_ids=true, to_apply=%region_2.3 | all-reduce | flops 1 | bytes 8 | tf_op jit(solution)/shard_map/psum | solution.py:493
  123.3 2.2 %collective-permute-start.19 = (f32[80,768]{1,0:T(8,128)}, f32[80,768]{1,0:T(8,128)S(1)}, u32[]{:S(2)}, u32[]{:S(2)}) collective-permute-start(f32[80,768]{1,0:T(8,128)} %get-tuple-element.84), channel_id=1, source_target_pairs={{0,24},{4,28},{8,16},{12,20},{16,8},{20,12},{24,0},{28,4},{1,25},{... | collective-permute-start | bytes 737288 | tf_op jit(solution)/shard_map/ppermute | solution.py:465
  125.5 2.7 %collective-permute-start.20 = (f32[80,768]{1,0:T(8,128)}, f32[80,768]{1,0:T(8,128)S(1)}, u32[]{:S(2)}, u32[]{:S(2)}) collective-permute-start(f32[80,768]{1,0:T(8,128)} %get-tuple-element.85), channel_id=1, source_target_pairs={{0,28},{4,24},{8,20},{12,16},{16,12},{20,8},{24,4},{28,0},{1,29},{... | collective-permute-start | bytes 737288 | tf_op jit(solution)/shard_map/ppermute | solution.py:465
  128.2 6.2 %schur.1 = (f32[80,768]{1,0:T(8,128)}, f32[80,768]{1,0:T(8,128)}, f32[80,768]{1,0:T(8,128)}, f32[80,768]{1,0:T(8,128)}, f32[80,768]{1,0:T(8,128)}, /*index=5*/f3...) custom-call(s32[1]{0:T(128)} %bitcast.row_ref.refs_0_, f32[1]{0:T(128)} %psum.7.count_ref, ...), custom_call_target="tpu_custom_call" | custom-call | tf_op jit(solution)/shard_map/schur/pallas_call | solution.py:426
  138.8 15.7 %collective-permute-start.13 = (f32[80,768]{1,0:T(8,128)}, f32[80,768]{1,0:T(8,128)S(1)}, u32[]{:S(2)}, u32[]{:S(2)}) collective-permute-start(f32[80,768]{1,0:T(8,128)} %get-tuple-element.78), channel_id=1, source_target_pairs={{0,8},{4,12},{8,0},{12,4},{16,24},{20,28},{24,16},{28,20},{1,9},{5... | collective-permute-start | bytes 737288 | tf_op jit(solution)/shard_map/ppermute | solution.py:465
  154.5 6.2 %collective-permute-start.14 = (f32[80,768]{1,0:T(8,128)}, f32[80,768]{1,0:T(8,128)S(1)}, u32[]{:S(2)}, u32[]{:S(2)}) collective-permute-start(f32[80,768]{1,0:T(8,128)} %get-tuple-element.79), channel_id=1, source_target_pairs={{0,12},{4,8},{8,4},{12,0},{16,28},{20,24},{24,20},{28,16},{1,13},{... | collective-permute-start | bytes 737288 | tf_op jit(solution)/shard_map/ppermute | solution.py:465
  160.7 3.9 %collective-permute-done.16.refs_0_ = f32[80,768]{1,0:T(8,128)S(1)} collective-permute-done((f32[80,768]{1,0:T(8,128)}, f32[80,768]{1,0:T(8,128)S(1)}, u32[]{:S(2)}, u32[]{:S(2)}) %collective-permute-start.16) | collective-permute-done | bytes 245792 | tf_op jit(solution)/shard_map/ppermute | solution.py:465
  164.6 2.2 %collective-permute-start.11 = (f32[80,768]{1,0:T(8,128)}, f32[80,768]{1,0:T(8,128)S(1)}, u32[]{:S(2)}, u32[]{:S(2)}) collective-permute-start(f32[80,768]{1,0:T(8,128)} %get-tuple-element.75), channel_id=1, source_target_pairs={{0,24},{4,28},{8,16},{12,20},{16,8},{20,12},{24,0},{28,4},{1,25},{... | collective-permute-start | bytes 737288 | tf_op jit(solution)/shard_map/ppermute | solution.py:465
  166.8 9.4 %collective-permute-done.15.refs_0_ = f32[80,768]{1,0:T(8,128)S(1)} collective-permute-done((f32[80,768]{1,0:T(8,128)}, f32[80,768]{1,0:T(8,128)S(1)}, u32[]{:S(2)}, u32[]{:S(2)}) %collective-permute-start.15) | collective-permute-done | bytes 245792 | tf_op jit(solution)/shard_map/ppermute | solution.py:465
  178.8 3.9 %last.7 = (f32[16,80,128]{2,1,0:T(8,128)}, f32[16,80,640]{2,1,0:T(8,128)}, f32[1,128]{1,0:T(1,128)}) custom-call(s32[1]{0:T(128)} %bitcast.row_ref.refs_0_, f32[16,80,768]{2,1,0:T(8,128)} %update_ref.13, f32[80,768]{1,0:T(8,128)} %get-tuple-element.86.refs_0_, f32[80,768]{1,0:T(8,128)} %copy-done.15, f32[80,768]{1,0:T(8,128)} %copy-done.16, ...), custom_call_target="tpu_custom_call" | custom-call | tf_op jit(solution)/shard_map/last/pallas_call | solution.py:439
  182.6 3.9 %last.8 = (f32[16,80,128]{2,1,0:T(8,128)}, f32[16,80,640]{2,1,0:T(8,128)}, f32[1,128]{1,0:T(1,128)}) custom-call(s32[1]{0:T(128)} %bitcast.row_ref.refs_0_, f32[16,80,768]{2,1,0:T(8,128)} %update_ref.13, f32[80,768]{1,0:T(8,128)} %copy-done.4, f32[80,768]{1,0:T(8,128)} %copy-done.5, ...), custom_call_target="tpu_custom_call", output_to_operand_aliasing={{0}: (7, {}), {1}: (8, {})} | custom-call | tf_op jit(solution)/shard_map/last/pallas_call | solution.py:439
  191.2 4.0 %last.11 = (f32[16,80,128]{2,1,0:T(8,128)}, f32[16,80,640]{2,1,0:T(8,128)}, f32[1,128]{1,0:T(1,128)}) custom-call(s32[1]{0:T(128)} %bitcast.row_ref.refs_0_, f32[16,80,768]{2,1,0:T(8,128)} %update_ref.13, f32[80,768]{1,0:T(8,128)} %get-tuple-element.76.refs_0_, f32[80,768]{1,0:T(8,128)} %copy-done.7, ...), custom_call_target="tpu_custom_call", output_to_operand_aliasing={{0}: (7, {}), {1}: (8, {})} | custom-call | tf_op jit(solution)/shard_map/last/pallas_call | solution.py:439
  (98 shorter events, 36.9 us)
Async XLA Ops:
  3.2 95.8 %all-to-all-start = ((f32[8,256,128]{2,1,0:T(8,128)}), f32[8,256,128]{2,1,0:T(8,128)S(1)}, u32[]{:S(2)}, u32[]{:S(2)}) async-start(f32[8,256,128]{2,1,0:T(8,128)} %pack.1), calls=%async_computation | async-start | bytes 2097152 | tf_op jit(solution)/shard_map/all_to_all | solution.py:477
  12.7 33.3 %collective-permute-start.3 = (f32[256,128]{1,0:T(8,128)}, f32[256,128]{1,0:T(8,128)S(1)}, u32[]{:S(2)}, u32[]{:S(2)}) collective-permute-start(f32[256,128]{1,0:T(8,128)} %get-tuple-element.61), channel_id=1, source_target_pairs={{0,16},{4,20},{8,24},{12,28},{16,0},{20,4},{24,8},{28,12},{1,17},{... | collective-permute-start | bytes 393224 | tf_op jit(solution)/shard_map/ppermute | solution.py:465
  15.6 34.0 %collective-permute-start.4 = (f32[256,128]{1,0:T(8,128)}, f32[256,128]{1,0:T(8,128)S(1)}, u32[]{:S(2)}, u32[]{:S(2)}) collective-permute-start(f32[256,128]{1,0:T(8,128)} %get-tuple-element.62), channel_id=1, source_target_pairs={{0,20},{4,16},{8,28},{12,24},{16,4},{20,0},{24,12},{28,8},{1,21},{... | collective-permute-start | bytes 393224 | tf_op jit(solution)/shard_map/ppermute | solution.py:465
  19.7 40.4 %collective-permute-start = (f32[512,128]{1,0:T(8,128)}, f32[512,128]{1,0:T(8,128)S(1)}, u32[]{:S(2)}, u32[]{:S(2)}) collective-permute-start(f32[512,128]{1,0:T(8,128)} %get-tuple-element.58), channel_id=1, source_target_pairs={{0,4},{4,0},{8,12},{12,8},{16,20},{20,16},{24,28},{28,24},{1,5},{5... | collective-permute-start | bytes 786440 | tf_op jit(solution)/shard_map/ppermute | solution.py:465
  19.8 40.3 %collective-permute-start.1 = (f32[512,128]{1,0:T(8,128)}, f32[512,128]{1,0:T(8,128)S(1)}, u32[]{:S(2)}, u32[]{:S(2)}) collective-permute-start(f32[512,128]{1,0:T(8,128)} %get-tuple-element.59), channel_id=1, source_target_pairs={{0,8},{4,12},{8,0},{12,4},{16,24},{20,28},{24,16},{28,20},{1,9},{5... | collective-permute-start | bytes 786440 | tf_op jit(solution)/shard_map/ppermute | solution.py:465
  21.7 38.4 %collective-permute-start.2 = (f32[512,128]{1,0:T(8,128)}, f32[512,128]{1,0:T(8,128)S(1)}, u32[]{:S(2)}, u32[]{:S(2)}) collective-permute-start(f32[512,128]{1,0:T(8,128)} %get-tuple-element.60), channel_id=1, source_target_pairs={{0,12},{4,8},{8,4},{12,0},{16,28},{20,24},{24,20},{28,16},{1,13},{... | collective-permute-start | bytes 786440 | tf_op jit(solution)/shard_map/ppermute | solution.py:465
  46.0 8.2 %collective-permute-start.5 = (f32[256,128]{1,0:T(8,128)S(1)}, f32[256,128]{1,0:T(8,128)S(1)}, u32[]{:S(2)}, u32[]{:S(2)}) collective-permute-start(f32[256,128]{1,0:T(8,128)S(1)} %copy-done.26), channel_id=1, source_target_pairs={{0,24},{4,28},{8,16},{12,20},{16,8},{20,12},{24,0},{28,4},{1,25},{... | collective-permute-start | bytes 393224 | tf_op jit(solution)/shard_map/ppermute | solution.py:465
  54.2 26.6 %collective-permute-start.7 = (f32[2,64,256]{2,1,0:T(8,128)}, f32[2,64,256]{2,1,0:T(8,128)S(1)}, u32[]{:S(2)}, u32[]{:S(2)}) collective-permute-start(f32[2,64,256]{2,1,0:T(8,128)} %get-tuple-element.67), channel_id=1, source_target_pairs={{0,4},{4,0},{8,12},{12,8},{16,20},{20,16},{24,28},{28,24},{1,5},{5... | collective-permute-start | bytes 393224 | tf_op jit(solution)/shard_map/ppermute | solution.py:465
  57.4 23.5 %collective-permute-start.8 = (f32[2,64,256]{2,1,0:T(8,128)}, f32[2,64,256]{2,1,0:T(8,128)S(1)}, u32[]{:S(2)}, u32[]{:S(2)}) collective-permute-start(f32[2,64,256]{2,1,0:T(8,128)} %get-tuple-element.68), channel_id=1, source_target_pairs={{0,8},{4,12},{8,0},{12,4},{16,24},{20,28},{24,16},{28,20},{1,9},{5... | collective-permute-start | bytes 393224 | tf_op jit(solution)/shard_map/ppermute | solution.py:465
  77.3 45.9 %collective-permute-start.21 = (f32[80,768]{1,0:T(8,128)}, f32[80,768]{1,0:T(8,128)S(1)}, u32[]{:S(2)}, u32[]{:S(2)}) collective-permute-start(f32[80,768]{1,0:T(8,128)} %get-tuple-element.87), channel_id=1, source_target_pairs={{0,4},{4,0},{8,12},{12,8},{16,20},{20,16},{24,28},{28,24},{1,5},{5... | collective-permute-start | bytes 737288 | tf_op jit(solution)/shard_map/ppermute | solution.py:465
  77.9 47.5 %collective-permute-start.22 = (f32[80,768]{1,0:T(8,128)}, f32[80,768]{1,0:T(8,128)S(1)}, u32[]{:S(2)}, u32[]{:S(2)}) collective-permute-start(f32[80,768]{1,0:T(8,128)} %get-tuple-element.88), channel_id=1, source_target_pairs={{0,8},{4,12},{8,0},{12,4},{16,24},{20,28},{24,16},{28,20},{1,9},{5... | collective-permute-start | bytes 737288 | tf_op jit(solution)/shard_map/ppermute | solution.py:465
  78.8 55.6 %collective-permute-start.23 = (f32[80,768]{1,0:T(8,128)}, f32[80,768]{1,0:T(8,128)S(1)}, u32[]{:S(2)}, u32[]{:S(2)}) collective-permute-start(f32[80,768]{1,0:T(8,128)} %get-tuple-element.89), channel_id=1, source_target_pairs={{0,12},{4,8},{8,4},{12,0},{16,28},{20,24},{24,20},{28,16},{1,13},{... | collective-permute-start | bytes 737288 | tf_op jit(solution)/shard_map/ppermute | solution.py:465
  80.8 54.3 %collective-permute-start.17 = (f32[80,768]{1,0:T(8,128)}, f32[80,768]{1,0:T(8,128)S(1)}, u32[]{:S(2)}, u32[]{:S(2)}) collective-permute-start(f32[80,768]{1,0:T(8,128)} %get-tuple-element.82), channel_id=1, source_target_pairs={{0,16},{4,20},{8,24},{12,28},{16,0},{20,4},{24,8},{28,12},{1,17},{... | collective-permute-start | bytes 737288 | tf_op jit(solution)/shard_map/ppermute | solution.py:465
  80.9 17.9 %collective-permute-start.9 = (f32[2,64,256]{2,1,0:T(8,128)}, f32[2,64,256]{2,1,0:T(8,128)S(1)}, u32[]{:S(2)}, u32[]{:S(2)}) collective-permute-start(f32[2,64,256]{2,1,0:T(8,128)} %get-tuple-element.69), channel_id=1, source_target_pairs={{0,12},{4,8},{8,4},{12,0},{16,28},{20,24},{24,20},{28,16},{1,13},{... | collective-permute-start | bytes 393224 | tf_op jit(solution)/shard_map/ppermute | solution.py:465
  98.7 38.4 %collective-permute-start.18 = (f32[80,768]{1,0:T(8,128)}, f32[80,768]{1,0:T(8,128)S(1)}, u32[]{:S(2)}, u32[]{:S(2)}) collective-permute-start(f32[80,768]{1,0:T(8,128)} %get-tuple-element.83), channel_id=1, source_target_pairs={{0,20},{4,16},{8,28},{12,24},{16,4},{20,0},{24,12},{28,8},{1,21},{... | collective-permute-start | bytes 737288 | tf_op jit(solution)/shard_map/ppermute | solution.py:465
  123.3 15.6 %collective-permute-start.19 = (f32[80,768]{1,0:T(8,128)}, f32[80,768]{1,0:T(8,128)S(1)}, u32[]{:S(2)}, u32[]{:S(2)}) collective-permute-start(f32[80,768]{1,0:T(8,128)} %get-tuple-element.84), channel_id=1, source_target_pairs={{0,24},{4,28},{8,16},{12,20},{16,8},{20,12},{24,0},{28,4},{1,25},{... | collective-permute-start | bytes 737288 | tf_op jit(solution)/shard_map/ppermute | solution.py:465
  125.5 29.0 %collective-permute-start.20 = (f32[80,768]{1,0:T(8,128)}, f32[80,768]{1,0:T(8,128)S(1)}, u32[]{:S(2)}, u32[]{:S(2)}) collective-permute-start(f32[80,768]{1,0:T(8,128)} %get-tuple-element.85), channel_id=1, source_target_pairs={{0,28},{4,24},{8,20},{12,16},{16,12},{20,8},{24,4},{28,0},{1,29},{... | collective-permute-start | bytes 737288 | tf_op jit(solution)/shard_map/ppermute | solution.py:465
  134.4 30.2 %collective-permute-start.16 = (f32[80,768]{1,0:T(8,128)}, f32[80,768]{1,0:T(8,128)S(1)}, u32[]{:S(2)}, u32[]{:S(2)}) collective-permute-start(f32[80,768]{1,0:T(8,128)} %get-tuple-element.81), channel_id=1, source_target_pairs={{0,16},{4,20},{8,24},{12,28},{16,0},{20,4},{24,8},{28,12},{1,17},{... | collective-permute-start | bytes 737288 | tf_op jit(solution)/shard_map/ppermute | solution.py:465
  135.1 41.1 %collective-permute-start.15 = (f32[80,768]{1,0:T(8,128)}, f32[80,768]{1,0:T(8,128)S(1)}, u32[]{:S(2)}, u32[]{:S(2)}) collective-permute-start(f32[80,768]{1,0:T(8,128)} %get-tuple-element.80), channel_id=1, source_target_pairs={{0,20},{4,16},{8,28},{12,24},{16,4},{20,0},{24,12},{28,8},{1,21},{... | collective-permute-start | bytes 737288 | tf_op jit(solution)/shard_map/ppermute | solution.py:465
  137.2 53.1 %collective-permute-start.12 = (f32[80,768]{1,0:T(8,128)}, f32[80,768]{1,0:T(8,128)S(1)}, u32[]{:S(2)}, u32[]{:S(2)}) collective-permute-start(f32[80,768]{1,0:T(8,128)} %get-tuple-element.77), channel_id=1, source_target_pairs={{0,4},{4,0},{8,12},{12,8},{16,20},{20,16},{24,28},{28,24},{1,5},{5... | collective-permute-start | bytes 737288 | tf_op jit(solution)/shard_map/ppermute | solution.py:465
  138.8 51.4 %collective-permute-start.13 = (f32[80,768]{1,0:T(8,128)}, f32[80,768]{1,0:T(8,128)S(1)}, u32[]{:S(2)}, u32[]{:S(2)}) collective-permute-start(f32[80,768]{1,0:T(8,128)} %get-tuple-element.78), channel_id=1, source_target_pairs={{0,8},{4,12},{8,0},{12,4},{16,24},{20,28},{24,16},{28,20},{1,9},{5... | collective-permute-start | bytes 737288 | tf_op jit(solution)/shard_map/ppermute | solution.py:465
  154.5 35.8 %collective-permute-start.14 = (f32[80,768]{1,0:T(8,128)}, f32[80,768]{1,0:T(8,128)S(1)}, u32[]{:S(2)}, u32[]{:S(2)}) collective-permute-start(f32[80,768]{1,0:T(8,128)} %get-tuple-element.79), channel_id=1, source_target_pairs={{0,12},{4,8},{8,4},{12,0},{16,28},{20,24},{24,20},{28,16},{1,13},{... | collective-permute-start | bytes 737288 | tf_op jit(solution)/shard_map/ppermute | solution.py:465
  164.6 30.6 %collective-permute-start.11 = (f32[80,768]{1,0:T(8,128)}, f32[80,768]{1,0:T(8,128)S(1)}, u32[]{:S(2)}, u32[]{:S(2)}) collective-permute-start(f32[80,768]{1,0:T(8,128)} %get-tuple-element.75), channel_id=1, source_target_pairs={{0,24},{4,28},{8,16},{12,20},{16,8},{20,12},{24,0},{28,4},{1,25},{... | collective-permute-start | bytes 737288 | tf_op jit(solution)/shard_map/ppermute | solution.py:465
  176.2 21.6 %collective-permute-start.10 = (f32[80,768]{1,0:T(8,128)}, f32[80,768]{1,0:T(8,128)S(1)}, u32[]{:S(2)}, u32[]{:S(2)}) collective-permute-start(f32[80,768]{1,0:T(8,128)} %get-tuple-element.74), channel_id=1, source_target_pairs={{0,28},{4,24},{8,20},{12,16},{16,12},{20,8},{24,4},{28,0},{1,29},{... | collective-permute-start | bytes 737288 | tf_op jit(solution)/shard_map/ppermute | solution.py:465
  (28 other events, 484.5 us)
